TPU v7x, 16 devices: a whole 2x2x2 slice. The times are simulated.
16 devices in a mesh: data: 16 (over z, y, x, core).
Axes of the slice: x: 2, y: 2, z: 2, core: 2. Of those that a mesh axis runs over, the one named last changes fastest.
Arguments:
- q_in: bfloat16 [1024, 1024], P('data')
- d_in: bfloat16 [2, 1024, 1024], P(None, 'data')
- temperature: float32 [], replicated
- q_w1: bfloat16 [2, 1024, 4096], replicated
- q_w2: bfloat16 [2, 4096, 1024], replicated
- q_proj: bfloat16 [1024, 1024], replicated
- d_w1: bfloat16 [2, 1024, 4096], replicated
- d_w2: bfloat16 [2, 4096, 1024], replicated
- d_proj: bfloat16 [1024, 1024], replicated
Outputs:
- output 1: float32 [], replicated
- output 2: float32 [2, 1024, 4096], replicated
- output 3: float32 [2, 4096, 1024], replicated
- output 4: float32 [1024, 1024], replicated
- output 5: float32 [2, 1024, 4096], replicated
- output 6: float32 [2, 4096, 1024], replicated
- output 7: float32 [1024, 1024], replicated
All inputs are finite; a program needn't handle non-finite values.
Results may differ from a plain program's by a relative error of at most 0.0113187.
Values are sent between devices in bfloat16 or wider.
A program may use at most 1 GiB of HBM per device.

v0:
```python
import jax
import jax.numpy as jnp
from jax import lax
from jax.sharding import PartitionSpec as P

SUB_COUNT = 4
ROWS_CONTRACT = (((0,), (0,)), ((), ()))
LAST_CONTRACT = (((1,), (1,)), ((), ()))


def tower_forward(row_block, w_one, w_two, w_proj):
    hidden = row_block
    saved = []
    for layer in range(2):
        pre_act = jnp.dot(hidden, w_one[layer], preferred_element_type=jnp.float32)
        act_bf = jax.nn.gelu(pre_act).astype(jnp.bfloat16)
        saved.append((hidden, pre_act, act_bf))
        hidden = (hidden.astype(jnp.float32) + jnp.dot(act_bf, w_two[layer], preferred_element_type=jnp.float32)).astype(jnp.bfloat16)
    out_reps = jnp.dot(hidden, w_proj, preferred_element_type=jnp.float32).astype(jnp.bfloat16)
    return out_reps, hidden, saved


def tower_backward(upstream, w_one, w_two, w_proj, hidden, saved):
    g_proj = lax.dot_general(hidden, upstream, ROWS_CONTRACT, preferred_element_type=jnp.float32)
    resid_grad = lax.dot_general(upstream, w_proj, LAST_CONTRACT, preferred_element_type=jnp.float32)
    grads_one = [None, None]
    grads_two = [None, None]
    for layer in (1, 0):
        h_in, pre_act, act_bf = saved[layer]
        resid_bf = resid_grad.astype(jnp.bfloat16)
        grads_two[layer] = lax.dot_general(act_bf, resid_bf, ROWS_CONTRACT, preferred_element_type=jnp.float32)
        act_grad = lax.dot_general(resid_bf, w_two[layer], LAST_CONTRACT, preferred_element_type=jnp.float32)
        gelu_back = jax.vjp(jax.nn.gelu, pre_act)[1]
        pre_grad = gelu_back(act_grad)[0].astype(jnp.bfloat16)
        grads_one[layer] = lax.dot_general(h_in, pre_grad, ROWS_CONTRACT, preferred_element_type=jnp.float32)
        if layer == 1:
            resid_grad = resid_grad + lax.dot_general(pre_grad, w_one[layer], LAST_CONTRACT, preferred_element_type=jnp.float32)
    return jnp.stack(grads_one), jnp.stack(grads_two), g_proj


def tower_grads(row_subs, up_subs, w_one, w_two, w_proj):
    def body(running, block_in):
        row_block, upstream = block_in
        hidden, saved = tower_forward(row_block, w_one, w_two, w_proj)[1:]
        new_grads = tower_backward(upstream, w_one, w_two, w_proj, hidden, saved)
        return tuple(old_sum + new_part for old_sum, new_part in zip(running, new_grads)), None

    zeros_init = (jnp.zeros(w_one.shape, jnp.float32), jnp.zeros(w_two.shape, jnp.float32), jnp.zeros(w_proj.shape, jnp.float32))
    return lax.scan(body, zeros_init, (row_subs, up_subs))[0]


def local_step(q_loc, d_loc, value_a11, q_w1, q_w2, q_proj, d_w1, d_w2, d_proj):
    rows_loc, width_in = q_loc.shape
    q_sub = q_loc.reshape(SUB_COUNT, rows_loc // SUB_COUNT, width_in)
    d_sub = d_loc.reshape(SUB_COUNT, 2 * rows_loc // SUB_COUNT, width_in)
    q_reps = lax.map(lambda row_block: tower_forward(row_block, q_w1, q_w2, q_proj)[0], q_sub).reshape(rows_loc, -1)
    d_reps = lax.map(lambda row_block: tower_forward(row_block, d_w1, d_w2, d_proj)[0], d_sub).reshape(2, rows_loc, -1)
    all_docs = lax.all_gather(d_reps, 'data', axis=1, tiled=True)
    global_batch = all_docs.shape[1]
    rep_width = all_docs.shape[2]
    doc_flat = all_docs.reshape(2 * global_batch, rep_width)
    logits = lax.dot_general(q_reps, doc_flat, LAST_CONTRACT, preferred_element_type=jnp.float32) / value_a11
    row_start = lax.axis_index('data') * rows_loc
    target = jnp.arange(2 * global_batch)[None, :] == (row_start + jnp.arange(rows_loc))[:, None]
    log_norm = jax.nn.logsumexp(logits, axis=1)
    pos_logit = jnp.sum(jnp.where(target, logits, 0.0), axis=1)
    loss = lax.psum(jnp.sum(log_norm - pos_logit), 'data') / global_batch
    soft_prob = jnp.exp(logits - log_norm[:, None])
    grad_logit = ((soft_prob - target.astype(jnp.float32)) / (global_batch * value_a11)).astype(jnp.bfloat16)
    q_up = jnp.dot(grad_logit, doc_flat, preferred_element_type=jnp.float32).astype(jnp.bfloat16)
    doc_part = lax.dot_general(grad_logit, q_reps, ROWS_CONTRACT, preferred_element_type=jnp.float32)
    doc_up = lax.psum_scatter(doc_part.reshape(2, global_batch, rep_width), 'data', scatter_dimension=1, tiled=True).astype(jnp.bfloat16)
    q_grads = tower_grads(q_sub, q_up.reshape(SUB_COUNT, -1, rep_width), q_w1, q_w2, q_proj)
    d_grads = tower_grads(d_sub, doc_up.reshape(SUB_COUNT, -1, rep_width), d_w1, d_w2, d_proj)
    q_one, q_two, q_pgrad = lax.psum(q_grads, 'data')
    d_one, d_two, d_pgrad = lax.psum(d_grads, 'data')
    return (loss, q_one, q_two, q_pgrad, d_one, d_two, d_pgrad)


def solution(mesh):
    specs_in = (P('data', None), P(None, 'data', None), P(), P(), P(), P(), P(), P(), P())
    specs_out = (P(), P(), P(), P(), P(), P(), P())
    return jax.shard_map(local_step, mesh=mesh, in_specs=specs_in, out_specs=specs_out, check_vma=False)
```

profile of v0, /device:TPU:0, one launch (start us, length us, event | category | flops | bytes accessed | tf_op | source)
XLA Modules:
  0.0 2359.7 jit_solution(13690760513779414697)
XLA Ops:
  7.2 79.8 %while.57 = (s32[]{:T(128)}, bf16[4,32,1024]{2,1,0:T(8,128)(2,1)}, bf16[4,32,1024]{2,1,0:T(8,128)(2,1)}, bf16[2,1024,4096]{2,1,0:T(8,128)(2,1)}, bf16[2,4096,102...) while((s32[]{:T(128)}, bf16[4,32,1024]{2,1,0:T(8,128)(2,1)}, bf16[4,32,1024]{2,1,0:T(8,128)(2,1)}, ...), condition=%wide.region_3.4_spmd, body=%wide.region_2.3_spmd.sunk | while | flops 1143439360 | bytes 44958836 | solution.py:57
  7.3 9.0 fusion.420
  27.2 9.0 fusion.420
  47.1 9.0 fusion.420
  67.1 9.0 fusion.420
  87.9 70.9 %while.56 = (s32[]{:T(128)}, bf16[4,16,1024]{2,1,0:T(8,128)(2,1)S(1)}, bf16[4,16,1024]{2,1,0:T(8,128)(2,1)S(1)}, bf16[2,1024,4096]{2,1,0:T(8,128)(2,1)}, bf16[2,...) while((s32[]{:T(128)}, bf16[4,16,1024]{2,1,0:T(8,128)(2,1)S(1)}, ...), condition=%wide.region_1.2_spmd, body=%wide.region_0.1_spmd.sunk | while | flops 571719680 | bytes 44500084 | solution.py:56
  88.0 8.2 fusion.409
  105.7 8.2 fusion.409
  123.4 8.2 fusion.409
  141.1 8.2 fusion.409
  172.2 91.9 %reduce-scatter.2.cloned.1.call-done = f32[2,64,1024]{2,1,0:T(8,128)} async-done(((f32[2,1024,1024]{2,1,0:T(8,128)}), f32[2,64,1024]{2,1,0:T(8,128)}) %reduce-scatter.2.cloned.1.call-update) | async-done | bytes 524304 | tf_op jit(solution)/shard_map/reduce_scatter | solution.py:72
  265.2 549.5 %while.59 = (s32[]{:T(128)}, f32[2,1024,4096]{2,1,0:T(8,128)}, f32[2,4096,1024]{2,1,0:T(8,128)}, f32[1024,1024]{1,0:T(8,128)}, bf16[4,32,1024]{2,1,0:T(8,128)(2,...) while((s32[]{:T(128)}, f32[2,1024,4096]{2,1,0:T(8,128)}, ...), condition=%wide.region_16.17_spmd.clone, body=%wide.region_15.16_spmd.clone.sunk | while | flops 3149725696 | bytes 416809312 | solution.py:49
  310.0 8.1 convolution_bitcast_fusion.23
  318.1 26.8 %maximum_add_fusion.11 = f32[2,4096,1024]{2,1,0:T(8,128)} fusion(f32[1,4096,1024]{2,1,0:T(8,128)} %convolution_bitcast_fusion.22, f32[1,4096,1024]{2,1,0:T(8,128)} %convolution_bitcast_fusion.23, f32[2,4096,1024]{2,1,0:T(8,128)} %get-tuple-element.760, pred[]{:T(512)S(6)} %compare.7), kind=kLoop, calls=%fused_computation.169.clone.1 | loop fusion | flops 25165824 | bytes 100663296 | tf_op jit(solution)/shard_map/while/body/eval_jaxpr/add | solution.py:46
  353.0 8.9 convolution_bitcast_fusion.21
  362.0 24.5 %maximum_add_fusion.10 = f32[2,1024,4096]{2,1,0:T(8,128)} fusion(f32[1,1024,4096]{2,1,0:T(8,128)} %convolution_bitcast_fusion.20, f32[1,1024,4096]{2,1,0:T(8,128)} %convolution_bitcast_fusion.21, f32[2,1024,4096]{2,1,0:T(8,128)} %get-tuple-element.759, pred[]{:T(512)S(6)} %compare.7), kind=kLoop, calls=%fused_computation.168.clone.1 | loop fusion | flops 25165824 | bytes 100663296 | tf_op jit(solution)/shard_map/while/body/eval_jaxpr/add | solution.py:46
  415.3 8.8 select_add_fusion.5
  432.1 8.1 convolution_bitcast_fusion.23
  440.3 33.4 %maximum_add_fusion.11 = f32[2,4096,1024]{2,1,0:T(8,128)} fusion(f32[1,4096,1024]{2,1,0:T(8,128)} %convolution_bitcast_fusion.22, f32[1,4096,1024]{2,1,0:T(8,128)} %convolution_bitcast_fusion.23, f32[2,4096,1024]{2,1,0:T(8,128)} %get-tuple-element.760, pred[]{:T(512)S(6)} %compare.7), kind=kLoop, calls=%fused_computation.169.clone.1 | loop fusion | flops 25165824 | bytes 100663296 | tf_op jit(solution)/shard_map/while/body/eval_jaxpr/add | solution.py:46
  481.8 8.9 convolution_bitcast_fusion.21
  490.7 33.4 %maximum_add_fusion.10 = f32[2,1024,4096]{2,1,0:T(8,128)} fusion(f32[1,1024,4096]{2,1,0:T(8,128)} %convolution_bitcast_fusion.20, f32[1,1024,4096]{2,1,0:T(8,128)} %convolution_bitcast_fusion.21, f32[2,1024,4096]{2,1,0:T(8,128)} %get-tuple-element.759, pred[]{:T(512)S(6)} %compare.7), kind=kLoop, calls=%fused_computation.168.clone.1 | loop fusion | flops 25165824 | bytes 100663296 | tf_op jit(solution)/shard_map/while/body/eval_jaxpr/add | solution.py:46
  553.0 8.8 select_add_fusion.5
  577.9 33.4 %maximum_add_fusion.11 = f32[2,4096,1024]{2,1,0:T(8,128)} fusion(f32[1,4096,1024]{2,1,0:T(8,128)} %convolution_bitcast_fusion.22, f32[1,4096,1024]{2,1,0:T(8,128)} %convolution_bitcast_fusion.23, f32[2,4096,1024]{2,1,0:T(8,128)} %get-tuple-element.760, pred[]{:T(512)S(6)} %compare.7), kind=kLoop, calls=%fused_computation.169.clone.1 | loop fusion | flops 25165824 | bytes 100663296 | tf_op jit(solution)/shard_map/while/body/eval_jaxpr/add | solution.py:46
  619.5 8.9 convolution_bitcast_fusion.21
  628.4 33.4 %maximum_add_fusion.10 = f32[2,1024,4096]{2,1,0:T(8,128)} fusion(f32[1,1024,4096]{2,1,0:T(8,128)} %convolution_bitcast_fusion.20, f32[1,1024,4096]{2,1,0:T(8,128)} %convolution_bitcast_fusion.21, f32[2,1024,4096]{2,1,0:T(8,128)} %get-tuple-element.759, pred[]{:T(512)S(6)} %compare.7), kind=kLoop, calls=%fused_computation.168.clone.1 | loop fusion | flops 25165824 | bytes 100663296 | tf_op jit(solution)/shard_map/while/body/eval_jaxpr/add | solution.py:46
  690.6 8.8 select_add_fusion.5
  707.5 8.1 convolution_bitcast_fusion.23
  715.6 33.4 %maximum_add_fusion.11 = f32[2,4096,1024]{2,1,0:T(8,128)} fusion(f32[1,4096,1024]{2,1,0:T(8,128)} %convolution_bitcast_fusion.22, f32[1,4096,1024]{2,1,0:T(8,128)} %convolution_bitcast_fusion.23, f32[2,4096,1024]{2,1,0:T(8,128)} %get-tuple-element.760, pred[]{:T(512)S(6)} %compare.7), kind=kLoop, calls=%fused_computation.169.clone.1 | loop fusion | flops 25165824 | bytes 100663296 | tf_op jit(solution)/shard_map/while/body/eval_jaxpr/add | solution.py:46
  757.1 8.9 convolution_bitcast_fusion.21
  766.1 33.4 %maximum_add_fusion.10 = f32[2,1024,4096]{2,1,0:T(8,128)} fusion(f32[1,1024,4096]{2,1,0:T(8,128)} %convolution_bitcast_fusion.20, f32[1,1024,4096]{2,1,0:T(8,128)} %convolution_bitcast_fusion.21, f32[2,1024,4096]{2,1,0:T(8,128)} %get-tuple-element.759, pred[]{:T(512)S(6)} %compare.7), kind=kLoop, calls=%fused_computation.168.clone.1 | loop fusion | flops 25165824 | bytes 100663296 | tf_op jit(solution)/shard_map/while/body/eval_jaxpr/add | solution.py:46
  816.3 516.5 %while.58 = (s32[]{:T(128)}, f32[2,1024,4096]{2,1,0:T(8,128)}, f32[2,4096,1024]{2,1,0:T(8,128)}, f32[1024,1024]{1,0:T(8,128)}, bf16[4,16,1024]{2,1,0:T(8,128)(2,...) while((s32[]{:T(128)}, f32[2,1024,4096]{2,1,0:T(8,128)}, ...), condition=%wide.region_10.11_spmd.clone, body=%wide.region_9.10_spmd.clone.sunk | while | flops 1601077248 | bytes 408158368 | solution.py:49
  865.5 26.8 %maximum_add_fusion.9 = f32[2,4096,1024]{2,1,0:T(8,128)} fusion(f32[1,4096,1024]{2,1,0:T(8,128)} %convolution_bitcast_fusion.18, f32[1,4096,1024]{2,1,0:T(8,128)} %convolution_bitcast_fusion.19, f32[2,4096,1024]{2,1,0:T(8,128)} %get-tuple-element.727, pred[]{:T(512)S(6)} %compare.6), kind=kLoop, calls=%fused_computation.99.clone.1 | loop fusion | flops 25165824 | bytes 100663296 | tf_op jit(solution)/shard_map/while/body/eval_jaxpr/add | solution.py:46
  908.4 24.5 %maximum_add_fusion.8 = f32[2,1024,4096]{2,1,0:T(8,128)} fusion(f32[1,1024,4096]{2,1,0:T(8,128)} %convolution_bitcast_fusion.16, f32[1,1024,4096]{2,1,0:T(8,128)} %convolution_bitcast_fusion.17, f32[2,1024,4096]{2,1,0:T(8,128)} %get-tuple-element.726, pred[]{:T(512)S(6)} %compare.6), kind=kLoop, calls=%fused_computation.98.clone.1 | loop fusion | flops 25165824 | bytes 100663296 | tf_op jit(solution)/shard_map/while/body/eval_jaxpr/add | solution.py:46
  958.7 8.4 select_add_fusion.4
  983.3 33.4 %maximum_add_fusion.9 = f32[2,4096,1024]{2,1,0:T(8,128)} fusion(f32[1,4096,1024]{2,1,0:T(8,128)} %convolution_bitcast_fusion.18, f32[1,4096,1024]{2,1,0:T(8,128)} %convolution_bitcast_fusion.19, f32[2,4096,1024]{2,1,0:T(8,128)} %get-tuple-element.727, pred[]{:T(512)S(6)} %compare.6), kind=kLoop, calls=%fused_computation.99.clone.1 | loop fusion | flops 25165824 | bytes 100663296 | tf_op jit(solution)/shard_map/while/body/eval_jaxpr/add | solution.py:46
  1032.8 33.4 %maximum_add_fusion.8 = f32[2,1024,4096]{2,1,0:T(8,128)} fusion(f32[1,1024,4096]{2,1,0:T(8,128)} %convolution_bitcast_fusion.16, f32[1,1024,4096]{2,1,0:T(8,128)} %convolution_bitcast_fusion.17, f32[2,1024,4096]{2,1,0:T(8,128)} %get-tuple-element.726, pred[]{:T(512)S(6)} %compare.6), kind=kLoop, calls=%fused_computation.98.clone.1 | loop fusion | flops 25165824 | bytes 100663296 | tf_op jit(solution)/shard_map/while/body/eval_jaxpr/add | solution.py:46
  1092.0 8.4 select_add_fusion.4
  1116.6 33.4 %maximum_add_fusion.9 = f32[2,4096,1024]{2,1,0:T(8,128)} fusion(f32[1,4096,1024]{2,1,0:T(8,128)} %convolution_bitcast_fusion.18, f32[1,4096,1024]{2,1,0:T(8,128)} %convolution_bitcast_fusion.19, f32[2,4096,1024]{2,1,0:T(8,128)} %get-tuple-element.727, pred[]{:T(512)S(6)} %compare.6), kind=kLoop, calls=%fused_computation.99.clone.1 | loop fusion | flops 25165824 | bytes 100663296 | tf_op jit(solution)/shard_map/while/body/eval_jaxpr/add | solution.py:46
  1166.1 33.4 %maximum_add_fusion.8 = f32[2,1024,4096]{2,1,0:T(8,128)} fusion(f32[1,1024,4096]{2,1,0:T(8,128)} %convolution_bitcast_fusion.16, f32[1,1024,4096]{2,1,0:T(8,128)} %convolution_bitcast_fusion.17, f32[2,1024,4096]{2,1,0:T(8,128)} %get-tuple-element.726, pred[]{:T(512)S(6)} %compare.6), kind=kLoop, calls=%fused_computation.98.clone.1 | loop fusion | flops 25165824 | bytes 100663296 | tf_op jit(solution)/shard_map/while/body/eval_jaxpr/add | solution.py:46
  1225.2 8.4 select_add_fusion.4
  1249.9 33.4 %maximum_add_fusion.9 = f32[2,4096,1024]{2,1,0:T(8,128)} fusion(f32[1,4096,1024]{2,1,0:T(8,128)} %convolution_bitcast_fusion.18, f32[1,4096,1024]{2,1,0:T(8,128)} %convolution_bitcast_fusion.19, f32[2,4096,1024]{2,1,0:T(8,128)} %get-tuple-element.727, pred[]{:T(512)S(6)} %compare.6), kind=kLoop, calls=%fused_computation.99.clone.1 | loop fusion | flops 25165824 | bytes 100663296 | tf_op jit(solution)/shard_map/while/body/eval_jaxpr/add | solution.py:46
  1299.4 33.4 %maximum_add_fusion.8 = f32[2,1024,4096]{2,1,0:T(8,128)} fusion(f32[1,1024,4096]{2,1,0:T(8,128)} %convolution_bitcast_fusion.16, f32[1,1024,4096]{2,1,0:T(8,128)} %convolution_bitcast_fusion.17, f32[2,1024,4096]{2,1,0:T(8,128)} %get-tuple-element.726, pred[]{:T(512)S(6)} %compare.6), kind=kLoop, calls=%fused_computation.98.clone.1 | loop fusion | flops 25165824 | bytes 100663296 | tf_op jit(solution)/shard_map/while/body/eval_jaxpr/add | solution.py:46
  1332.8 31.9 %psum.49 = f32[]{:T(128)} all-reduce(f32[]{:T(128)} %get-tuple-element.484), channel_id=1, replica_groups=mesh['data'=16] {'data'}, use_global_device_ids=true, to_apply=%region_8.9 | all-reduce | flops 1 | bytes 8 | tf_op jit(solution)/shard_map/psum | solution.py:67
  1365.4 894.0 %all-reduce.6.cloned.1.call-done = (f32[2,1024,4096]{2,1,0:T(8,128)}, f32[2,4096,1024]{2,1,0:T(8,128)}, f32[1024,1024]{1,0:T(8,128)}, f32[2,1024,4096]{2,1,0:T(8,128)}, f32[1024,1024]{1,0:T(8,128)}) async-done(((f32[2,1024,4096]{2,1,0:T(8,128)}, f32[2,4096,1024]{2,1,0:T(8,128)}, f32[1024,1024]{1,0:T(8,128)}, f32[2,1024,4096]{2,1,0:T(8,128)}, f32[1024,1024]{1,0:T(8,128)}), (f32[2,1024,4096]{2,1,0:T(8,128)}, ...) | async-done | bytes 109051920 | tf_op jit(solution)/shard_map/psum | solution.py:75
  2259.4 24.3 %copy.67 = f32[2,1024,4096]{2,1,0:T(8,128)} copy(f32[2,1024,4096]{2,1,0:T(8,128)} %get-tuple-element.781) | data formatting | bytes 67108864
  2291.2 12.6 copy.68
  2305.9 27.2 %copy.70 = f32[2,1024,4096]{2,1,0:T(8,128)} copy(f32[2,1024,4096]{2,1,0:T(8,128)} %get-tuple-element.784) | data formatting | bytes 67108864
  2337.3 12.6 copy.71
  (233 shorter events, 548.8 us)
Async XLA Ops:
  7.2 151.6 %all-gather.2.cloned.1.call-start = ((), (), s32[]{:S(2)}) async-start(), calls=%async_computation.1 | async-start | bytes 4456448 | tf_op jit(solution)/shard_map/all_gather | solution.py:58
  7.2 80.7 %copy-start.14 = (bf16[64,1024]{1,0:T(8,128)(2,1)S(1)}, bf16[64,1024]{1,0:T(8,128)(2,1)}, u32[]{:S(2)}) copy-start(bf16[64,1024]{1,0:T(8,128)(2,1)} %param.17) | copy-start | bytes 393220
  7.2 14.0 copy-start.2
  27.2 14.0 copy-start.2
  47.1 14.0 copy-start.2
  67.1 14.0 copy-start.2
  87.0 177.1 %reduce-scatter.2.cloned.1.call-start = ((), (), s32[]{:S(2)}) async-start(), calls=%async_computation.2 | async-start | bytes 8912896 | tf_op jit(solution)/shard_map/reduce_scatter | solution.py:72
  87.9 12.8 copy-start.4
  105.7 12.8 copy-start.4
  123.4 12.8 copy-start.4
  141.1 12.8 copy-start.4
  158.8 106.4 %copy-start.3 = (bf16[1024,1024]{1,0:T(8,128)(2,1)S(1)}, bf16[1024,1024]{1,0:T(8,128)(2,1)}, u32[]{:S(2)}) copy-start(bf16[1024,1024]{1,0:T(8,128)(2,1)} %get-tuple-element.810) | copy-start | bytes 6291460
  168.4 1197.0 %all-reduce.4.cloned.1.call-start = ((), (), s32[]{:S(2)}) async-start(), calls=%async_computation.3 | async-start | bytes 67108864 | tf_op jit(solution)/shard_map/psum | solution.py:76
  265.5 6.1 copy-start.12
  265.5 11.8 copy-start.1
  318.1 26.8 %copy-start.9 = (bf16[32,4096]{1,0:T(8,128)(2,1)S(1)}, bf16[32,4096]{1,0:T(8,128)(2,1)}, u32[]{:S(2)}) copy-start(bf16[32,4096]{1,0:T(8,128)(2,1)} %copy-done.8) | copy-start | bytes 786436 | tf_op jit(solution)/shard_map/while
  344.9 8.1 copy-start.7
  362.0 24.6 %copy-start.13 = (bf16[4,32,1024]{2,1,0:T(8,128)(2,1)S(1)}, bf16[4,32,1024]{2,1,0:T(8,128)(2,1)}, u32[]{:S(2)}) copy-start(bf16[4,32,1024]{2,1,0:T(8,128)(2,1)} %copy-done.12) | copy-start | bytes 786436 | tf_op jit(solution)/shard_map/while
  386.5 6.1 copy-start.12
  386.5 11.8 copy-start.1
  440.3 33.4 %copy-start.9 = (bf16[32,4096]{1,0:T(8,128)(2,1)S(1)}, bf16[32,4096]{1,0:T(8,128)(2,1)}, u32[]{:S(2)}) copy-start(bf16[32,4096]{1,0:T(8,128)(2,1)} %copy-done.8) | copy-start | bytes 786436 | tf_op jit(solution)/shard_map/while
  473.7 8.1 copy-start.7
  490.7 33.4 %copy-start.13 = (bf16[4,32,1024]{2,1,0:T(8,128)(2,1)S(1)}, bf16[4,32,1024]{2,1,0:T(8,128)(2,1)}, u32[]{:S(2)}) copy-start(bf16[4,32,1024]{2,1,0:T(8,128)(2,1)} %copy-done.12) | copy-start | bytes 786436 | tf_op jit(solution)/shard_map/while
  524.2 6.1 copy-start.12
  524.2 11.8 copy-start.1
  577.9 33.4 %copy-start.9 = (bf16[32,4096]{1,0:T(8,128)(2,1)S(1)}, bf16[32,4096]{1,0:T(8,128)(2,1)}, u32[]{:S(2)}) copy-start(bf16[32,4096]{1,0:T(8,128)(2,1)} %copy-done.8) | copy-start | bytes 786436 | tf_op jit(solution)/shard_map/while
  611.4 8.1 copy-start.7
  628.4 33.4 %copy-start.13 = (bf16[4,32,1024]{2,1,0:T(8,128)(2,1)S(1)}, bf16[4,32,1024]{2,1,0:T(8,128)(2,1)}, u32[]{:S(2)}) copy-start(bf16[4,32,1024]{2,1,0:T(8,128)(2,1)} %copy-done.12) | copy-start | bytes 786436 | tf_op jit(solution)/shard_map/while
  661.9 11.8 copy-start.1
  715.6 33.4 %copy-start.9 = (bf16[32,4096]{1,0:T(8,128)(2,1)S(1)}, bf16[32,4096]{1,0:T(8,128)(2,1)}, u32[]{:S(2)}) copy-start(bf16[32,4096]{1,0:T(8,128)(2,1)} %copy-done.8) | copy-start | bytes 786436 | tf_op jit(solution)/shard_map/while
  749.0 8.1 copy-start.7
  766.1 33.4 %copy-start.13 = (bf16[4,32,1024]{2,1,0:T(8,128)(2,1)S(1)}, bf16[4,32,1024]{2,1,0:T(8,128)(2,1)}, u32[]{:S(2)}) copy-start(bf16[4,32,1024]{2,1,0:T(8,128)(2,1)} %copy-done.12) | copy-start | bytes 786436 | tf_op jit(solution)/shard_map/while
  814.8 1444.6 %all-reduce.6.cloned.1.call-start = ((), (), s32[]{:S(2)}) async-start(), calls=%async_computation.4 | async-start | bytes 218103808 | tf_op jit(solution)/shard_map/psum | solution.py:75
  816.3 10.9 copy-start
  932.9 10.9 copy-start
  1066.2 10.9 copy-start
  1199.5 10.9 copy-start
  2259.4 31.8 %copy-start.6 = (f32[2,4096,1024]{2,1,0:T(8,128)S(1)}, f32[2,4096,1024]{2,1,0:T(8,128)}, u32[]{:S(2)}) copy-start(f32[2,4096,1024]{2,1,0:T(8,128)} %get-tuple-element.782) | copy-start | bytes 100663296
  2291.2 12.6 copy-start.11
  2303.7 29.3 %slice-start = ((s8[33554432]{0:T(1024)(128)(4,1)}), s8[4194304]{0:T(1024)(128)(4,1)S(1)}, s32[]{:S(2)}) async-start(s8[33554432]{0:T(1024)(128)(4,1)} %bitcast.367), calls=%async_computation.5 | async-start | bytes 8388608
  2305.9 27.2 %slice-start.1 = ((s8[33554432]{0:T(1024)(128)(4,1)}), s8[4194304]{0:T(1024)(128)(4,1)S(1)}, s32[]{:S(2)}) async-start(s8[33554432]{0:T(1024)(128)(4,1)} %bitcast.367), calls=%async_computation.6 | async-start | bytes 8388608
  2305.9 27.2 %slice-start.2 = ((s8[33554432]{0:T(1024)(128)(4,1)}), s8[4194304]{0:T(1024)(128)(4,1)S(1)}, s32[]{:S(2)}) async-start(s8[33554432]{0:T(1024)(128)(4,1)} %bitcast.367), calls=%async_computation.7 | async-start | bytes 8388608
  2305.9 27.2 %slice-start.3 = ((s8[33554432]{0:T(1024)(128)(4,1)}), s8[4194304]{0:T(1024)(128)(4,1)S(1)}, s32[]{:S(2)}) async-start(s8[33554432]{0:T(1024)(128)(4,1)} %bitcast.367), calls=%async_computation.8 | async-start | bytes 8388608
  2305.9 27.2 %slice-start.4 = ((s8[33554432]{0:T(1024)(128)(4,1)}), s8[4194304]{0:T(1024)(128)(4,1)S(1)}, s32[]{:S(2)}) async-start(s8[33554432]{0:T(1024)(128)(4,1)} %bitcast.367), calls=%async_computation.9 | async-start | bytes 8388608
  2305.9 29.0 %slice-start.5 = ((s8[33554432]{0:T(1024)(128)(4,1)}), s8[4194304]{0:T(1024)(128)(4,1)S(1)}, s32[]{:S(2)}) async-start(s8[33554432]{0:T(1024)(128)(4,1)} %bitcast.367), calls=%async_computation.10 | async-start | bytes 8388608
  2305.9 30.2 %slice-start.6 = ((s8[33554432]{0:T(1024)(128)(4,1)}), s8[4194304]{0:T(1024)(128)(4,1)S(1)}, s32[]{:S(2)}) async-start(s8[33554432]{0:T(1024)(128)(4,1)} %bitcast.367), calls=%async_computation.11 | async-start | bytes 8388608
  2305.9 31.4 %slice-start.7 = ((s8[33554432]{0:T(1024)(128)(4,1)}), s8[4194304]{0:T(1024)(128)(4,1)S(1)}, s32[]{:S(2)}) async-start(s8[33554432]{0:T(1024)(128)(4,1)} %bitcast.367), calls=%async_computation.12 | async-start | bytes 8388608
  2337.3 12.6 copy-start.10
  (8 other events, 21.3 us)
Sparse Core Ops, SparseCore 0:
  87.1 37.7 all-gather.1
  168.5 95.5 reduce-scatter.1
  814.9 314.9 all-reduce.3
  1333.0 926.3 all-reduce.5
where the time goes:
time: 2370 us; the launch traced here: 2360 us
  waiting for transfers between devices  986 us (42%)
  matrix products  709 us (30%)
  other arithmetic  506 us (21%)
  local copies, waits for them, and re-layouts  94.2 us (4%)
  blocking collectives  31.9 us (1%)
    psum x1, waiting for transfers between devices, local_step(): q_one, q_two, q_pgrad = lax.psum(q_grads, 'data')  894 us
    add x16, other arithmetic, body(): old_sum + new_part  504 us
    dot_general x16, matrix products, tower_backward(): lax.dot_general(h_in, pre_grad, ROWS_CONTRACT, preferred_element_type=jnp...  133 us
    dot_general x16, matrix products, tower_backward(): lax.dot_general(act_bf, resid_bf, ROWS_CONTRACT, preferred_element_type=j...  130 us
    dot_general x16, matrix products, tower_forward(): jnp.dot(act_bf, w_two[layer], preferred_element_type=jnp.float32)  113 us
    dot_general x16, matrix products, tower_backward(): lax.dot_general(resid_bf, w_two[layer], LAST_CONTRACT, preferred_element_...  96.8 us
    unnamed x38, local copies, waits for them, and re-layouts  94 us
    reduce_scatter x1, waiting for transfers between devices, local_step(): lax.psum_scatter(doc_part.reshape(2, global_batch, rep_width), 'data', sc...  91.9 us
  transfers between devices with their start and end apart: 4, of which 2 were waited for; matrix products, arithmetic and copies ran while one was open for 25% of the time, Pallas kernels for 0%

commit v1 on v0

v1 whole, which is shorter than its diff:
```python
import jax
import jax.numpy as jnp
from jax import lax
from jax.sharding import PartitionSpec as P

ROWS_CONTRACT = (((0,), (0,)), ((), ()))
LAST_CONTRACT = (((1,), (1,)), ((), ()))
F32 = jnp.float32
BF16 = jnp.bfloat16


def dot(a, b):
    return jnp.dot(a, b, preferred_element_type=F32)


def dot_nt(a, b):
    return lax.dot_general(a, b, LAST_CONTRACT, preferred_element_type=F32)


def dot_tn(a, b):
    return lax.dot_general(a, b, ROWS_CONTRACT, preferred_element_type=F32)


def ffn(h, w1, w2):
    u = jax.nn.gelu(dot(h, w1)).astype(BF16)
    return (h.astype(F32) + dot(u, w2)).astype(BF16)


def gather(x):
    return lax.all_gather(x, 'data', axis=0, tiled=True)


def hidden_grads(h, e_bf, w1, w2):
    pre = dot(h, w1)
    u = jax.nn.gelu(pre).astype(BF16)
    t = dot_nt(e_bf, w2)
    delta = jax.vjp(jax.nn.gelu, pre)[1](t)[0].astype(BF16)
    return u, delta


def layer_grads(h, e_bf, w1, w2):
    u, delta = hidden_grads(h, e_bf, w1, w2)
    return dot_tn(h, delta), dot_tn(u, e_bf)


def local_step(q_loc, d_loc, temperature, q_w1, q_w2, q_proj, d_w1, d_w2, d_proj):
    rows = q_loc.shape[0]
    me = lax.axis_index('data')
    d_rows = d_loc.reshape(2 * rows, d_loc.shape[2])
    d_h = [d_rows]
    q_h = [q_loc]
    for k in range(2):
        d_h.append(ffn(d_h[k], d_w1[k], d_w2[k]))
    for k in range(2):
        q_h.append(ffn(q_h[k], q_w1[k], q_w2[k]))
    d_all = [gather(h) for h in d_h]
    q_all = [gather(h) for h in q_h]
    docs = dot(d_all[2], d_proj).astype(BF16)
    queries = dot(q_all[2], q_proj).astype(BF16)
    batch = queries.shape[0]
    logits = dot_nt(queries, docs) / temperature
    row = jnp.arange(batch)
    target = jnp.arange(2 * batch)[None, :] == ((row // rows) * 2 * rows + row % rows)[:, None]
    log_norm = jax.nn.logsumexp(logits, axis=1)
    pos = jnp.sum(jnp.where(target, logits, 0.0), axis=1)
    loss = jnp.sum(log_norm - pos) / batch
    prob = jnp.exp(logits - log_norm[:, None])
    grad = ((prob - target.astype(F32)) / (batch * temperature)).astype(BF16)
    q_up = dot(grad, docs).astype(BF16)
    d_up = dot_tn(grad, queries).astype(BF16)

    def tower(h_own, h_all, up, w1, w2, proj):
        own_rows = h_own[0].shape[0]
        g_proj = dot_tn(h_all[2], up)
        e1 = dot_nt(up, proj)
        e1_bf = e1.astype(BF16)
        e1_own = lax.dynamic_slice_in_dim(e1, me * own_rows, own_rows, 0)
        delta_own = hidden_grads(h_own[1], e1_own.astype(BF16), w1[1], w2[1])[1]
        e0_own = (e1_own + dot_nt(delta_own, w1[1])).astype(BF16)
        e0_bf = gather(e0_own)
        one1, two1 = layer_grads(h_all[1], e1_bf, w1[1], w2[1])
        one0, two0 = layer_grads(h_all[0], e0_bf, w1[0], w2[0])
        return jnp.stack([one0, one1]), jnp.stack([two0, two1]), g_proj

    d_grads = tower(d_h, d_all, d_up, d_w1, d_w2, d_proj)
    q_grads = tower(q_h, q_all, q_up, q_w1, q_w2, q_proj)
    return (loss, *q_grads, *d_grads)


def solution(mesh):
    specs_in = (P('data', None), P(None, 'data', None), P(), P(), P(), P(), P(), P(), P())
    specs_out = (P(), P(), P(), P(), P(), P(), P())
    return jax.shard_map(local_step, mesh=mesh, in_specs=specs_in, out_specs=specs_out, check_vma=False)
```

time: 2370 us -> 752 us (0.32)
  waiting for transfers between devices: 986 us -> 59.1 us
  other arithmetic: 506 us -> 96.4 us
  matrix products: 709 us -> 505 us
  blocking collectives: 31.9 us -> 0 us
  local copies, waits for them, and re-layouts: 94.2 us -> 64.6 us
    psum x2 -> x0, waiting for transfers between devices: 894 us -> none  [the longest x1 894 us: local_step(): q_one, q_two, q_pgrad = lax.psum(q_grads, 'data')]
    add x17 -> x1, other arithmetic: 504 us -> 0.01 us  [local_step(): row // rows * 2 * rows + row % rows]
    dot_general x123 -> x31, matrix products: 709 us -> 505 us  [the longest x11 232 us: dot_tn(): return lax.dot_general(a, b, ROWS_CONTRACT, preferred_element_type=F32)]
    reduce_scatter x1 -> x0, waiting for transfers between devices: 91.9 us -> none  [local_step(): lax.psum_scatter(doc_part.reshape(2, global_batch, rep_width), 'data', sc...]
    another operation x0 -> x4, other arithmetic: none -> 89.8 us  [tower(): return (jnp.stack([one0, one1]), jnp.stack([two0, two1]), g_proj)]
    all_gather x1 -> x8, waiting for transfers between devices: 0.01 us -> 57.3 us  [gather(): return lax.all_gather(x, 'data', axis=0, tiled=True)]
    psum x1 -> x0, blocking collectives: 31.9 us -> none  [local_step(): loss = lax.psum(jnp.sum(log_norm - pos_logit), 'data') / global_batch]
    unnamed x38 -> x36, local copies, waits for them, and re-layouts: 94 us -> 64.6 us
  transfers between devices with their start and end apart: 4 -> 8, of which waited for: 2 -> 3; matrix products, arithmetic and copies ran while one was open for 25% -> 65% of each run, Pallas kernels for 0% -> 0%
where the time goes in v1:
time: 752 us; the launch traced here: 743 us
  matrix products  505 us (67%)
  other arithmetic  96.4 us (13%)
  local copies, waits for them, and re-layouts  64.6 us (9%)
  waiting for transfers between devices  59.1 us (8%)
  between operations  17.2 us (2%)
    dot_general x11, matrix products, dot_tn(): return lax.dot_general(a, b, ROWS_CONTRACT, preferred_element_type=F32)  232 us
    dot_general x13, matrix products, dot(): return jnp.dot(a, b, preferred_element_type=F32)  141 us
    dot_general x7, matrix products, dot_nt(): return lax.dot_general(a, b, LAST_CONTRACT, preferred_element_type=F32)  132 us
    another operation x4, other arithmetic, tower(): return (jnp.stack([one0, one1]), jnp.stack([two0, two1]), g_proj)  89.8 us
    unnamed x36, local copies, waits for them, and re-layouts  64.6 us
    all_gather x8, waiting for transfers between devices, gather(): return lax.all_gather(x, 'data', axis=0, tiled=True)  57.3 us
  transfers between devices with their start and end apart: 8, of which 3 were waited for; matrix products, arithmetic and copies ran while one was open for 65% of the time, Pallas kernels for 0%

profile of v1, /device:TPU:0, one launch (start us, length us, event | category | flops | bytes accessed | tf_op | source)
XLA Modules:
  0.0 743.0 jit_solution(11498990529792505296)
XLA Ops:
  7.2 9.9 %fusion.186 = bf16[64,1024]{1,0:T(8,128)(2,1)} fusion(bf16[2,4096,1024]{2,1,0:T(8,128)(2,1)} %param.13, bf16[64,1024]{1,0:T(8,128)(2,1)} %param.9, bf16[2,1024,4096]{2,1,0:T(8,128)(2,1)} %param.12), kind=kOutput, calls=%fused_computation.168 | convolution fusion | flops 1076297728 | bytes 17170432 | tf_op jit(solution)/shard_map/dot_general | solution.py:13
  17.2 0.7 all-gather.15.cloned.1.call-update
  17.9 5.0 fusion.72
  23.0 1.0 copy-done.10
  23.9 5.6 fusion.180
  29.6 8.5 %fusion.168 = bf16[128,1024]{1,0:T(8,128)(2,1)S(1)} fusion(bf16[2,4096,1024]{2,1,0:T(8,128)(2,1)} %param.16, bf16[128,1024]{1,0:T(8,128)(2,1)S(1)} %bitcast.179, bf16[2,1024,4096]{2,1,0:T(8,128)(2,1)} %param.15), kind=kOutput, calls=%fused_computation.162 | convolution fusion | flops 2152595456 | bytes 17563648 | tf_op jit(solution)/shard_map/dot_general | solution.py:13
  38.1 4.7 fusion.52
  42.9 1.3 copy-done.12
  44.2 5.7 fusion.162
  50.0 0.5 all-gather.23.cloned.1.call-update
  50.5 0.5 all-gather.21.cloned.1.call-update
  52.0 16.2 %fusion.68 = f32[1024,4096]{1,0:T(8,128)} fusion(bf16[1024,1024]{1,0:T(8,128)(2,1)} %all-gather.17.cloned.1.call-done, bf16[2,1024,4096]{2,1,0:T(8,128)(2,1)} %param.12), kind=kOutput, calls=%fused_computation.82 | convolution fusion | flops 8589934592 | bytes 27262976 | tf_op jit(solution)/shard_map/dot_general | solution.py:13
  68.2 10.8 %all-gather.15.cloned.1.call-done = bf16[1024,1024]{1,0:T(8,128)(2,1)} async-done(((bf16[64,1024]{1,0:T(8,128)(2,1)}), bf16[1024,1024]{1,0:T(8,128)(2,1)}) %all-gather.15.cloned.1.call-update) | async-done | bytes 2097168 | tf_op jit(solution)/shard_map/all_gather | solution.py:30
  78.9 16.0 %fusion.78 = f32[1024,4096]{1,0:T(8,128)} fusion(bf16[1024,1024]{1,0:T(8,128)(2,1)} %all-gather.15.cloned.1.call-done, bf16[2,1024,4096]{2,1,0:T(8,128)(2,1)} %param.12), kind=kOutput, calls=%fused_computation.92 | convolution fusion | flops 8589934592 | bytes 27262976 | tf_op jit(solution)/shard_map/dot_general | solution.py:13
  94.9 14.6 %all-gather.9.cloned.1.call-done = bf16[1024,1024]{1,0:T(8,128)(2,1)} async-done(((bf16[64,1024]{1,0:T(8,128)(2,1)}), bf16[1024,1024]{1,0:T(8,128)(2,1)}) %all-gather.9.cloned.1.call-update) | async-done | bytes 2097168 | tf_op jit(solution)/shard_map/all_gather | solution.py:30
  109.5 5.9 convolution_convert_fusion.3
  115.4 31.9 %all-gather.11.cloned.1.call-done = bf16[2048,1024]{1,0:T(8,128)(2,1)} async-done(((bf16[128,1024]{1,0:T(8,128)(2,1)}), bf16[2048,1024]{1,0:T(8,128)(2,1)}) %all-gather.11.cloned.1.call-update) | async-done | bytes 4194320 | tf_op jit(solution)/shard_map/all_gather | solution.py:30
  147.2 7.5 %convolution_convert_fusion.1 = bf16[2048,1024]{1,0:T(8,128)(2,1)S(1)} fusion(bf16[2048,1024]{1,0:T(8,128)(2,1)} %all-gather.11.cloned.1.call-done, bf16[1024,1024]{1,0:T(8,128)(2,1)S(1)} %copy-done), kind=kOutput, calls=%fused_computation.130 | convolution fusion | flops 4297064448 | bytes 10485760 | tf_op jit(solution)/shard_map/dot_general | solution.py:13
  154.7 4.7 fusion.320
  159.4 3.2 select_reduce_fusion
  162.6 0.6 subtract_reduce_fusion
  163.2 2.8 divide_convert_fusion
  166.0 4.7 convolution_convert_fusion.2
  170.8 6.4 convolution_convert_fusion
  177.2 4.4 fusion.321
  181.6 12.0 %fusion.183 = bf16[64,1024]{1,0:T(8,128)(2,1)} fusion(bf16[2,1024,4096]{2,1,0:T(8,128)(2,1)} %param.12, f32[64,4096]{1,0:T(8,128)S(1)} %copy-done.11, bf16[2,4096,1024]{2,1,0:T(8,128)(2,1)} %param.13, f32[1024,1024]{1,0:T(8,128)} %fusion.321, s32[]{:T(128)S(6)} %select_n.48), kind=kOutput, calls=%fused_computation.167 | convolution fusion | flops 1079181312 | bytes 18482176 | tf_op jit(solution)/shard_map/dot_general | solution.py:17
  193.6 19.7 %convolution_bitcast_fusion = f32[1,4096,1024]{2,1,0:T(8,128)} fusion(f32[1024,4096]{1,0:T(8,128)} %fusion.68, f32[1024,1024]{1,0:T(8,128)} %fusion.321), kind=kOutput, calls=%fused_computation.52 | convolution fusion | flops 8628731904 | bytes 37748736 | tf_op jit(solution)/shard_map/dot_general | solution.py:21
  213.2 25.5 %fusion.48 = f32[2048,4096]{1,0:T(8,128)} fusion(bf16[2048,1024]{1,0:T(8,128)(2,1)} %all-gather.23.cloned.1.call-done, bf16[2,1024,4096]{2,1,0:T(8,128)(2,1)} %param.15), kind=kOutput, calls=%fused_computation.62 | convolution fusion | flops 17179869184 | bytes 46137344 | tf_op jit(solution)/shard_map/dot_general | solution.py:13
  238.8 6.8 fusion.323
  246.3 13.6 %fusion.165 = bf16[128,1024]{1,0:T(8,128)(2,1)} fusion(bf16[2,1024,4096]{2,1,0:T(8,128)(2,1)} %param.15, f32[128,4096]{1,0:T(8,128)} %copy-done.12, bf16[2,4096,1024]{2,1,0:T(8,128)(2,1)} %param.16, f32[2048,1024]{1,0:T(8,128)} %fusion.323, s32[]{:T(128)S(6)} %select_n.49), kind=kOutput, calls=%fused_computation.161 | convolution fusion | flops 2158362624 | bytes 20186112 | tf_op jit(solution)/shard_map/dot_general | solution.py:17
  259.9 46.1 %fusion.379 = bf16[2048,4096]{1,0:T(8,128)(2,1)} fusion(f32[2048,4096]{1,0:T(8,128)} %fusion.48, bf16[2,4096,1024]{2,1,0:T(8,128)(2,1)} %param.16, f32[2048,1024]{1,0:T(8,128)} %fusion.323), kind=kOutput, calls=%fused_computation.17.clone.clone.clone.clone.1 | convolution fusion | flops 17349738496 | bytes 67108864 | tf_op jit(solution)/shard_map/dot_general | solution.py:17
  306.1 32.7 %fusion.40 = f32[1,4096,1024]{2,1,0:T(8,128)} fusion(f32[2048,4096]{1,0:T(8,128)} %fusion.48, f32[2048,1024]{1,0:T(8,128)} %fusion.323), kind=kOutput, calls=%fused_computation.50 | convolution fusion | flops 17257463808 | bytes 58720256 | tf_op jit(solution)/shard_map/dot_general | solution.py:21
  338.8 10.2 %fusion.324 = f32[1024,1024]{1,0:T(8,128)} fusion(bf16[2048,1024]{1,0:T(8,128)(2,1)} %all-gather.11.cloned.1.call-done, bf16[2048,1024]{1,0:T(8,128)(2,1)} %convolution_convert_fusion), kind=kOutput, calls=%fused_computation.297 | convolution fusion | flops 4294967296 | bytes 12582912 | tf_op jit(solution)/shard_map/dot_general | solution.py:21
  349.0 4.4 fusion.322
  353.4 32.7 %convolution_bitcast_fusion.2 = f32[1,1024,4096]{1,2,0:T(8,128)} fusion(bf16[1024,1024]{1,0:T(8,128)(2,1)S(1)} %copy-done.7, f32[1024,4096]{1,0:T(8,128)} %fusion.68, bf16[2,4096,1024]{2,1,0:T(8,128)(2,1)} %param.13, f32[1024,1024]{1,0:T(8,128)} %fusion.321), kind=kOutput, calls=%fused_computation.54 | convolution fusion | flops 17264803840 | bytes 48234496 | tf_op jit(solution)/shard_map/dot_general | solution.py:21
  386.1 23.8 %fusion.37 = f32[1,1024,4096]{1,2,0:T(8,128)} fusion(bf16[2048,1024]{1,0:T(8,128)(2,1)} %all-gather.23.cloned.1.call-done, bf16[2048,4096]{1,0:T(8,128)(2,1)} %fusion.379), kind=kOutput, calls=%fused_computation.49 | convolution fusion | flops 17179869184 | bytes 37748736 | tf_op jit(solution)/shard_map/dot_general | solution.py:21
  409.9 25.6 %fusion.58 = f32[2048,4096]{1,0:T(8,128)} fusion(bf16[2048,1024]{1,0:T(8,128)(2,1)} %all-gather.21.cloned.1.call-done, bf16[2,1024,4096]{2,1,0:T(8,128)(2,1)} %param.15), kind=kOutput, calls=%fused_computation.72 | convolution fusion | flops 17179869184 | bytes 46137344 | tf_op jit(solution)/shard_map/dot_general | solution.py:13
  435.5 30.7 %convolution_bitcast_fusion.3 = f32[1,1024,4096]{1,2,0:T(8,128)} fusion(bf16[1024,1024]{1,0:T(8,128)(2,1)S(1)} %copy-done.6, f32[1024,4096]{1,0:T(8,128)} %fusion.78, bf16[1024,1024]{1,0:T(8,128)(2,1)} %all-gather.13.cloned.1.call-done, bf16[2,4096,1024]{2,1,0:T(8,128)(2,1)} %param.13), kind=kOutput, calls=%fused_computation.55 | convolution fusion | flops 17263755264 | bytes 46137344 | tf_op jit(solution)/shard_map/dot_general | solution.py:21
  466.2 23.6 %pad_maximum_fusion = f32[2,1024,4096]{1,2,0:T(8,128)} fusion(f32[1,1024,4096]{1,2,0:T(8,128)} %convolution_bitcast_fusion.2, f32[1,1024,4096]{1,2,0:T(8,128)} %convolution_bitcast_fusion.3), kind=kLoop, calls=%fused_computation.18 | loop fusion | flops 8388608 | bytes 67108864 | tf_op jit(solution)/shard_map/stack | solution.py:83
  489.8 31.2 %copy.18 = f32[2,1024,4096]{2,1,0:T(8,128)} copy(f32[2,1024,4096]{1,2,0:T(8,128)} %pad_maximum_fusion) | data formatting | bytes 67108864
  521.0 18.8 %convolution_bitcast_fusion.1 = f32[1,4096,1024]{2,1,0:T(8,128)} fusion(bf16[1024,1024]{1,0:T(8,128)(2,1)S(1)} %copy-done.9, f32[1024,4096]{1,0:T(8,128)} %fusion.78), kind=kOutput, calls=%fused_computation.53 | convolution fusion | flops 8627683328 | bytes 35651584 | tf_op jit(solution)/shard_map/dot_general | solution.py:21
  539.8 23.6 %pad_maximum_fusion.1 = f32[2,4096,1024]{2,1,0:T(8,128)} fusion(f32[1,4096,1024]{2,1,0:T(8,128)} %convolution_bitcast_fusion, f32[1,4096,1024]{2,1,0:T(8,128)} %convolution_bitcast_fusion.1), kind=kLoop, calls=%fused_computation.19 | loop fusion | flops 8388608 | bytes 67108864 | tf_op jit(solution)/shard_map/stack | solution.py:83
  563.4 44.6 %fusion.375 = bf16[2048,4096]{1,0:T(8,128)(2,1)} fusion(f32[2048,4096]{1,0:T(8,128)} %fusion.58, bf16[2048,1024]{1,0:T(8,128)(2,1)} %all-gather.19.cloned.1.call-done, bf16[2,4096,1024]{2,1,0:T(8,128)(2,1)} %param.16), kind=kOutput, calls=%fused_computation.10.clone.clone.clone.clone.1 | convolution fusion | flops 17347641344 | bytes 62914560 | tf_op jit(solution)/shard_map/dot_general | solution.py:17
  608.1 21.6 %fusion.34 = f32[1,1024,4096]{1,2,0:T(8,128)S(1)} fusion(bf16[2048,1024]{1,0:T(8,128)(2,1)S(1)} %copy-done.4, bf16[2048,4096]{1,0:T(8,128)(2,1)} %fusion.375), kind=kOutput, calls=%fused_computation.48 | convolution fusion | flops 17179869184 | bytes 37748736 | tf_op jit(solution)/shard_map/dot_general | solution.py:21
  629.7 18.6 %pad_maximum_fusion.2 = f32[2,1024,4096]{1,2,0:T(8,128)} fusion(f32[1,1024,4096]{1,2,0:T(8,128)} %fusion.37, f32[1,1024,4096]{1,2,0:T(8,128)S(1)} %fusion.34), kind=kLoop, calls=%fused_computation.20 | loop fusion | flops 8388608 | bytes 67108864 | tf_op jit(solution)/shard_map/stack | solution.py:83
  648.3 31.1 %copy.19 = f32[2,1024,4096]{2,1,0:T(8,128)} copy(f32[2,1024,4096]{1,2,0:T(8,128)} %pad_maximum_fusion.2) | data formatting | bytes 67108864
  679.4 31.3 %fusion.41 = f32[1,4096,1024]{2,1,0:T(8,128)} fusion(bf16[2048,1024]{1,0:T(8,128)(2,1)} %all-gather.19.cloned.1.call-done, f32[2048,4096]{1,0:T(8,128)} %fusion.58), kind=kOutput, calls=%fused_computation.51 | convolution fusion | flops 17255366656 | bytes 54525952 | tf_op jit(solution)/shard_map/dot_general | solution.py:21
  710.7 23.9 %pad_maximum_fusion.3 = f32[2,4096,1024]{2,1,0:T(8,128)} fusion(f32[1,4096,1024]{2,1,0:T(8,128)} %fusion.40, f32[1,4096,1024]{2,1,0:T(8,128)} %fusion.41), kind=kLoop, calls=%fused_computation.21 | loop fusion | flops 8388608 | bytes 67108864 | tf_op jit(solution)/shard_map/stack | solution.py:83
  (52 shorter events, 0.7 us)
Async XLA Ops:
  7.2 140.1 %copy-start = (bf16[1024,1024]{1,0:T(8,128)(2,1)S(1)}, bf16[1024,1024]{1,0:T(8,128)(2,1)}, u32[]{:S(2)}) copy-start(bf16[1024,1024]{1,0:T(8,128)(2,1)} %param.17) | copy-start | bytes 6291460
  7.2 44.8 %all-gather.17.cloned.1.call-start = ((), (), s32[]{:S(2)}) async-start(), calls=%async_computation.4 | async-start | bytes 2228224 | tf_op jit(solution)/shard_map/all_gather | solution.py:30
  17.1 12.5 %copy-start.2 = (bf16[2,64,1024]{2,1,0:T(8,128)(2,1)S(1)}, bf16[2,64,1024]{2,1,0:T(8,128)(2,1)}, u32[]{:S(2)}) copy-start(bf16[2,64,1024]{2,1,0:T(8,128)(2,1)} %param.10) | copy-start | bytes 786436
  17.1 61.8 %all-gather.15.cloned.1.call-start = ((), (), s32[]{:S(2)}) async-start(), calls=%async_computation.3 | async-start | bytes 2228224 | tf_op jit(solution)/shard_map/all_gather | solution.py:30
  17.9 91.6 %all-gather.9.cloned.1.call-start = ((), (), s32[]{:S(2)}) async-start(), calls=%async_computation | async-start | bytes 2228224 | tf_op jit(solution)/shard_map/all_gather | solution.py:30
  23.0 1.0 copy-start.10
  29.6 117.7 %all-gather.11.cloned.1.call-start = ((), (), s32[]{:S(2)}) async-start(), calls=%async_computation.1 | async-start | bytes 4456448 | tf_op jit(solution)/shard_map/all_gather | solution.py:30
  38.1 11.8 %copy-start.3 = (bf16[128,1024]{1,0:T(8,128)(2,1)}, bf16[128,1024]{1,0:T(8,128)(2,1)S(1)}, u32[]{:S(2)}) copy-start(bf16[128,1024]{1,0:T(8,128)(2,1)S(1)} %fusion.168) | copy-start | bytes 786436
  42.9 1.3 copy-start.12
  49.9 163.3 %all-gather.23.cloned.1.call-start = ((), (), s32[]{:S(2)}) async-start(), calls=%async_computation.7 | async-start | bytes 4456448 | tf_op jit(solution)/shard_map/all_gather | solution.py:30
  50.5 359.4 %all-gather.21.cloned.1.call-start = ((), (), s32[]{:S(2)}) async-start(), calls=%async_computation.6 | async-start | bytes 4456448 | tf_op jit(solution)/shard_map/all_gather | solution.py:30
  51.1 384.5 %all-gather.13.cloned.1.call-start = ((), (), s32[]{:S(2)}) async-start(), calls=%async_computation.2 | async-start | bytes 2228224 | tf_op jit(solution)/shard_map/all_gather | solution.py:30
  147.2 7.5 %copy-start.16 = (bf16[1024,1024]{1,0:T(8,128)(2,1)S(1)}, bf16[1024,1024]{1,0:T(8,128)(2,1)}, u32[]{:S(2)}) copy-start(bf16[1024,1024]{1,0:T(8,128)(2,1)} %convolution_convert_fusion.3) | copy-start | bytes 6291460
  170.7 6.4 copy-start.14
  170.8 6.4 copy-start.5
  170.8 10.8 %copy-start.11 = (f32[64,4096]{1,0:T(8,128)S(1)}, f32[64,4096]{1,0:T(8,128)}, u32[]{:S(2)}) copy-start(f32[64,4096]{1,0:T(8,128)} %copy-done.10) | copy-start | bytes 3145732
  213.2 25.5 %copy-start.13 = (bf16[2048,1024]{1,0:T(8,128)(2,1)S(1)}, bf16[2048,1024]{1,0:T(8,128)(2,1)}, u32[]{:S(2)}) copy-start(bf16[2048,1024]{1,0:T(8,128)(2,1)} %convolution_convert_fusion) | copy-start | bytes 12582916
  306.0 257.4 %all-gather.19.cloned.1.call-start = ((), (), s32[]{:S(2)}) async-start(), calls=%async_computation.5 | async-start | bytes 4456448 | tf_op jit(solution)/shard_map/all_gather | solution.py:30
  338.8 10.2 %copy-start.8 = (bf16[1024,1024]{1,0:T(8,128)(2,1)S(1)}, bf16[1024,1024]{1,0:T(8,128)(2,1)}, u32[]{:S(2)}) copy-start(bf16[1024,1024]{1,0:T(8,128)(2,1)} %all-gather.9.cloned.1.call-done) | copy-start | bytes 6291460
  338.8 10.2 %copy-start.15 = (bf16[1024,1024]{1,0:T(8,128)(2,1)S(1)}, bf16[1024,1024]{1,0:T(8,128)(2,1)}, u32[]{:S(2)}) copy-start(bf16[1024,1024]{1,0:T(8,128)(2,1)} %copy-done.14) | copy-start | bytes 6291460
  338.8 14.6 %copy-start.7 = (bf16[1024,1024]{1,0:T(8,128)(2,1)S(1)}, bf16[1024,1024]{1,0:T(8,128)(2,1)}, u32[]{:S(2)}) copy-start(bf16[1024,1024]{1,0:T(8,128)(2,1)} %all-gather.17.cloned.1.call-done) | copy-start | bytes 6291460
  409.9 25.6 %copy-start.6 = (bf16[1024,1024]{1,0:T(8,128)(2,1)S(1)}, bf16[1024,1024]{1,0:T(8,128)(2,1)}, u32[]{:S(2)}) copy-start(bf16[1024,1024]{1,0:T(8,128)(2,1)} %all-gather.15.cloned.1.call-done) | copy-start | bytes 6291460
  489.8 31.2 %copy-start.9 = (bf16[1024,1024]{1,0:T(8,128)(2,1)S(1)}, bf16[1024,1024]{1,0:T(8,128)(2,1)}, u32[]{:S(2)}) copy-start(bf16[1024,1024]{1,0:T(8,128)(2,1)} %all-gather.13.cloned.1.call-done) | copy-start | bytes 6291460
  563.4 44.6 %copy-start.4 = (bf16[2048,1024]{1,0:T(8,128)(2,1)S(1)}, bf16[2048,1024]{1,0:T(8,128)(2,1)}, u32[]{:S(2)}) copy-start(bf16[2048,1024]{1,0:T(8,128)(2,1)} %all-gather.21.cloned.1.call-done) | copy-start | bytes 12582916
  710.7 24.0 %copy-start.1 = (bf16[1024,1024]{1,0:T(8,128)(2,1)S(1)}, bf16[1024,1024]{1,0:T(8,128)(2,1)}, u32[]{:S(2)}) copy-start(bf16[1024,1024]{1,0:T(8,128)(2,1)} %param.17) | copy-start | bytes 6291460
Sparse Core Ops, SparseCore 0:
  17.2 31.0 all-gather.16
  50.6 28.2 all-gather.14
  81.2 28.2 all-gather.8
  112.2 35.0 all-gather.10
  149.9 35.0 all-gather.22
  187.1 35.0 all-gather.20
  306.1 28.2 all-gather.12
  338.9 35.0 all-gather.18

commit v2 on v1

v2 whole, which is shorter than its diff:
```python
import functools

import jax
import jax.numpy as jnp
from jax import lax
from jax.experimental import pallas as pl
from jax.experimental.pallas import tpu as pltpu
from jax.sharding import PartitionSpec as P

ROWS_CONTRACT = (((0,), (0,)), ((), ()))
LAST_CONTRACT = (((1,), (1,)), ((), ()))
F32 = jnp.float32
BF16 = jnp.bfloat16
GELU_C = 0.7978845608028654
GELU_D = 0.044715
MIB = 1024 * 1024


def dot(a, b):
    return jnp.dot(a, b, preferred_element_type=F32)


def dot_nt(a, b):
    return lax.dot_general(a, b, LAST_CONTRACT, preferred_element_type=F32)


def dot_tn(a, b):
    return lax.dot_general(a, b, ROWS_CONTRACT, preferred_element_type=F32)


def gelu_cdf(a):
    sq = a * a
    return sq, 0.5 + 0.5 * jnp.tanh(a * (GELU_C + (GELU_C * GELU_D) * sq))


def gelu_and_back(a, t):
    sq, cdf = gelu_cdf(a)
    u = a * cdf
    slope = cdf + u * (1.0 - cdf) * (2.0 * GELU_C + (6.0 * GELU_C * GELU_D) * sq)
    return u.astype(BF16), (slope * t).astype(BF16)


def gather_kernel(x_ref, out_ref, send_sem, recv_sem, pair_send, pair_recv, own_sem, own_pair):
    parts, rows = 3, x_ref.shape[0] // 3
    me = lax.axis_index('data')

    def flip(device, bit):
        return device + bit * (1 - 2 * (lax.div(device, bit) % 2))

    def walk(device, mask, axes):
        for i in range(3):
            if mask & (1 << i):
                device = flip(device, axes[i])
        return device

    partner = flip(me, 1)
    barrier = pltpu.get_barrier_semaphore()
    for bit in (1, 2, 4, 8):
        pl.semaphore_signal(barrier, inc=1, device_id=(flip(me, bit),), device_id_type=pl.DeviceIdType.MESH)
    pl.semaphore_wait(barrier, 4)

    started = []

    def piece(shard, p):
        return out_ref.at[shard, pl.ds(p * rows, rows)]

    def send(p, mask, step, axes):
        shard = walk(me, mask, axes)
        source = x_ref.at[pl.ds(p * rows, rows)] if mask == 0 else piece(shard, p)
        seen = mask | (1 << step)
        copy = pltpu.make_async_remote_copy(
            src_ref=source, dst_ref=piece(shard, p), send_sem=send_sem.at[p, seen], recv_sem=recv_sem.at[p, seen],
            device_id=(flip(me, axes[step]),), device_id_type=pl.DeviceIdType.MESH)
        copy.start()
        started.append(copy)

    def relay(p, mask, axes):
        shard = walk(me, mask, axes)
        copy = pltpu.make_async_remote_copy(
            src_ref=piece(shard, p), dst_ref=piece(shard, p), send_sem=pair_send.at[p, mask], recv_sem=pair_recv.at[p, mask],
            device_id=(partner,), device_id_type=pl.DeviceIdType.MESH)
        copy.start()
        pairs.append(copy)

    pairs = []
    orders = [(2, 4, 8), (4, 8, 2), (8, 2, 4)]
    for step in range(3):
        for p in range(parts):
            send(p, 0, step, orders[p])
    own = pltpu.make_async_copy(x_ref, out_ref.at[me], own_sem)
    own.start()
    pair_own = pltpu.make_async_remote_copy(
        src_ref=x_ref, dst_ref=out_ref.at[me], send_sem=own_pair.at[0], recv_sem=own_pair.at[1],
        device_id=(partner,), device_id_type=pl.DeviceIdType.MESH)
    pair_own.start()

    def arrived(p, mask):
        pltpu.make_async_remote_copy(
            src_ref=piece(me, p), dst_ref=piece(walk(me, mask, orders[p]), p), send_sem=send_sem.at[p, mask],
            recv_sem=recv_sem.at[p, mask], device_id=(partner,), device_id_type=pl.DeviceIdType.MESH).wait_recv()

    for mask in (1, 2, 3, 4, 5, 6, 7):
        first = 1 if mask == 1 else 2 if mask < 4 else 3
        for p in range(parts):
            arrived(p, mask)
            for step in range(first, 3):
                send(p, mask, step, orders[p])
            relay(p, mask, orders[p])
    for copy in started:
        copy.wait_send()
    for copy in pairs:
        copy.wait()
    own.wait()
    pair_own.wait()


def gather_rows(x):
    return pl.pallas_call(
        gather_kernel,
        out_shape=jax.ShapeDtypeStruct((16, *x.shape), x.dtype),
        in_specs=[pl.BlockSpec(memory_space=pltpu.VMEM)],
        out_specs=pl.BlockSpec(memory_space=pl.ANY),
        scratch_shapes=[pltpu.SemaphoreType.DMA((3, 8))] * 4 + [pltpu.SemaphoreType.DMA, pltpu.SemaphoreType.DMA((2,))],
        compiler_params=pltpu.CompilerParams(collective_id=0, has_side_effects=True),
        name='gather_rows',
    )(x)


def layer_kernel(row_tile, h_ref, e_ref, w1_ref, w2_ref, *rest):
    one_ref, two_ref, u_ref, delta_ref = rest[-4:]
    n, r, width = h_ref.shape
    h = h_ref.reshape(n * r, width)
    e = e_ref.reshape(n * r, width)
    w1_t = w1_ref[0].T
    for i in range(n * r // row_tile):
        rows = pl.ds(i * row_tile, row_tile)
        pre = dot_nt(w1_t, h[rows, :])
        t = dot_nt(w2_ref[0], e[rows, :])
        u_ref[:, rows], delta_ref[:, rows] = gelu_and_back(pre, t)
    for c in range(4):
        cols = pl.ds(c * (width // 4), width // 4)
        two_ref[0, :, cols] = dot(u_ref[...], e[:, cols])
        one_ref[0, cols, :] = dot(delta_ref[...], h[:, cols]).T


def layer_grads(layer, h_all, h_place, e_all, e_place, rows, w1, w2, grads=None):
    _, width, ffn_width = w1.shape
    n = h_all.shape[0]
    block = 512
    row_tile = 512
    total = n * rows
    in_specs = [
        pl.BlockSpec((n, rows, width), lambda j: (0, h_place, 0)),
        pl.BlockSpec((n, rows, width), lambda j: (0, e_place, 0)),
        pl.BlockSpec((1, width, block), lambda j: (layer, 0, j)),
        pl.BlockSpec((1, block, width), lambda j: (layer, j, 0)),
    ]
    args = [h_all, e_all, w1, w2]
    aliases = {}
    if grads is not None:
        in_specs += [pl.BlockSpec(memory_space=pl.ANY)] * 2
        args += list(grads)
        aliases = {4: 0, 5: 1}
    return pl.pallas_call(
        functools.partial(layer_kernel, row_tile),
        grid=(ffn_width // block,),
        in_specs=in_specs,
        out_specs=[
            pl.BlockSpec((1, width, block), lambda j: (layer, 0, j)),
            pl.BlockSpec((1, block, width), lambda j: (layer, j, 0)),
        ],
        out_shape=[jax.ShapeDtypeStruct(w1.shape, F32), jax.ShapeDtypeStruct(w2.shape, F32)],
        scratch_shapes=[pltpu.VMEM((block, total), BF16)] * 2,
        input_output_aliases=aliases,
        compiler_params=pltpu.CompilerParams(vmem_limit_bytes=56 * MIB, dimension_semantics=('arbitrary',)),
        cost_estimate=pl.CostEstimate(flops=8 * total * width * ffn_width, bytes_accessed=60 * MIB, transcendentals=0),
        name='layer_grads',
    )(*args)


def ffn(h, w1, w2):
    pre = dot(h, w1)
    u = (pre * gelu_cdf(pre)[1]).astype(BF16)
    return (h.astype(F32) + dot(u, w2)).astype(BF16)


def gather(x):
    return lax.all_gather(x, 'data', axis=0)


def local_step(q_loc, d_loc, temperature, q_w1, q_w2, q_proj, d_w1, d_w2, d_proj):
    rows, width = q_loc.shape
    me = lax.axis_index('data')
    d_h = [d_loc.reshape(2 * rows, width)]
    q_h = [q_loc]
    for k in range(2):
        d_h.append(ffn(d_h[k], d_w1[k], d_w2[k]))
        q_h.append(ffn(q_h[k], q_w1[k], q_w2[k]))
    h0_all = gather(jnp.concatenate([d_h[0], q_h[0]], axis=0))
    h1_all = gather(jnp.concatenate([d_h[1], q_h[1]], axis=0))
    h2_all = gather_rows(jnp.concatenate([d_h[2], q_h[2]], axis=0))
    d_last = h2_all[:, :2 * rows].reshape(-1, width)
    q_last = h2_all[:, 2 * rows:].reshape(-1, width)
    docs = dot(d_last, d_proj).astype(BF16)
    queries = dot(q_last, q_proj).astype(BF16)
    batch = queries.shape[0]
    logits = dot_nt(queries, docs) / temperature
    row = jnp.arange(batch)
    target = jnp.arange(2 * batch)[None, :] == ((row // rows) * 2 * rows + row % rows)[:, None]
    log_norm = jax.nn.logsumexp(logits, axis=1)
    pos = jnp.sum(jnp.where(target, logits, 0.0), axis=1)
    loss = jnp.sum(log_norm - pos) / batch
    prob = jnp.exp(logits - log_norm[:, None])
    grad = ((prob - target.astype(F32)) / (batch * temperature)).astype(BF16)
    q_up = dot(grad, docs).astype(BF16)
    d_up = dot_tn(grad, queries).astype(BF16)

    def chain(h1_own, up, w1, w2, proj):
        own = h1_own.shape[0]
        e1_bf = dot_nt(up, proj).astype(BF16)
        e1_own = dot_nt(lax.dynamic_slice_in_dim(up, me * own, own, 0), proj)
        delta = gelu_and_back(dot(h1_own, w1[1]), dot_nt(e1_own.astype(BF16), w2[1]))[1]
        return e1_bf.reshape(16, own, width), (e1_own + dot_nt(delta, w1[1])).astype(BF16)

    d_e1, d_e0 = chain(d_h[1], d_up, d_w1, d_w2, d_proj)
    q_e1, q_e0 = chain(q_h[1], q_up, q_w1, q_w2, q_proj)
    e0_all = gather(jnp.concatenate([d_e0, q_e0], axis=0))
    d_p = dot_tn(d_last, d_up)
    q_p = dot_tn(q_last, q_up)
    d_g = layer_grads(1, h1_all, 0, d_e1, 0, 2 * rows, d_w1, d_w2)
    q_g = layer_grads(1, h1_all, 2, q_e1, 0, rows, q_w1, q_w2)
    d_g = layer_grads(0, h0_all, 0, e0_all, 0, 2 * rows, d_w1, d_w2, d_g)
    q_g = layer_grads(0, h0_all, 2, e0_all, 2, rows, q_w1, q_w2, q_g)
    return (loss, *q_g, q_p, *d_g, d_p)


def solution(mesh):
    specs_in = (P('data', None), P(None, 'data', None), P(), P(), P(), P(), P(), P(), P())
    specs_out = (P(), P(), P(), P(), P(), P(), P())
    return jax.shard_map(local_step, mesh=mesh, in_specs=specs_in, out_specs=specs_out, check_vma=False)
```

time: 752 us -> 429 us (0.57)
  matrix products: 505 us -> 105 us
  Pallas kernels: 0 us -> 281 us
  other arithmetic: 96.4 us -> 9.73 us
  waiting for transfers between devices: 59.1 us -> 0.07 us
  local copies, waits for them, and re-layouts: 64.6 us -> 12.3 us
    pallas_call x0 -> x5, Pallas kernels: none -> 281 us  [the longest x4 241 us: layer_grads(): pl.pallas_call(functools.partial(layer_kernel, row_tile), grid=(ffn_width...]
    dot_general x11 -> x3, matrix products: 232 us -> 18.2 us  [dot_tn(): return lax.dot_general(a, b, ROWS_CONTRACT, preferred_element_type=F32)]
    dot_general x7, matrix products: 132 us -> 37.7 us  [dot_nt(): return lax.dot_general(a, b, LAST_CONTRACT, preferred_element_type=F32)]
    dot_general x13 -> x9, matrix products: 141 us -> 48.7 us  [dot(): return jnp.dot(a, b, preferred_element_type=F32)]
    another operation x4 -> x0, other arithmetic: 89.8 us -> none  [tower(): return (jnp.stack([one0, one1]), jnp.stack([two0, two1]), g_proj)]
    unnamed x36, local copies, waits for them, and re-layouts: 64.6 us -> 4.38 us
    all_gather x8 -> x3, waiting for transfers between devices: 57.3 us -> 0.02 us  [gather(): return lax.all_gather(x, 'data', axis=0)]
    slice x0 -> x2, local copies, waits for them, and re-layouts: none -> 7.96 us  [the longest x1 4.81 us: local_step(): d_last = h2_all[:, :2 * rows].reshape(-1, width)]
  transfers between devices with their start and end apart: 8 -> 3, of which waited for: 3 -> 0; matrix products, arithmetic and copies ran while one was open for 65% -> 24% of each run, Pallas kernels for 0% -> 38%
where the time goes in v2:
time: 429 us; the launch traced here: 424 us
  Pallas kernels  281 us (66%)
  matrix products  105 us (24%)
  between operations  16.8 us (4%)
  local copies, waits for them, and re-layouts  12.3 us (3%)
  other arithmetic  9.73 us (2%)
    pallas_call x4, Pallas kernels, layer_grads(): pl.pallas_call(functools.partial(layer_kernel, row_tile), grid=(ffn_width...  241 us
    dot_general x9, matrix products, dot(): return jnp.dot(a, b, preferred_element_type=F32)  48.7 us
    pallas_call x1, Pallas kernels, gather_rows(): pl.pallas_call(gather_kernel, out_shape=jax.ShapeDtypeStruct((16, *x.shap...  39.7 us
    dot_general x7, matrix products, dot_nt(): return lax.dot_general(a, b, LAST_CONTRACT, preferred_element_type=F32)  37.7 us
    dot_general x3, matrix products, dot_tn(): return lax.dot_general(a, b, ROWS_CONTRACT, preferred_element_type=F32)  18.2 us
  transfers between devices with their start and end apart: 3, of which 0 were waited for; matrix products, arithmetic and copies ran while one was open for 24% of the time, Pallas kernels for 38%

profile of v2, /device:TPU:0, one launch (start us, length us, event | category | flops | bytes accessed | tf_op | source)
XLA Modules:
  0.0 424.4 jit_solution(4787656577308412000)
XLA Ops:
  7.2 0.0 copy-start
  7.2 0.0 all-gather.11.cloned.1.call-start
  7.2 9.1 %fusion.85 = bf16[64,1024]{1,0:T(8,128)(2,1)S(1)} fusion(bf16[2,4096,1024]{2,1,0:T(8,128)(2,1)} %w2_ref.5, bf16[64,1024]{1,0:T(8,128)(2,1)} %param.9, bf16[2,1024,4096]{2,1,0:T(8,128)(2,1)} %w1_ref.5), kind=kOutput, calls=%fused_computation.66 | convolution fusion | flops 1076035584 | bytes 17170432 | tf_op jit(solution)/shard_map/dot_general | solution.py:20
  16.4 0.0 copy-start.7
  16.4 8.7 %fusion.67 = bf16[128,1024]{1,0:T(8,128)(2,1)S(1)} fusion(bf16[2,4096,1024]{2,1,0:T(8,128)(2,1)} %w2_ref.7, bf16[128,1024]{1,0:T(8,128)(2,1)S(1)} %bitcast.112, bf16[2,1024,4096]{2,1,0:T(8,128)(2,1)} %w1_ref.7), kind=kOutput, calls=%fused_computation.60 | convolution fusion | flops 2152071168 | bytes 17563648 | tf_op jit(solution)/shard_map/dot_general | solution.py:20
  25.1 0.8 pad_maximum_fusion.3
  25.9 0.0 all-gather.11.cloned.1.call-update
  25.9 0.0 all-gather.7.cloned.1.call-start
  26.0 0.8 pad_maximum_fusion.1
  26.8 0.0 all-gather.7.cloned.1.call-update
  26.8 0.2 all-gather.9.cloned.1.call-start
  27.0 0.0 slice-start
  27.0 5.1 %fusion.6 = f32[64,4096]{1,0:T(8,128)S(1)} fusion(bf16[64,1024]{1,0:T(8,128)(2,1)S(1)} %fusion.85, bf16[2,1024,4096]{2,1,0:T(8,128)(2,1)} %w1_ref.5), kind=kOutput, calls=%fused_computation.6 | convolution fusion | flops 536870912 | bytes 9568256 | tf_op jit(solution)/shard_map/dot_general | solution.py:20
  32.1 0.0 copy-start.12
  32.1 1.0 copy-done.12
  33.1 5.0 %fusion.79 = bf16[64,1024]{1,0:T(8,128)(2,1)S(1)} fusion(bf16[2,4096,1024]{2,1,0:T(8,128)(2,1)} %w2_ref.5, f32[64,4096]{1,0:T(8,128)S(1)} %fusion.6, bf16[64,1024]{1,0:T(8,128)(2,1)S(1)} %fusion.85), kind=kOutput, calls=%fused_computation.64 | convolution fusion | flops 539164672 | bytes 9699328 | tf_op jit(solution)/shard_map/dot_general | solution.py:20
  38.2 0.0 slice-start.3
  38.2 4.8 %fusion.18 = f32[128,4096]{1,0:T(8,128)S(1)} fusion(bf16[128,1024]{1,0:T(8,128)(2,1)S(1)} %fusion.67, bf16[2,1024,4096]{2,1,0:T(8,128)(2,1)} %w1_ref.7), kind=kOutput, calls=%fused_computation.18 | convolution fusion | flops 1073741824 | bytes 10747904 | tf_op jit(solution)/shard_map/dot_general | solution.py:20
  43.0 1.6 fusion.61
  44.6 0.8 pad_maximum_fusion.x_ref
  45.4 39.7 %gather_rows.1 = bf16[16,192,1024]{2,1,0:T(8,128)(2,1)} custom-call(bf16[192,1024]{1,0:T(8,128)(2,1)} %pad_maximum_fusion.x_ref), custom_call_target="tpu_custom_call" | custom-call | tf_op jit(solution)/shard_map/gather_rows/pallas_call | solution.py:118
  85.1 3.1 slice.44
  88.3 4.8 %slice.45 = bf16[16,128,1024]{2,1,0:T(8,128)(2,1)} slice(bf16[16,192,1024]{2,1,0:T(8,128)(2,1)} %gather_rows.1), slice={[0:16], [0:128], [0:1024]} | slice | bytes 8388608 | tf_op jit(solution)/shard_map/slice | solution.py:202
  93.8 4.7 %convolution_convert_fusion.5 = bf16[1024,1024]{1,0:T(8,128)(2,1)S(1)} fusion(bf16[1024,1024]{1,0:T(8,128)(2,1)} %bitcast.110, bf16[1024,1024]{1,0:T(8,128)(2,1)} %param.14), kind=kOutput, calls=%fused_computation.54 | convolution fusion | flops 2148532224 | bytes 6291456 | tf_op jit(solution)/shard_map/dot_general | solution.py:20
  98.5 4.9 %convolution_convert_fusion.2 = bf16[2048,1024]{1,0:T(8,128)(2,1)S(1)} fusion(bf16[2048,1024]{1,0:T(8,128)(2,1)S(1)} %bitcast.108, bf16[1024,1024]{1,0:T(8,128)(2,1)S(1)} %copy-done), kind=kOutput, calls=%fused_computation.47 | convolution fusion | flops 4297064448 | bytes 10485760 | tf_op jit(solution)/shard_map/dot_general | solution.py:20
  103.5 4.6 %fusion.160 = (f32[1024]{0:T(1024)S(1)}, f32[1024,2048]{1,0:T(8,128)S(1)}) fusion(f32[]{:T(128)S(6)} %copy.24, bf16[1024,1024]{1,0:T(8,128)(2,1)S(1)} %convolution_convert_fusion.5, bf16[2048,1024]{1,0:T(8,128)(2,1)S(1)} %convolution_convert_fusion.2), kind=kOutput, calls=%fused_computation.138 | convolution fusion | flops 4299160576 | bytes 14684164 | tf_op jit(solution)/shard_map/dot_general | solution.py:24
  108.1 3.2 select_reduce_fusion
  111.3 0.6 subtract_reduce_fusion
  111.9 2.8 divide_convert_fusion
  114.7 4.7 %convolution_convert_fusion.4 = bf16[1024,1024]{1,0:T(8,128)(2,1)S(1)} fusion(bf16[1024,2048]{1,0:T(8,128)(2,1)S(1)} %divide_convert_fusion, bf16[2048,1024]{1,0:T(8,128)(2,1)S(1)} %convolution_convert_fusion.2), kind=kOutput, calls=%fused_computation.53 | convolution fusion | flops 4296015872 | bytes 10485760 | tf_op jit(solution)/shard_map/dot_general | solution.py:20
  119.5 1.3 copy-done.10
  120.8 0.8 fusion.123
  121.6 5.3 %convolution_convert_fusion.1 = bf16[2048,1024]{1,0:T(8,128)(2,1)S(1)} fusion(bf16[1024,2048]{1,0:T(8,128)(2,1)S(1)} %divide_convert_fusion, bf16[1024,1024]{1,0:T(8,128)(2,1)S(1)} %convolution_convert_fusion.5), kind=kOutput, calls=%fused_computation.46 | convolution fusion | flops 4297064448 | bytes 10485760 | tf_op jit(solution)/shard_map/dot_general | solution.py:28
  126.9 2.0 copy-done.8
  128.9 0.8 fusion.119
  129.7 9.1 %fusion.82 = bf16[64,1024]{1,0:T(8,128)(2,1)S(1)} fusion(f32[64,1024]{1,0:T(8,128)S(1)} %fusion.123, bf16[2,1024,4096]{2,1,0:T(8,128)(2,1)} %w1_ref.5, bf16[2,4096,1024]{2,1,0:T(8,128)(2,1)} %w2_ref.5, f32[64,4096]{1,0:T(8,128)} %copy-done.12), kind=kOutput, calls=%fused_computation.65 | convolution fusion | flops 1077870592 | bytes 18481152 | tf_op jit(solution)/shard_map/dot_general | solution.py:24
  138.8 9.9 %fusion.64 = bf16[128,1024]{1,0:T(8,128)(2,1)S(1)} fusion(f32[128,1024]{1,0:T(8,128)S(1)} %fusion.119, bf16[2,1024,4096]{2,1,0:T(8,128)(2,1)} %w1_ref.7, bf16[2,4096,1024]{2,1,0:T(8,128)(2,1)} %w2_ref.7, f32[128,4096]{1,0:T(8,128)} %copy-done.13), kind=kOutput, calls=%fused_computation.59 | convolution fusion | flops 2155741184 | bytes 20185088 | tf_op jit(solution)/shard_map/dot_general | solution.py:24
  148.8 0.8 pad_maximum_fusion.2
  149.5 0.0 all-gather.9.cloned.1.call-update
  149.6 6.8 %fusion.161 = f32[1024,1024]{1,0:T(8,128)} fusion(bf16[1024,1024]{1,0:T(8,128)(2,1)} %bitcast.111, bf16[1024,1024]{1,0:T(8,128)(2,1)} %copy-done.10), kind=kOutput, calls=%fused_computation.139 | convolution fusion | flops 2147483648 | bytes 8388608 | tf_op jit(solution)/shard_map/dot_general | solution.py:28
  156.4 3.7 convolution_convert_fusion.3
  160.7 8.7 %convolution_convert_fusion = bf16[2048,1024]{1,0:T(8,128)(2,1)} fusion(bf16[2048,1024]{1,0:T(8,128)(2,1)} %copy-done.8, bf16[1024,1024]{1,0:T(8,128)(2,1)S(1)} %copy-done), kind=kOutput, calls=%fused_computation.45 | convolution fusion | flops 4297064448 | bytes 10485760 | tf_op jit(solution)/shard_map/dot_general | solution.py:24
  169.4 6.1 %fusion.162 = f32[1024,1024]{1,0:T(8,128)} fusion(bf16[2048,1024]{1,0:T(8,128)(2,1)S(1)} %bitcast.109, bf16[2048,1024]{1,0:T(8,128)(2,1)S(1)} %copy-done.9), kind=kOutput, calls=%fused_computation.140 | convolution fusion | flops 4294967296 | bytes 12582912 | tf_op jit(solution)/shard_map/dot_general | solution.py:28
  175.5 42.1 %layer_grads.4 = (f32[2,1024,4096]{2,1,0:T(8,128)}, f32[2,4096,1024]{2,1,0:T(8,128)}) custom-call(bf16[16,192,1024]{2,1,0:T(8,128)(2,1)} %bitcast.118, bf16[16,64,1024]{2,1,0:T(8,128)(2,1)} %bitcast.123, bf16[2,1024,4096]{2,1,0:T(8,128)(2,1)} %w1_ref.5, bf16[2,4096,1024]{2,1,0:T(8,128)(2,1)} %w2_ref.5), custom_call_target="tpu_custom_call" | custom-call | flops 34359738368 | bytes 62914560 | tf_op jit(solution)/shard_map/layer_grads/pallas_call | solution.py:164
  217.7 78.2 %layer_grads.6 = (f32[2,1024,4096]{2,1,0:T(8,128)}, f32[2,4096,1024]{2,1,0:T(8,128)}) custom-call(bf16[16,192,1024]{2,1,0:T(8,128)(2,1)} %bitcast.119, bf16[16,128,1024]{2,1,0:T(8,128)(2,1)} %bitcast.122, bf16[2,1024,4096]{2,1,0:T(8,128)(2,1)} %w1_ref.7, bf16[2,4096,1024]{2,1,0:T(8,128)(2,1)} %w2_ref.7), custom_call_target="tpu_custom_call" | custom-call | flops 68719476736 | bytes 62914560 | tf_op jit(solution)/shard_map/layer_grads/pallas_call | solution.py:164
  295.9 0.0 all-gather.9.cloned.1.call-done
  295.9 78.3 %layer_grads.7 = (f32[2,1024,4096]{2,1,0:T(8,128)}, f32[2,4096,1024]{2,1,0:T(8,128)}) custom-call(bf16[16,192,1024]{2,1,0:T(8,128)(2,1)} %bitcast.116, bf16[16,192,1024]{2,1,0:T(8,128)(2,1)} %bitcast.120, bf16[2,1024,4096]{2,1,0:T(8,128)(2,1)} %w1_ref.7, bf16[2,4096,1024]{2,1,0:T(8,128)(2,1)} %w2_ref.7, ...), custom_call_target="tpu_custom_call", output_to_operand_aliasing={{0}: (4, {}), {1}: (5, {})} | custom-call | flops 68719476736 | bytes 62914560 | tf_op jit(solution)/shard_map/layer_grads/pallas_call | solution.py:164
  374.2 42.3 %layer_grads.5 = (f32[2,1024,4096]{2,1,0:T(8,128)}, f32[2,4096,1024]{2,1,0:T(8,128)}) custom-call(bf16[16,192,1024]{2,1,0:T(8,128)(2,1)} %bitcast.117, bf16[16,192,1024]{2,1,0:T(8,128)(2,1)} %bitcast.121, bf16[2,1024,4096]{2,1,0:T(8,128)(2,1)} %w1_ref.5, bf16[2,4096,1024]{2,1,0:T(8,128)(2,1)} %w2_ref.5, ...), custom_call_target="tpu_custom_call", output_to_operand_aliasing={{0}: (4, {}), {1}: (5, {})} | custom-call | flops 34359738368 | bytes 62914560 | tf_op jit(solution)/shard_map/layer_grads/pallas_call | solution.py:164
  (33 shorter events, 0.1 us)
Async XLA Ops:
  7.2 91.3 %copy-start = (bf16[1024,1024]{1,0:T(8,128)(2,1)S(1)}, bf16[1024,1024]{1,0:T(8,128)(2,1)}, u32[]{:S(2)}) copy-start(bf16[1024,1024]{1,0:T(8,128)(2,1)} %param.17) | copy-start | bytes 6291460
  7.2 9.2 %copy-start.6 = (bf16[2,64,1024]{2,1,0:T(8,128)(2,1)S(1)}, bf16[2,64,1024]{2,1,0:T(8,128)(2,1)}, u32[]{:S(2)}) copy-start(bf16[2,64,1024]{2,1,0:T(8,128)(2,1)} %param.10) | copy-start | bytes 786436
  7.2 168.3 %all-gather.11.cloned.1.call-start = ((), (), s32[]{:S(2)}) async-start(), calls=%async_computation.2 | async-start | bytes 6684672 | tf_op jit(solution)/shard_map/all_gather | solution.py:188
  16.4 9.6 %copy-start.7 = (bf16[64,1024]{1,0:T(8,128)(2,1)S(1)}, bf16[64,1024]{1,0:T(8,128)(2,1)}, u32[]{:S(2)}) copy-start(bf16[64,1024]{1,0:T(8,128)(2,1)} %param.9) | copy-start | bytes 393220
  25.9 270.0 %all-gather.7.cloned.1.call-start = ((), (), s32[]{:S(2)}) async-start(), calls=%async_computation | async-start | bytes 6684672 | tf_op jit(solution)/shard_map/all_gather | solution.py:188
  26.8 269.1 %all-gather.9.cloned.1.call-start = ((), (), s32[]{:S(2)}) async-start(), calls=%async_computation.1 | async-start | bytes 6684672 | tf_op jit(solution)/shard_map/all_gather | solution.py:188
  27.0 16.0 %slice-start = ((s8[16777216]{0:T(1024)(128)(4,1)}), s8[4194304]{0:T(1024)(128)(4,1)S(1)}, s32[]{:S(2)}) async-start(s8[16777216]{0:T(1024)(128)(4,1)} %bitcast.114), calls=%async_computation.3 | async-start | bytes 8388608
  27.0 16.0 %slice-start.1 = ((s8[16777216]{0:T(1024)(128)(4,1)}), s8[4194304]{0:T(1024)(128)(4,1)S(1)}, s32[]{:S(2)}) async-start(s8[16777216]{0:T(1024)(128)(4,1)} %bitcast.114), calls=%async_computation.4 | async-start | bytes 8388608
  32.1 1.0 copy-start.12
  33.1 9.9 %slice-start.2 = ((s8[16777216]{0:T(1024)(128)(4,1)}), s8[4194304]{0:T(1024)(128)(4,1)S(1)}, s32[]{:S(2)}) async-start(s8[16777216]{0:T(1024)(128)(4,1)} %bitcast.114), calls=%async_computation.5 | async-start | bytes 8388608
  38.2 4.9 %slice-start.3 = ((s8[16777216]{0:T(1024)(128)(4,1)}), s8[4194304]{0:T(1024)(128)(4,1)S(1)}, s32[]{:S(2)}) async-start(s8[16777216]{0:T(1024)(128)(4,1)} %bitcast.114), calls=%async_computation.6 | async-start | bytes 8388608
  43.0 1.6 copy-start.13
  93.8 4.7 %copy-start.2 = (bf16[16,128,1024]{2,1,0:T(8,128)(2,1)S(1)}, bf16[16,128,1024]{2,1,0:T(8,128)(2,1)}, u32[]{:S(2)}) copy-start(bf16[16,128,1024]{2,1,0:T(8,128)(2,1)} %slice.45) | copy-start | bytes 12582916
  114.7 6.1 %copy-start.4 = (bf16[1024,1024]{1,0:T(8,128)(2,1)S(1)}, bf16[1024,1024]{1,0:T(8,128)(2,1)}, u32[]{:S(2)}) copy-start(bf16[1024,1024]{1,0:T(8,128)(2,1)} %param.14) | copy-start | bytes 6291460
  119.5 1.3 copy-start.10
  126.9 2.0 copy-start.8
  149.5 6.8 %copy-start.5 = (bf16[1024,1024]{1,0:T(8,128)(2,1)S(1)}, bf16[1024,1024]{1,0:T(8,128)(2,1)}, u32[]{:S(2)}) copy-start(bf16[1024,1024]{1,0:T(8,128)(2,1)} %param.14) | copy-start | bytes 6291460
  149.6 6.8 %copy-start.11 = (bf16[1024,1024]{1,0:T(8,128)(2,1)S(1)}, bf16[1024,1024]{1,0:T(8,128)(2,1)}, u32[]{:S(2)}) copy-start(bf16[1024,1024]{1,0:T(8,128)(2,1)} %copy-done.10) | copy-start | bytes 6291460
  160.7 8.7 %copy-start.3 = (bf16[16,128,1024]{2,1,0:T(8,128)(2,1)S(1)}, bf16[16,128,1024]{2,1,0:T(8,128)(2,1)}, u32[]{:S(2)}) copy-start(bf16[16,128,1024]{2,1,0:T(8,128)(2,1)} %slice.45) | copy-start | bytes 12582916
  160.7 8.7 %copy-start.9 = (bf16[2048,1024]{1,0:T(8,128)(2,1)S(1)}, bf16[2048,1024]{1,0:T(8,128)(2,1)}, u32[]{:S(2)}) copy-start(bf16[2048,1024]{1,0:T(8,128)(2,1)} %copy-done.8) | copy-start | bytes 12582916
  374.2 42.3 %copy-start.1 = (bf16[1024,1024]{1,0:T(8,128)(2,1)S(1)}, bf16[1024,1024]{1,0:T(8,128)(2,1)}, u32[]{:S(2)}) copy-start(bf16[1024,1024]{1,0:T(8,128)(2,1)} %param.17) | copy-start | bytes 6291460
Sparse Core Ops, SparseCore 0:
  26.0 57.3 all-gather.10
  85.6 41.8 all-gather.6
  149.7 41.7 all-gather.8

commit v3 on v2

--- a/solution.py
+++ b/solution.py
@@ -40,7 +40,7 @@
     return u.astype(BF16), (slope * t).astype(BF16)
 
 
-def gather_kernel(x_ref, out_ref, send_sem, recv_sem, pair_send, pair_recv, own_sem, own_pair):
+def gather_kernel(x_ref, d_ref, q_ref, send_sem, recv_sem, pair_send, pair_recv, own_sem, own_send, own_recv):
     parts, rows = 3, x_ref.shape[0] // 3
     me = lax.axis_index('data')
 
@@ -62,7 +62,7 @@
     started = []
 
     def piece(shard, p):
-        return out_ref.at[shard, pl.ds(p * rows, rows)]
+        return q_ref.at[shard] if p == 2 else d_ref.at[shard, pl.ds(p * rows, rows)]
 
     def send(p, mask, step, axes):
         shard = walk(me, mask, axes)
@@ -87,12 +87,17 @@
     for step in range(3):
         for p in range(parts):
             send(p, 0, step, orders[p])
-    own = pltpu.make_async_copy(x_ref, out_ref.at[me], own_sem)
-    own.start()
-    pair_own = pltpu.make_async_remote_copy(
-        src_ref=x_ref, dst_ref=out_ref.at[me], send_sem=own_pair.at[0], recv_sem=own_pair.at[1],
-        device_id=(partner,), device_id_type=pl.DeviceIdType.MESH)
-    pair_own.start()
+    owns = []
+    for p in range(parts):
+        source = x_ref.at[pl.ds(p * rows, rows)]
+        own = pltpu.make_async_copy(source, piece(me, p), own_sem.at[p])
+        own.start()
+        owns.append(own)
+        copy = pltpu.make_async_remote_copy(
+            src_ref=source, dst_ref=piece(me, p), send_sem=own_send.at[p], recv_sem=own_recv.at[p],
+            device_id=(partner,), device_id_type=pl.DeviceIdType.MESH)
+        copy.start()
+        pairs.append(copy)
 
     def arrived(p, mask):
         pltpu.make_async_remote_copy(
@@ -110,24 +115,32 @@
         copy.wait_send()
     for copy in pairs:
         copy.wait()
-    own.wait()
-    pair_own.wait()
+    for copy in owns:
+        copy.wait()
 
 
 def gather_rows(x):
+    rows = x.shape[0] // 3
     return pl.pallas_call(
         gather_kernel,
-        out_shape=jax.ShapeDtypeStruct((16, *x.shape), x.dtype),
+        out_shape=[jax.ShapeDtypeStruct((16, 2 * rows, x.shape[1]), x.dtype), jax.ShapeDtypeStruct((16, rows, x.shape[1]), x.dtype)],
         in_specs=[pl.BlockSpec(memory_space=pltpu.VMEM)],
-        out_specs=pl.BlockSpec(memory_space=pl.ANY),
-        scratch_shapes=[pltpu.SemaphoreType.DMA((3, 8))] * 4 + [pltpu.SemaphoreType.DMA, pltpu.SemaphoreType.DMA((2,))],
+        out_specs=[pl.BlockSpec(memory_space=pl.ANY)] * 2,
+        scratch_shapes=[pltpu.SemaphoreType.DMA((3, 8))] * 4 + [pltpu.SemaphoreType.DMA((3,))] * 3,
         compiler_params=pltpu.CompilerParams(collective_id=0, has_side_effects=True),
         name='gather_rows',
     )(x)
 
 
-def layer_kernel(row_tile, h_ref, e_ref, w1_ref, w2_ref, *rest):
-    one_ref, two_ref, u_ref, delta_ref = rest[-4:]
+def layer_kernel(row_tile, in_place, incoming, send, core_ref, h_ref, e_ref, w1_ref, w2_ref, *rest):
+    u_ref, delta_ref = rest[-2:]
+    rest = rest[2 if in_place else 0:-2]
+    if incoming:
+        y_refs, rest = rest[:2], rest[4:]
+        for y_ref, t_ref in zip(y_refs, rest[-2:]):
+            t_ref[...] = y_ref[...]
+        rest = rest[:-2]
+    one_ref, two_ref = rest[:2]
     n, r, width = h_ref.shape
     h = h_ref.reshape(n * r, width)
     e = e_ref.reshape(n * r, width)
@@ -139,43 +152,71 @@
         u_ref[:, rows], delta_ref[:, rows] = gelu_and_back(pre, t)
     for c in range(4):
         cols = pl.ds(c * (width // 4), width // 4)
-        two_ref[0, :, cols] = dot(u_ref[...], e[:, cols])
-        one_ref[0, cols, :] = dot(delta_ref[...], h[:, cols]).T
-
-
-def layer_grads(layer, h_all, h_place, e_all, e_place, rows, w1, w2, grads=None):
+        two = dot(u_ref[...], e[:, cols])
+        one = dot(delta_ref[...], h[:, cols]).T
+        two_ref[0, :, cols] = two
+        one_ref[0, cols, :] = one
+        if send:
+            rest[3][0, :, cols] = two
+            rest[2][0, cols, :] = one
+
+
+def layer_grads(core, layer, first, h_all, h_place, e_all, e_place, rows, w1, w2, grads=None, incoming=None):
     _, width, ffn_width = w1.shape
     n = h_all.shape[0]
-    block = 512
-    row_tile = 512
+    block, row_tile, steps = 512, 512, 4
     total = n * rows
+    send = first is None
+    resident = pl.Buffered(buffer_count=1)
+
+    def mine(j, c):
+        return c[0] * steps + j if send else first + j
+
+    def other(j, c):
+        return (1 - c[0]) * steps + j
+
+    def wide(at, place):
+        return pl.BlockSpec((1, width, block), lambda j, c: (at, 0, place(j, c)))
+
+    def tall(at, place):
+        return pl.BlockSpec((1, block, width), lambda j, c: (at, place(j, c), 0))
+
     in_specs = [
-        pl.BlockSpec((n, rows, width), lambda j: (0, h_place, 0)),
-        pl.BlockSpec((n, rows, width), lambda j: (0, e_place, 0)),
-        pl.BlockSpec((1, width, block), lambda j: (layer, 0, j)),
-        pl.BlockSpec((1, block, width), lambda j: (layer, j, 0)),
+        pl.BlockSpec((n, rows, width), lambda j, c: (0, h_place, 0), pipeline_mode=resident),
+        pl.BlockSpec((n, rows, width), lambda j, c: (0, e_place, 0), pipeline_mode=resident),
+        wide(layer, mine), tall(layer, mine),
     ]
-    args = [h_all, e_all, w1, w2]
+    args = [core, h_all, e_all, w1, w2]
+    out_specs = [wide(layer, mine), tall(layer, mine)]
+    out_shape = [jax.ShapeDtypeStruct(w1.shape, F32), jax.ShapeDtypeStruct(w2.shape, F32)]
     aliases = {}
+    anywhere = [pl.BlockSpec(memory_space=pl.ANY)] * 2
     if grads is not None:
-        in_specs += [pl.BlockSpec(memory_space=pl.ANY)] * 2
+        aliases.update({len(args): 0, len(args) + 1: 1})
+        in_specs += anywhere
         args += list(grads)
-        aliases = {4: 0, 5: 1}
-    return pl.pallas_call(
-        functools.partial(layer_kernel, row_tile),
-        grid=(ffn_width // block,),
-        in_specs=in_specs,
-        out_specs=[
-            pl.BlockSpec((1, width, block), lambda j: (layer, 0, j)),
-            pl.BlockSpec((1, block, width), lambda j: (layer, j, 0)),
-        ],
-        out_shape=[jax.ShapeDtypeStruct(w1.shape, F32), jax.ShapeDtypeStruct(w2.shape, F32)],
-        scratch_shapes=[pltpu.VMEM((block, total), BF16)] * 2,
+    if send:
+        out_specs += [wide(0, lambda j, c: j), tall(0, lambda j, c: j)]
+        out_shape += [jax.ShapeDtypeStruct((1, width, ffn_width // 2), F32), jax.ShapeDtypeStruct((1, ffn_width // 2, width), F32)]
+    if incoming is not None:
+        at, halves, targets = incoming
+        in_specs += [wide(0, lambda j, c: j), tall(0, lambda j, c: j)] + anywhere
+        aliases.update({len(args) + 2: len(out_shape), len(args) + 3: len(out_shape) + 1})
+        args += [*halves, *targets]
+        out_specs += [wide(at, other), tall(at, other)]
+        out_shape += [jax.ShapeDtypeStruct(t.shape, F32) for t in targets]
+    out = pl.pallas_call(
+        functools.partial(layer_kernel, row_tile, grads is not None, incoming is not None, send),
+        grid_spec=pltpu.PrefetchScalarGridSpec(
+            num_scalar_prefetch=1, grid=(steps,), in_specs=in_specs, out_specs=out_specs,
+            scratch_shapes=[pltpu.VMEM((block, total), BF16)] * 2),
+        out_shape=out_shape,
         input_output_aliases=aliases,
-        compiler_params=pltpu.CompilerParams(vmem_limit_bytes=56 * MIB, dimension_semantics=('arbitrary',)),
-        cost_estimate=pl.CostEstimate(flops=8 * total * width * ffn_width, bytes_accessed=60 * MIB, transcendentals=0),
+        compiler_params=pltpu.CompilerParams(vmem_limit_bytes=58 * MIB, dimension_semantics=('arbitrary',)),
+        cost_estimate=pl.CostEstimate(flops=8 * total * width * block * steps, bytes_accessed=40 * MIB, transcendentals=0),
         name='layer_grads',
     )(*args)
+    return [out[i:i + 2] for i in range(0, len(out), 2)]
 
 
 def ffn(h, w1, w2):
@@ -191,16 +232,15 @@
 def local_step(q_loc, d_loc, temperature, q_w1, q_w2, q_proj, d_w1, d_w2, d_proj):
     rows, width = q_loc.shape
     me = lax.axis_index('data')
-    d_h = [d_loc.reshape(2 * rows, width)]
-    q_h = [q_loc]
+    own0 = lax.optimization_barrier(jnp.concatenate([d_loc.reshape(2 * rows, width), q_loc], axis=0))
+    h0_all = gather(own0)
+    d_h = [own0[:2 * rows]]
+    q_h = [own0[2 * rows:]]
     for k in range(2):
         d_h.append(ffn(d_h[k], d_w1[k], d_w2[k]))
         q_h.append(ffn(q_h[k], q_w1[k], q_w2[k]))
-    h0_all = gather(jnp.concatenate([d_h[0], q_h[0]], axis=0))
     h1_all = gather(jnp.concatenate([d_h[1], q_h[1]], axis=0))
-    h2_all = gather_rows(jnp.concatenate([d_h[2], q_h[2]], axis=0))
-    d_last = h2_all[:, :2 * rows].reshape(-1, width)
-    q_last = h2_all[:, 2 * rows:].reshape(-1, width)
+    d_last, q_last = [h.reshape(-1, width) for h in gather_rows(jnp.concatenate([d_h[2], q_h[2]], axis=0))]
     docs = dot(d_last, d_proj).astype(BF16)
     queries = dot(q_last, q_proj).astype(BF16)
     batch = queries.shape[0]
@@ -227,10 +267,19 @@
     e0_all = gather(jnp.concatenate([d_e0, q_e0], axis=0))
     d_p = dot_tn(d_last, d_up)
     q_p = dot_tn(q_last, q_up)
-    d_g = layer_grads(1, h1_all, 0, d_e1, 0, 2 * rows, d_w1, d_w2)
-    q_g = layer_grads(1, h1_all, 2, q_e1, 0, rows, q_w1, q_w2)
-    d_g = layer_grads(0, h0_all, 0, e0_all, 0, 2 * rows, d_w1, d_w2, d_g)
-    q_g = layer_grads(0, h0_all, 2, e0_all, 2, rows, q_w1, q_w2, q_g)
+    core = (me % 2).reshape(1)
+
+    def swap(halves):
+        return [lax.ppermute(x, 'data', [(i, i ^ 1) for i in range(16)]) for x in halves]
+
+    q_g, q1 = layer_grads(core, 1, None, h1_all, 2, q_e1, 0, rows, q_w1, q_w2)
+    q1 = swap(q1)
+    d_g, d1 = layer_grads(core, 1, None, h1_all, 0, d_e1, 0, 2 * rows, d_w1, d_w2)
+    d1 = swap(d1)
+    d_g, d0, q_g = layer_grads(core, 0, None, h0_all, 0, e0_all, 0, 2 * rows, d_w1, d_w2, d_g, (1, q1, q_g))
+    d0 = swap(d0)
+    q_g, d_g = layer_grads(core, 0, 0, h0_all, 2, e0_all, 2, rows, q_w1, q_w2, q_g, (1, d1, d_g))
+    q_g, d_g = layer_grads(core, 0, 4, h0_all, 2, e0_all, 2, rows, q_w1, q_w2, q_g, (0, d0, d_g))
     return (loss, *q_g, q_p, *d_g, d_p)
 
 

time: 429 us -> 361 us (0.84)
  Pallas kernels: 281 us -> 212 us
  local copies, waits for them, and re-layouts: 12.3 us -> 4.34 us
  matrix products: 105 us -> 111 us
    pallas_call x5 -> x6, Pallas kernels: 281 us -> 212 us  [the longest x5 172 us: layer_grads(): pl.pallas_call(functools.partial(layer_kernel, row_tile, grads is not Non...]
    slice x2 -> x0, local copies, waits for them, and re-layouts: 7.96 us -> none  [the longest x1 4.81 us: local_step(): d_last = h2_all[:, :2 * rows].reshape(-1, width)]
    dot_general x9, matrix products: 48.7 us -> 53.5 us  [dot(): return jnp.dot(a, b, preferred_element_type=F32)]
  transfers between devices with their start and end apart: 3 -> 9, of which waited for: 0 -> 0; matrix products, arithmetic and copies ran while one was open for 24% -> 28% of each run, Pallas kernels for 38% -> 52%
where the time goes in v3:
time: 361 us; the launch traced here: 356 us
  Pallas kernels  212 us (59%)
  matrix products  111 us (31%)
  between operations  16.9 us (5%)
  other arithmetic  10.1 us (3%)
  local copies, waits for them, and re-layouts  4.34 us (1%)
    pallas_call x5, Pallas kernels, layer_grads(): pl.pallas_call(functools.partial(layer_kernel, row_tile, grads is not Non...  172 us
    dot_general x9, matrix products, dot(): return jnp.dot(a, b, preferred_element_type=F32)  53.5 us
    dot_general x7, matrix products, dot_nt(): return lax.dot_general(a, b, LAST_CONTRACT, preferred_element_type=F32)  39.5 us
    pallas_call x1, Pallas kernels, gather_rows(): pl.pallas_call(gather_kernel, out_shape=[jax.ShapeDtypeStruct((16, 2 * ro...  39.4 us
    dot_general x3, matrix products, dot_tn(): return lax.dot_general(a, b, ROWS_CONTRACT, preferred_element_type=F32)  17.6 us
  transfers between devices with their start and end apart: 9, of which 0 were waited for; matrix products, arithmetic and copies ran while one was open for 28% of the time, Pallas kernels for 52%

profile of v3, /device:TPU:0, one launch (start us, length us, event | category | flops | bytes accessed | tf_op | source)
XLA Modules:
  0.0 356.4 jit_solution(11704087774193392196)
XLA Ops:
  7.2 0.0 copy-start
  7.2 0.0 all-gather.11.cloned.1.call-start
  7.2 1.2 pad_maximum_fusion
  8.4 9.0 %fusion.85 = bf16[64,1024]{1,0:T(8,128)(2,1)S(1)} fusion(bf16[2,4096,1024]{2,1,0:T(8,128)(2,1)} %w2_ref.9, bf16[2,1024,4096]{2,1,0:T(8,128)(2,1)} %w1_ref.9, bf16[192,1024]{1,0:T(8,128)(2,1)S(1)} %pad_maximum_fusion), kind=kOutput, calls=%fused_computation.66 | convolution fusion | flops 1076035584 | bytes 17170432 | tf_op jit(solution)/shard_map/dot_general | solution.py:20
  17.5 8.7 %fusion.67 = bf16[128,1024]{1,0:T(8,128)(2,1)S(1)} fusion(bf16[2,4096,1024]{2,1,0:T(8,128)(2,1)} %w2_ref.7, bf16[2,1024,4096]{2,1,0:T(8,128)(2,1)} %w1_ref.7, bf16[192,1024]{1,0:T(8,128)(2,1)S(1)} %pad_maximum_fusion), kind=kOutput, calls=%fused_computation.60 | convolution fusion | flops 2152071168 | bytes 17563648 | tf_op jit(solution)/shard_map/dot_general | solution.py:20
  26.2 0.8 pad_maximum_fusion.3
  26.9 0.0 all-gather.11.cloned.1.call-update
  27.0 0.0 all-gather.7.cloned.1.call-start
  27.0 0.7 all-gather.7.cloned.1.call-update
  27.7 0.3 all-gather.9.cloned.1.call-start
  28.0 5.0 %fusion.6 = f32[64,4096]{1,0:T(8,128)S(1)} fusion(bf16[64,1024]{1,0:T(8,128)(2,1)S(1)} %fusion.85, bf16[2,1024,4096]{2,1,0:T(8,128)(2,1)} %w1_ref.9), kind=kOutput, calls=%fused_computation.6 | convolution fusion | flops 536870912 | bytes 9568256 | tf_op jit(solution)/shard_map/dot_general | solution.py:20
  32.9 1.0 copy-done.10
  33.9 4.9 %fusion.79 = bf16[64,1024]{1,0:T(8,128)(2,1)S(1)} fusion(bf16[2,4096,1024]{2,1,0:T(8,128)(2,1)} %w2_ref.9, f32[64,4096]{1,0:T(8,128)S(1)} %fusion.6, bf16[64,1024]{1,0:T(8,128)(2,1)S(1)} %fusion.85), kind=kOutput, calls=%fused_computation.64 | convolution fusion | flops 539164672 | bytes 9699328 | tf_op jit(solution)/shard_map/dot_general | solution.py:20
  38.8 6.0 %fusion.18 = f32[128,4096]{1,0:T(8,128)} fusion(bf16[128,1024]{1,0:T(8,128)(2,1)S(1)} %fusion.67, bf16[2,1024,4096]{2,1,0:T(8,128)(2,1)} %w1_ref.7), kind=kOutput, calls=%fused_computation.18 | convolution fusion | flops 1073741824 | bytes 10747904 | tf_op jit(solution)/shard_map/dot_general | solution.py:20
  45.4 5.5 %fusion.61 = bf16[128,1024]{1,0:T(8,128)(2,1)S(1)} fusion(bf16[2,4096,1024]{2,1,0:T(8,128)(2,1)} %w2_ref.7, f32[128,4096]{1,0:T(8,128)} %fusion.18, bf16[128,1024]{1,0:T(8,128)(2,1)S(1)} %fusion.67), kind=kOutput, calls=%fused_computation.58 | convolution fusion | flops 1078329344 | bytes 11010048 | tf_op jit(solution)/shard_map/dot_general | solution.py:20
  50.9 0.8 pad_maximum_fusion.1.x_ref
  51.7 39.4 %gather_rows.1 = (bf16[16,128,1024]{2,1,0:T(8,128)(2,1)}, bf16[16,64,1024]{2,1,0:T(8,128)(2,1)}) custom-call(bf16[192,1024]{1,0:T(8,128)(2,1)} %pad_maximum_fusion.1.x_ref), custom_call_target="tpu_custom_call" | custom-call | tf_op jit(solution)/shard_map/gather_rows/pallas_call | solution.py:124
  91.2 4.7 %convolution_convert_fusion.5 = bf16[1024,1024]{1,0:T(8,128)(2,1)S(1)} fusion(bf16[1024,1024]{1,0:T(8,128)(2,1)} %bitcast.118, bf16[1024,1024]{1,0:T(8,128)(2,1)} %param.14), kind=kOutput, calls=%fused_computation.54 | convolution fusion | flops 2148532224 | bytes 6291456 | tf_op jit(solution)/shard_map/dot_general | solution.py:20
  95.9 5.0 %convolution_convert_fusion.2 = bf16[2048,1024]{1,0:T(8,128)(2,1)S(1)} fusion(bf16[2048,1024]{1,0:T(8,128)(2,1)S(1)} %bitcast.116, bf16[1024,1024]{1,0:T(8,128)(2,1)S(1)} %copy-done), kind=kOutput, calls=%fused_computation.47 | convolution fusion | flops 4297064448 | bytes 10485760 | tf_op jit(solution)/shard_map/dot_general | solution.py:20
  100.9 4.6 %fusion.164 = (f32[1024]{0:T(1024)S(1)}, f32[1024,2048]{1,0:T(8,128)S(1)}) fusion(f32[]{:T(128)S(6)} %copy.40, bf16[1024,1024]{1,0:T(8,128)(2,1)S(1)} %convolution_convert_fusion.5, bf16[2048,1024]{1,0:T(8,128)(2,1)S(1)} %convolution_convert_fusion.2), kind=kOutput, calls=%fused_computation.140 | convolution fusion | flops 4299160576 | bytes 14684164 | tf_op jit(solution)/shard_map/dot_general | solution.py:24
  105.5 3.2 select_reduce_fusion
  108.7 0.6 subtract_reduce_fusion
  109.4 2.8 divide_convert_fusion
  112.2 4.7 %convolution_convert_fusion.4 = bf16[1024,1024]{1,0:T(8,128)(2,1)S(1)} fusion(bf16[1024,2048]{1,0:T(8,128)(2,1)S(1)} %divide_convert_fusion, bf16[2048,1024]{1,0:T(8,128)(2,1)S(1)} %convolution_convert_fusion.2), kind=kOutput, calls=%fused_computation.53 | convolution fusion | flops 4296015872 | bytes 10485760 | tf_op jit(solution)/shard_map/dot_general | solution.py:20
  116.9 1.3 copy-done.6
  118.2 0.8 fusion.127
  119.0 5.4 %convolution_convert_fusion.1 = bf16[2048,1024]{1,0:T(8,128)(2,1)S(1)} fusion(bf16[1024,2048]{1,0:T(8,128)(2,1)S(1)} %divide_convert_fusion, bf16[1024,1024]{1,0:T(8,128)(2,1)S(1)} %convolution_convert_fusion.5), kind=kOutput, calls=%fused_computation.46 | convolution fusion | flops 4297064448 | bytes 10485760 | tf_op jit(solution)/shard_map/dot_general | solution.py:28
  124.4 2.0 copy-done.4
  126.4 0.8 fusion.121
  127.2 9.1 %fusion.82 = bf16[64,1024]{1,0:T(8,128)(2,1)S(1)} fusion(f32[64,1024]{1,0:T(8,128)S(1)} %fusion.127, bf16[2,1024,4096]{2,1,0:T(8,128)(2,1)} %w1_ref.9, bf16[2,4096,1024]{2,1,0:T(8,128)(2,1)} %w2_ref.9, f32[64,4096]{1,0:T(8,128)} %copy-done.10), kind=kOutput, calls=%fused_computation.65 | convolution fusion | flops 1077870592 | bytes 18481152 | tf_op jit(solution)/shard_map/dot_general | solution.py:24
  136.3 9.9 %fusion.64 = bf16[128,1024]{1,0:T(8,128)(2,1)S(1)} fusion(f32[128,1024]{1,0:T(8,128)S(1)} %fusion.121, bf16[2,1024,4096]{2,1,0:T(8,128)(2,1)} %w1_ref.7, bf16[2,4096,1024]{2,1,0:T(8,128)(2,1)} %w2_ref.7, f32[128,4096]{1,0:T(8,128)} %fusion.18), kind=kOutput, calls=%fused_computation.59 | convolution fusion | flops 2155741184 | bytes 20185088 | tf_op jit(solution)/shard_map/dot_general | solution.py:24
  146.3 0.8 pad_maximum_fusion.2
  147.0 0.0 all-gather.9.cloned.1.call-update
  147.1 5.9 %convolution_convert_fusion.3 = bf16[1024,1024]{1,0:T(8,128)(2,1)} fusion(bf16[1024,1024]{1,0:T(8,128)(2,1)} %copy-done.6, bf16[1024,1024]{1,0:T(8,128)(2,1)} %param.14), kind=kOutput, calls=%fused_computation.52 | convolution fusion | flops 2148532224 | bytes 6291456 | tf_op jit(solution)/shard_map/dot_general | solution.py:24
  153.0 25.4 %layer_grads.6 = (f32[2,1024,4096]{2,1,0:T(8,128)}, f32[2,4096,1024]{2,1,0:T(8,128)}, f32[1,1024,2048]{2,1,0:T(8,128)}, f32[1,2048,1024]{2,1,0:T(8,128)}) custom-call(s32[1]{0:T(128)} %bitcast.11.core_ref, bf16[16,192,1024]{2,1,0:T(8,128)(2,1)} %bitcast.114, bf16[16,64,1024]{2,1,0:T(8,128)(2,1)} %bitcast.121, bf16[2,1024,4096]{2,1,0:T(8,128)(2,1)} %w1_ref.9, ...), custom_call_target="tpu_custom_call" | custom-call | flops 17179869184 | bytes 41943040 | tf_op jit(solution)/shard_map/layer_grads/pallas_call | solution.py:208
  178.4 0.3 collective-permute-start
  178.7 0.2 collective-permute-start.1
  178.9 8.3 %convolution_convert_fusion = bf16[2048,1024]{1,0:T(8,128)(2,1)} fusion(bf16[2048,1024]{1,0:T(8,128)(2,1)} %copy-done.4, bf16[1024,1024]{1,0:T(8,128)(2,1)S(1)} %copy-done), kind=kOutput, calls=%fused_computation.45 | convolution fusion | flops 4297064448 | bytes 10485760 | tf_op jit(solution)/shard_map/dot_general | solution.py:24
  187.2 44.1 %layer_grads.5 = (f32[2,1024,4096]{2,1,0:T(8,128)}, f32[2,4096,1024]{2,1,0:T(8,128)}, f32[1,1024,2048]{2,1,0:T(8,128)}, f32[1,2048,1024]{2,1,0:T(8,128)}) custom-call(s32[1]{0:T(128)} %bitcast.11.core_ref, bf16[16,192,1024]{2,1,0:T(8,128)(2,1)} %bitcast.115, bf16[16,128,1024]{2,1,0:T(8,128)(2,1)} %bitcast.120, bf16[2,1024,4096]{2,1,0:T(8,128)(2,1)} %w1_ref.7, ...), custom_call_target="tpu_custom_call" | custom-call | flops 34359738368 | bytes 41943040 | tf_op jit(solution)/shard_map/layer_grads/pallas_call | solution.py:208
  231.3 0.3 collective-permute-start.2
  231.6 0.2 collective-permute-start.3
  231.8 47.7 %layer_grads.7 = (f32[2,1024,4096]{2,1,0:T(8,128)}, f32[2,4096,1024]{2,1,0:T(8,128)}, f32[1,1024,2048]{2,1,0:T(8,128)}, f32[1,2048,1024]{2,1,0:T(8,128)}, f32[2,...) custom-call(s32[1]{0:T(128)} %bitcast.11.core_ref, ...), custom_call_target="tpu_custom_call", output_to_operand_aliasing={{0}: (5, {}), {1}: (6, {}), {4}: (9, {}), {5}: (10, {})} | custom-call | flops 34359738368 | bytes 41943040 | tf_op jit(solution)/shard_map/layer_grads/pallas_call | solution.py:208
  279.5 0.3 collective-permute-start.4
  279.8 0.2 collective-permute-start.5
  280.7 6.1 %fusion.165 = f32[1024,1024]{1,0:T(8,128)} fusion(bf16[1024,1024]{1,0:T(8,128)(2,1)} %bitcast.119, bf16[1024,1024]{1,0:T(8,128)(2,1)S(1)} %copy-done.7), kind=kOutput, calls=%fused_computation.141 | convolution fusion | flops 2147483648 | bytes 8388608 | tf_op jit(solution)/shard_map/dot_general | solution.py:28
  286.9 6.1 %fusion.166 = f32[1024,1024]{1,0:T(8,128)} fusion(bf16[2048,1024]{1,0:T(8,128)(2,1)S(1)} %bitcast.117, bf16[2048,1024]{1,0:T(8,128)(2,1)S(1)} %copy-done.5), kind=kOutput, calls=%fused_computation.142 | convolution fusion | flops 4294967296 | bytes 12582912 | tf_op jit(solution)/shard_map/dot_general | solution.py:28
  292.9 27.7 %layer_grads.8 = (f32[2,1024,4096]{2,1,0:T(8,128)}, f32[2,4096,1024]{2,1,0:T(8,128)}, f32[2,1024,4096]{2,1,0:T(8,128)}, f32[2,4096,1024]{2,1,0:T(8,128)}) custom-call(s32[1]{0:T(128)} %bitcast.11.core_ref, bf16[16,192,1024]{2,1,0:T(8,128)(2,1)} %bitcast.108, ...), custom_call_target="tpu_custom_call", output_to_operand_aliasing={{0}: (5, {}), {1}: (6, {}), {2}: (9, {}), {3}: (10, {})} | custom-call | flops 17179869184 | bytes 41943040 | tf_op jit(solution)/shard_map/layer_grads/pallas_call | solution.py:208
  320.7 27.5 %layer_grads.9 = (f32[2,1024,4096]{2,1,0:T(8,128)}, f32[2,4096,1024]{2,1,0:T(8,128)}, f32[2,1024,4096]{2,1,0:T(8,128)}, f32[2,4096,1024]{2,1,0:T(8,128)}) custom-call(s32[1]{0:T(128)} %bitcast.11.core_ref, bf16[16,192,1024]{2,1,0:T(8,128)(2,1)} %bitcast.109, ...), custom_call_target="tpu_custom_call", output_to_operand_aliasing={{0}: (5, {}), {1}: (6, {}), {2}: (9, {}), {3}: (10, {})} | custom-call | flops 17179869184 | bytes 41943040 | tf_op jit(solution)/shard_map/layer_grads/pallas_call | solution.py:208
  (29 shorter events, 0.1 us)
Async XLA Ops:
  7.2 88.7 %copy-start = (bf16[1024,1024]{1,0:T(8,128)(2,1)S(1)}, bf16[1024,1024]{1,0:T(8,128)(2,1)}, u32[]{:S(2)}) copy-start(bf16[1024,1024]{1,0:T(8,128)(2,1)} %param.17) | copy-start | bytes 6291460
  7.2 145.8 %all-gather.11.cloned.1.call-start = ((), (), s32[]{:S(2)}) async-start(), calls=%async_computation.2 | async-start | bytes 6684672 | tf_op jit(solution)/shard_map/all_gather | solution.py:229
  8.4 9.1 %copy-start.3 = (bf16[192,1024]{1,0:T(8,128)(2,1)}, bf16[192,1024]{1,0:T(8,128)(2,1)S(1)}, u32[]{:S(2)}) copy-start(bf16[192,1024]{1,0:T(8,128)(2,1)S(1)} %pad_maximum_fusion) | copy-start | bytes 1179652
  27.0 204.8 %all-gather.7.cloned.1.call-start = ((), (), s32[]{:S(2)}) async-start(), calls=%async_computation | async-start | bytes 6684672 | tf_op jit(solution)/shard_map/all_gather | solution.py:229
  27.7 204.1 %all-gather.9.cloned.1.call-start = ((), (), s32[]{:S(2)}) async-start(), calls=%async_computation.1 | async-start | bytes 6684672 | tf_op jit(solution)/shard_map/all_gather | solution.py:229
  32.9 1.0 copy-start.10
  91.2 4.7 %copy-start.8 = (bf16[16,128,1024]{2,1,0:T(8,128)(2,1)S(1)}, bf16[16,128,1024]{2,1,0:T(8,128)(2,1)}, u32[]{:S(2)}) copy-start(bf16[16,128,1024]{2,1,0:T(8,128)(2,1)} %get-tuple-element.32) | copy-start | bytes 12582916
  112.2 6.1 %copy-start.2 = (bf16[1024,1024]{1,0:T(8,128)(2,1)S(1)}, bf16[1024,1024]{1,0:T(8,128)(2,1)}, u32[]{:S(2)}) copy-start(bf16[1024,1024]{1,0:T(8,128)(2,1)} %param.14) | copy-start | bytes 6291460
  116.9 1.3 copy-start.6
  124.4 2.0 copy-start.4
  178.4 53.4 %collective-permute-start = (f32[1,1024,2048]{2,1,0:T(8,128)}, f32[1,1024,2048]{2,1,0:T(8,128)}, u32[]{:S(2)}, u32[]{:S(2)}) collective-permute-start(f32[1,1024,2048]{2,1,0:T(8,128)} %get-tuple-element.35), channel_id=1, source_target_pairs={{0,1},{1,0},{2,3},{3,2},{4,5},{5,4},{6,7},{7,6},{8,9},{9,8},{10,11... | collective-permute-start | bytes 25165832 | tf_op jit(solution)/shard_map/ppermute | solution.py:273
  178.7 53.1 %collective-permute-start.1 = (f32[1,2048,1024]{2,1,0:T(8,128)}, f32[1,2048,1024]{2,1,0:T(8,128)}, u32[]{:S(2)}, u32[]{:S(2)}) collective-permute-start(f32[1,2048,1024]{2,1,0:T(8,128)} %get-tuple-element.36), channel_id=1, source_target_pairs={{0,1},{1,0},{2,3},{3,2},{4,5},{5,4},{6,7},{7,6},{8,9},{9,8},{10,11... | collective-permute-start | bytes 25165832 | tf_op jit(solution)/shard_map/ppermute | solution.py:273
  231.3 61.7 %collective-permute-start.2 = (f32[1,1024,2048]{2,1,0:T(8,128)}, f32[1,1024,2048]{2,1,0:T(8,128)}, u32[]{:S(2)}, u32[]{:S(2)}) collective-permute-start(f32[1,1024,2048]{2,1,0:T(8,128)} %get-tuple-element.41), channel_id=1, source_target_pairs={{0,1},{1,0},{2,3},{3,2},{4,5},{5,4},{6,7},{7,6},{8,9},{9,8},{10,11... | collective-permute-start | bytes 25165832 | tf_op jit(solution)/shard_map/ppermute | solution.py:273
  231.6 61.3 %collective-permute-start.3 = (f32[1,2048,1024]{2,1,0:T(8,128)}, f32[1,2048,1024]{2,1,0:T(8,128)}, u32[]{:S(2)}, u32[]{:S(2)}) collective-permute-start(f32[1,2048,1024]{2,1,0:T(8,128)} %get-tuple-element.42), channel_id=1, source_target_pairs={{0,1},{1,0},{2,3},{3,2},{4,5},{5,4},{6,7},{7,6},{8,9},{9,8},{10,11... | collective-permute-start | bytes 25165832 | tf_op jit(solution)/shard_map/ppermute | solution.py:273
  231.8 48.9 %copy-start.7 = (bf16[1024,1024]{1,0:T(8,128)(2,1)S(1)}, bf16[1024,1024]{1,0:T(8,128)(2,1)}, u32[]{:S(2)}) copy-start(bf16[1024,1024]{1,0:T(8,128)(2,1)} %copy-done.6) | copy-start | bytes 6291460
  279.5 41.2 %collective-permute-start.4 = (f32[1,1024,2048]{2,1,0:T(8,128)}, f32[1,1024,2048]{2,1,0:T(8,128)}, u32[]{:S(2)}, u32[]{:S(2)}) collective-permute-start(f32[1,1024,2048]{2,1,0:T(8,128)} %get-tuple-element.47), channel_id=1, source_target_pairs={{0,1},{1,0},{2,3},{3,2},{4,5},{5,4},{6,7},{7,6},{8,9},{9,8},{10,11... | collective-permute-start | bytes 25165832 | tf_op jit(solution)/shard_map/ppermute | solution.py:273
  279.8 40.8 %collective-permute-start.5 = (f32[1,2048,1024]{2,1,0:T(8,128)}, f32[1,2048,1024]{2,1,0:T(8,128)}, u32[]{:S(2)}, u32[]{:S(2)}) collective-permute-start(f32[1,2048,1024]{2,1,0:T(8,128)} %get-tuple-element.48), channel_id=1, source_target_pairs={{0,1},{1,0},{2,3},{3,2},{4,5},{5,4},{6,7},{7,6},{8,9},{9,8},{10,11... | collective-permute-start | bytes 25165832 | tf_op jit(solution)/shard_map/ppermute | solution.py:273
  280.7 6.2 %copy-start.5 = (bf16[2048,1024]{1,0:T(8,128)(2,1)S(1)}, bf16[2048,1024]{1,0:T(8,128)(2,1)}, u32[]{:S(2)}) copy-start(bf16[2048,1024]{1,0:T(8,128)(2,1)} %copy-done.4) | copy-start | bytes 12582916
  280.7 6.2 %copy-start.9 = (bf16[16,128,1024]{2,1,0:T(8,128)(2,1)S(1)}, bf16[16,128,1024]{2,1,0:T(8,128)(2,1)}, u32[]{:S(2)}) copy-start(bf16[16,128,1024]{2,1,0:T(8,128)(2,1)} %get-tuple-element.32) | copy-start | bytes 12582916
  320.7 27.5 %copy-start.1 = (bf16[1024,1024]{1,0:T(8,128)(2,1)S(1)}, bf16[1024,1024]{1,0:T(8,128)(2,1)}, u32[]{:S(2)}) copy-start(bf16[1024,1024]{1,0:T(8,128)(2,1)} %param.17) | copy-start | bytes 6291460
Sparse Core Ops, SparseCore 0:
  27.1 56.2 all-gather.10
  85.6 41.8 all-gather.6
  147.2 42.2 all-gather.8

commit v4 on v3

--- a/solution.py
+++ b/solution.py
@@ -40,96 +40,241 @@
     return u.astype(BF16), (slope * t).astype(BF16)
 
 
-def gather_kernel(x_ref, d_ref, q_ref, send_sem, recv_sem, pair_send, pair_recv, own_sem, own_send, own_recv):
-    parts, rows = 3, x_ref.shape[0] // 3
+BLOCK = 1024
+THIRDS = ((0, 384), (384, 384), (768, 256))
+ORDERS = ((2, 4, 8), (4, 8, 2), (8, 2, 4))
+
+
+def flip(device, bit):
+    return device + bit * (1 - 2 * (lax.div(device, bit) % 2))
+
+
+def forward_kernel(x_ref, dw1_ref, dw2_ref, qw1_ref, qw2_ref, h1_ref, d_all, q_all, acc_ref, h_ref, h2_ref,
+                   send_sem, recv_sem, pair_send, pair_recv, own_sem, own_send, own_recv):
+    s = pl.program_id(0)
+    per = pl.num_programs(0) // 4
     me = lax.axis_index('data')
-
-    def flip(device, bit):
-        return device + bit * (1 - 2 * (lax.div(device, bit) % 2))
-
-    def walk(device, mask, axes):
+    partner = flip(me, 1)
+    d_rows = d_all.shape[1]
+    q_rows = q_all.shape[1]
+    towers = ((pl.ds(0, d_rows), d_all), (pl.ds(d_rows, q_rows), q_all))
+
+    def walk(p, mask):
+        device = me
         for i in range(3):
             if mask & (1 << i):
-                device = flip(device, axes[i])
+                device = flip(device, ORDERS[p][i])
         return device
 
-    partner = flip(me, 1)
-    barrier = pltpu.get_barrier_semaphore()
-    for bit in (1, 2, 4, 8):
-        pl.semaphore_signal(barrier, inc=1, device_id=(flip(me, bit),), device_id_type=pl.DeviceIdType.MESH)
-    pl.semaphore_wait(barrier, 4)
-
-    started = []
-
-    def piece(shard, p):
-        return q_ref.at[shard] if p == 2 else d_ref.at[shard, pl.ds(p * rows, rows)]
-
-    def send(p, mask, step, axes):
-        shard = walk(me, mask, axes)
-        source = x_ref.at[pl.ds(p * rows, rows)] if mask == 0 else piece(shard, p)
+    def remote(source, target, send, recv, device):
+        return pltpu.make_async_remote_copy(src_ref=source, dst_ref=target, send_sem=send, recv_sem=recv,
+                                            device_id=(device,), device_id_type=pl.DeviceIdType.MESH)
+
+    def hop(t, p, mask, step):
+        rows, out = towers[t]
+        cols = pl.ds(*THIRDS[p])
+        shard = walk(p, mask)
+        source = h2_ref.at[rows, cols] if mask == 0 else out.at[shard, :, cols]
         seen = mask | (1 << step)
-        copy = pltpu.make_async_remote_copy(
-            src_ref=source, dst_ref=piece(shard, p), send_sem=send_sem.at[p, seen], recv_sem=recv_sem.at[p, seen],
-            device_id=(flip(me, axes[step]),), device_id_type=pl.DeviceIdType.MESH)
-        copy.start()
-        started.append(copy)
-
-    def relay(p, mask, axes):
-        shard = walk(me, mask, axes)
-        copy = pltpu.make_async_remote_copy(
-            src_ref=piece(shard, p), dst_ref=piece(shard, p), send_sem=pair_send.at[p, mask], recv_sem=pair_recv.at[p, mask],
-            device_id=(partner,), device_id_type=pl.DeviceIdType.MESH)
-        copy.start()
-        pairs.append(copy)
-
-    pairs = []
-    orders = [(2, 4, 8), (4, 8, 2), (8, 2, 4)]
-    for step in range(3):
-        for p in range(parts):
-            send(p, 0, step, orders[p])
-    owns = []
-    for p in range(parts):
-        source = x_ref.at[pl.ds(p * rows, rows)]
-        own = pltpu.make_async_copy(source, piece(me, p), own_sem.at[p])
-        own.start()
-        owns.append(own)
-        copy = pltpu.make_async_remote_copy(
-            src_ref=source, dst_ref=piece(me, p), send_sem=own_send.at[p], recv_sem=own_recv.at[p],
-            device_id=(partner,), device_id_type=pl.DeviceIdType.MESH)
-        copy.start()
-        pairs.append(copy)
-
-    def arrived(p, mask):
-        pltpu.make_async_remote_copy(
-            src_ref=piece(me, p), dst_ref=piece(walk(me, mask, orders[p]), p), send_sem=send_sem.at[p, mask],
-            recv_sem=recv_sem.at[p, mask], device_id=(partner,), device_id_type=pl.DeviceIdType.MESH).wait_recv()
-
-    for mask in (1, 2, 3, 4, 5, 6, 7):
-        first = 1 if mask == 1 else 2 if mask < 4 else 3
-        for p in range(parts):
-            arrived(p, mask)
-            for step in range(first, 3):
-                send(p, mask, step, orders[p])
-            relay(p, mask, orders[p])
-    for copy in started:
-        copy.wait_send()
-    for copy in pairs:
-        copy.wait()
-    for copy in owns:
-        copy.wait()
-
-
-def gather_rows(x):
-    rows = x.shape[0] // 3
+        return remote(source, out.at[shard, :, cols], send_sem.at[t, p, seen], recv_sem.at[t, p, seen], flip(me, ORDERS[p][step]))
+
+    def relay(t, p, mask):
+        part = towers[t][1].at[walk(p, mask), :, pl.ds(*THIRDS[p])]
+        return remote(part, part, pair_send.at[t, p, mask], pair_recv.at[t, p, mask], partner)
+
+    def arrived(t, p, mask):
+        part = towers[t][1].at[walk(p, mask), :, pl.ds(*THIRDS[p])]
+        remote(part, part, send_sem.at[t, p, mask], recv_sem.at[t, p, mask], partner).wait_recv()
+
+    def own_pair(t):
+        rows, out = towers[t]
+        return remote(h2_ref.at[rows], out.at[me], own_send.at[t], own_recv.at[t], partner)
+
+    def own_copy(t):
+        rows, out = towers[t]
+        return pltpu.make_async_copy(h2_ref.at[rows], out.at[me], own_sem.at[t])
+
+    def begin(t):
+        for step in range(3):
+            for p in range(3):
+                hop(t, p, 0, step).start()
+        own_copy(t).start()
+        own_pair(t).start()
+
+    def onward(t, masks):
+        for mask in masks:
+            for p in range(3):
+                arrived(t, p, mask)
+                for step in range(mask.bit_length(), 3):
+                    hop(t, p, mask, step).start()
+                relay(t, p, mask).start()
+
+    def layers(first, rows, w1_ref, w2_ref):
+        @pl.when(s == first)
+        def _():
+            h_ref[rows, :] = x_ref[rows, :]
+
+        @pl.when((s - first) % per == 0)
+        def _():
+            acc_ref[rows, :] = h_ref[rows, :].astype(F32)
+
+        pre = dot(h_ref[rows, :], w1_ref[0])
+        acc_ref[rows, :] += dot((pre * gelu_cdf(pre)[1]).astype(BF16), w2_ref[0])
+
+        @pl.when(s == first + per - 1)
+        def _():
+            h1 = acc_ref[rows, :].astype(BF16)
+            h_ref[rows, :] = h1
+            h1_ref[rows, :] = h1
+
+        @pl.when(s == first + 2 * per - 1)
+        def _():
+            h2_ref[rows, :] = acc_ref[rows, :].astype(BF16)
+
+    @pl.when(s == 0)
+    def _():
+        barrier = pltpu.get_barrier_semaphore()
+        for bit in (1, 2, 4, 8):
+            pl.semaphore_signal(barrier, inc=1, device_id=(flip(me, bit),), device_id_type=pl.DeviceIdType.MESH)
+        pl.semaphore_wait(barrier, 4)
+
+    @pl.when(s == 2 * per)
+    def _():
+        begin(0)
+
+    @pl.when(s == 2 * per + per // 2)
+    def _():
+        onward(0, (1,))
+
+    @pl.when(s == 3 * per)
+    def _():
+        onward(0, (2,))
+
+    @pl.when(s == 3 * per + per // 4)
+    def _():
+        onward(0, (3,))
+
+    @pl.when(s < 2 * per)
+    def _():
+        layers(0, towers[0][0], dw1_ref, dw2_ref)
+
+    @pl.when((s >= 2 * per) & (s < 4 * per))
+    def _():
+        layers(2 * per, towers[1][0], qw1_ref, qw2_ref)
+
+    @pl.when(s == 4 * per)
+    def _():
+        begin(1)
+        onward(0, (4, 5, 6, 7))
+        onward(1, (1, 2, 3, 4, 5, 6, 7))
+        for t in range(2):
+            for p in range(3):
+                for mask in range(8):
+                    for step in range(mask.bit_length(), 3):
+                        hop(t, p, mask, step).wait_send()
+                    if mask:
+                        relay(t, p, mask).wait()
+            own_copy(t).wait()
+            own_pair(t).wait()
+
+
+def forward(own0, d_w1, d_w2, q_w1, q_w2):
+    rows, width = own0.shape
+    per = d_w1.shape[2] // BLOCK
+
+    def place(s):
+        f = s // (2 * per)
+        return f - f // 2, f // 2, (s // per) % 2, s % per
+
+    def at_d(s):
+        f, _, layer, j = place(s)
+        f = s // (2 * per)
+        f = f - f // 2
+        return layer * (1 - f) + f, j * (1 - f) + (per - 1) * f
+
+    def at_q(s):
+        f, end, layer, j = place(s)
+        live = f - end
+        return layer * live + end, j * live + (per - 1) * end
+
+    def wide(at):
+        return pl.BlockSpec((1, width, BLOCK), lambda s: (at(s)[0], 0, at(s)[1]))
+
+    def tall(at):
+        return pl.BlockSpec((1, BLOCK, width), lambda s: (at(s)[0], at(s)[1], 0))
+
+    third = rows // 3
+    sems = pltpu.SemaphoreType.DMA
     return pl.pallas_call(
-        gather_kernel,
-        out_shape=[jax.ShapeDtypeStruct((16, 2 * rows, x.shape[1]), x.dtype), jax.ShapeDtypeStruct((16, rows, x.shape[1]), x.dtype)],
-        in_specs=[pl.BlockSpec(memory_space=pltpu.VMEM)],
-        out_specs=[pl.BlockSpec(memory_space=pl.ANY)] * 2,
-        scratch_shapes=[pltpu.SemaphoreType.DMA((3, 8))] * 4 + [pltpu.SemaphoreType.DMA((3,))] * 3,
-        compiler_params=pltpu.CompilerParams(collective_id=0, has_side_effects=True),
-        name='gather_rows',
-    )(x)
+        forward_kernel,
+        grid=(4 * per + 1,),
+        in_specs=[pl.BlockSpec((rows, width), lambda s: (0, 0)), wide(at_d), tall(at_d), wide(at_q), tall(at_q)],
+        out_specs=[pl.BlockSpec((rows, width), lambda s: (0, 0))] + [pl.BlockSpec(memory_space=pl.ANY)] * 2,
+        out_shape=[jax.ShapeDtypeStruct((rows, width), BF16), jax.ShapeDtypeStruct((16, 2 * third, width), BF16),
+                   jax.ShapeDtypeStruct((16, third, width), BF16)],
+        scratch_shapes=[pltpu.VMEM((rows, width), F32), pltpu.VMEM((rows, width), BF16), pltpu.VMEM((rows, width), BF16),
+                        sems((2, 3, 8)), sems((2, 3, 8)), sems((2, 3, 8)), sems((2, 3, 8)), sems((2,)), sems((2,)), sems((2,))],
+        compiler_params=pltpu.CompilerParams(collective_id=0, has_side_effects=True, dimension_semantics=('arbitrary',)),
+        cost_estimate=pl.CostEstimate(flops=8 * rows * width * d_w1.shape[2], bytes_accessed=72 * MIB, transcendentals=0),
+        name='forward',
+    )(own0, d_w1, d_w2, q_w1, q_w2)
+
+
+def chain_kernel(h_ref, e_ref, dw1_ref, dw2_ref, qw1_ref, qw2_ref, out_ref, acc_ref):
+    s = pl.program_id(0)
+    per = pl.num_programs(0) // 2
+    third = h_ref.shape[0] // 3
+
+    def block(rows, w1_ref, w2_ref):
+        pre = dot(h_ref[rows, :], w1_ref[0])
+        t = dot_nt(e_ref[rows, :].astype(BF16), w2_ref[0])
+        acc_ref[rows, :] += dot_nt(gelu_and_back(pre, t)[1], w1_ref[0])
+
+    @pl.when(s == 0)
+    def _():
+        acc_ref[...] = e_ref[...]
+
+    @pl.when(s < per)
+    def _():
+        block(pl.ds(0, 2 * third), dw1_ref, dw2_ref)
+
+    @pl.when(s >= per)
+    def _():
+        block(pl.ds(2 * third, third), qw1_ref, qw2_ref)
+
+    @pl.when(s == 2 * per - 1)
+    def _():
+        out_ref[...] = acc_ref[...].astype(BF16)
+
+
+def chain(h1_own, e1_own, d_w1, d_w2, q_w1, q_w2):
+    rows, width = h1_own.shape
+    per = d_w1.shape[2] // BLOCK
+
+    def at_d(s):
+        return (s % per) * (1 - s // per) + (per - 1) * (s // per)
+
+    def at_q(s):
+        return (s % per) * (s // per)
+
+    def wide(at):
+        return pl.BlockSpec((1, width, BLOCK), lambda s: (1, 0, at(s)))
+
+    def tall(at):
+        return pl.BlockSpec((1, BLOCK, width), lambda s: (1, at(s), 0))
+
+    whole = pl.BlockSpec((rows, width), lambda s: (0, 0))
+    return pl.pallas_call(
+        chain_kernel,
+        grid=(2 * per,),
+        in_specs=[whole, whole, wide(at_d), tall(at_d), wide(at_q), tall(at_q)],
+        out_specs=whole,
+        out_shape=jax.ShapeDtypeStruct((rows, width), BF16),
+        scratch_shapes=[pltpu.VMEM((rows, width), F32)],
+        compiler_params=pltpu.CompilerParams(dimension_semantics=('arbitrary',)),
+        cost_estimate=pl.CostEstimate(flops=4 * rows * width * d_w1.shape[2], bytes_accessed=36 * MIB, transcendentals=0),
+        name='chain',
+    )(h1_own, e1_own, d_w1, d_w2, q_w1, q_w2)
 
 
 def layer_kernel(row_tile, in_place, incoming, send, core_ref, h_ref, e_ref, w1_ref, w2_ref, *rest):
@@ -219,12 +364,6 @@
     return [out[i:i + 2] for i in range(0, len(out), 2)]
 
 
-def ffn(h, w1, w2):
-    pre = dot(h, w1)
-    u = (pre * gelu_cdf(pre)[1]).astype(BF16)
-    return (h.astype(F32) + dot(u, w2)).astype(BF16)
-
-
 def gather(x):
     return lax.all_gather(x, 'data', axis=0)
 
@@ -232,15 +371,12 @@
 def local_step(q_loc, d_loc, temperature, q_w1, q_w2, q_proj, d_w1, d_w2, d_proj):
     rows, width = q_loc.shape
     me = lax.axis_index('data')
-    own0 = lax.optimization_barrier(jnp.concatenate([d_loc.reshape(2 * rows, width), q_loc], axis=0))
-    h0_all = gather(own0)
-    d_h = [own0[:2 * rows]]
-    q_h = [own0[2 * rows:]]
-    for k in range(2):
-        d_h.append(ffn(d_h[k], d_w1[k], d_w2[k]))
-        q_h.append(ffn(q_h[k], q_w1[k], q_w2[k]))
-    h1_all = gather(jnp.concatenate([d_h[1], q_h[1]], axis=0))
-    d_last, q_last = [h.reshape(-1, width) for h in gather_rows(jnp.concatenate([d_h[2], q_h[2]], axis=0))]
+    own0 = jnp.concatenate([d_loc.reshape(2 * rows, width), q_loc], axis=0)
+    h1_own, d_last, q_last = forward(own0, d_w1, d_w2, q_w1, q_w2)
+    d_last = d_last.reshape(-1, width)
+    q_last = q_last.reshape(-1, width)
+    h1_all = gather(h1_own)
+    h0_all = gather(lax.optimization_barrier((own0, h1_own))[0])
     docs = dot(d_last, d_proj).astype(BF16)
     queries = dot(q_last, q_proj).astype(BF16)
     batch = queries.shape[0]
@@ -255,16 +391,15 @@
     q_up = dot(grad, docs).astype(BF16)
     d_up = dot_tn(grad, queries).astype(BF16)
 
-    def chain(h1_own, up, w1, w2, proj):
-        own = h1_own.shape[0]
-        e1_bf = dot_nt(up, proj).astype(BF16)
+    def start(up, proj):
+        own = up.shape[0] // 16
         e1_own = dot_nt(lax.dynamic_slice_in_dim(up, me * own, own, 0), proj)
-        delta = gelu_and_back(dot(h1_own, w1[1]), dot_nt(e1_own.astype(BF16), w2[1]))[1]
-        return e1_bf.reshape(16, own, width), (e1_own + dot_nt(delta, w1[1])).astype(BF16)
-
-    d_e1, d_e0 = chain(d_h[1], d_up, d_w1, d_w2, d_proj)
-    q_e1, q_e0 = chain(q_h[1], q_up, q_w1, q_w2, q_proj)
-    e0_all = gather(jnp.concatenate([d_e0, q_e0], axis=0))
+        return dot_nt(up, proj).astype(BF16).reshape(16, own, width), e1_own
+
+    d_e1, d_e1_own = start(d_up, d_proj)
+    q_e1, q_e1_own = start(q_up, q_proj)
+    e1_own = jnp.concatenate([d_e1_own, q_e1_own], axis=0)
+    e0_all = gather(chain(h1_own, e1_own, d_w1, d_w2, q_w1, q_w2))
     d_p = dot_tn(d_last, d_up)
     q_p = dot_tn(q_last, q_up)
     core = (me % 2).reshape(1)

time: 361 us -> 333 us (0.922)
  matrix products: 111 us -> 52.5 us
  Pallas kernels: 212 us -> 245 us
    dot_general x9 -> x3, matrix products: 53.5 us -> 14.3 us  [dot(): return jnp.dot(a, b, preferred_element_type=F32)]
    pallas_call x1 -> x2, Pallas kernels: 39.4 us -> 72.8 us  [the longest x1 51.5 us: forward(): pl.pallas_call(forward_kernel, grid=(4 * per + 1,), in_specs=[pl.BlockSpe...]
    dot_general x7 -> x5, matrix products: 39.5 us -> 20.8 us  [dot_nt(): return lax.dot_general(a, b, LAST_CONTRACT, preferred_element_type=F32)]
  transfers between devices with their start and end apart: 9 -> 9, of which waited for: 0 -> 0; matrix products, arithmetic and copies ran while one was open for 28% -> 18% of each run, Pallas kernels for 52% -> 50%
where the time goes in v4:
time: 333 us; the launch traced here: 329 us
  Pallas kernels  245 us (74%)
  matrix products  52.5 us (16%)
  between operations  16.6 us (5%)
  other arithmetic  9.5 us (3%)
  local copies, waits for them, and re-layouts  3.39 us (1%)
    pallas_call x5, Pallas kernels, layer_grads(): pl.pallas_call(functools.partial(layer_kernel, row_tile, grads is not Non...  172 us
    pallas_call x1, Pallas kernels, forward(): pl.pallas_call(forward_kernel, grid=(4 * per + 1,), in_specs=[pl.BlockSpe...  51.5 us
    pallas_call x1, Pallas kernels, chain(): pl.pallas_call(chain_kernel, grid=(2 * per,), in_specs=[whole, whole, wid...  21.3 us
    dot_general x5, matrix products, dot_nt(): return lax.dot_general(a, b, LAST_CONTRACT, preferred_element_type=F32)  20.8 us
    dot_general x3, matrix products, dot_tn(): return lax.dot_general(a, b, ROWS_CONTRACT, preferred_element_type=F32)  17.3 us
    dot_general x3, matrix products, dot(): return jnp.dot(a, b, preferred_element_type=F32)  14.3 us
  transfers between devices with their start and end apart: 9, of which 0 were waited for; matrix products, arithmetic and copies ran while one was open for 18% of the time, Pallas kernels for 50%

profile of v4, /device:TPU:0, one launch (start us, length us, event | category | flops | bytes accessed | tf_op | source)
XLA Modules:
  0.0 329.0 jit_solution(5910064260887447147)
XLA Ops:
  7.2 0.0 copy-start
  7.2 0.0 all-gather.11.cloned.1.call-start
  7.2 1.9 pad_maximum_fusion.1.x_ref
  9.2 51.5 %forward.1 = (bf16[192,1024]{1,0:T(8,128)(2,1)}, bf16[16,128,1024]{2,1,0:T(8,128)(2,1)}, bf16[16,64,1024]{2,1,0:T(8,128)(2,1)}) custom-call(bf16[192,1024]{1,0:T(8,128)(2,1)} %pad_maximum_fusion.1.x_ref, bf16[2,1024,4096]{2,1,0:T(8,128)(2,1)} %w1_ref.7, bf16[2,4096,1024]{2,1,0:T(8,128)(2,1)} %w2_ref.7, bf16[2,1024,4096]{2,1,0:T(8,128)(2,1)} %w1_ref.9, ...), custom_call_target="tpu_custom_call" | custom-call | flops 6442450944 | bytes 75497472 | tf_op jit(solution)/shard_map/forward/pallas_call | solution.py:208
  60.7 0.0 all-gather.11.cloned.1.call-update
  60.7 0.0 all-gather.7.cloned.1.call-start
  60.8 0.7 all-gather.7.cloned.1.call-update
  61.5 0.0 all-gather.9.cloned.1.call-start
  62.2 4.7 %convolution_convert_fusion.5 = bf16[1024,1024]{1,0:T(8,128)(2,1)S(1)} fusion(bf16[1024,1024]{1,0:T(8,128)(2,1)} %bitcast.40, bf16[1024,1024]{1,0:T(8,128)(2,1)} %param.14), kind=kOutput, calls=%fused_computation.10 | convolution fusion | flops 2148532224 | bytes 6291456 | tf_op jit(solution)/shard_map/dot_general | solution.py:20
  66.9 4.9 %convolution_convert_fusion.2 = bf16[2048,1024]{1,0:T(8,128)(2,1)S(1)} fusion(bf16[2048,1024]{1,0:T(8,128)(2,1)S(1)} %bitcast.38, bf16[1024,1024]{1,0:T(8,128)(2,1)S(1)} %copy-done), kind=kOutput, calls=%fused_computation.7 | convolution fusion | flops 4297064448 | bytes 10485760 | tf_op jit(solution)/shard_map/dot_general | solution.py:20
  71.8 4.6 %fusion.15 = (f32[1024]{0:T(1024)S(1)}, f32[1024,2048]{1,0:T(8,128)S(1)}) fusion(f32[]{:T(128)S(6)} %copy.40, bf16[1024,1024]{1,0:T(8,128)(2,1)S(1)} %convolution_convert_fusion.5, bf16[2048,1024]{1,0:T(8,128)(2,1)S(1)} %convolution_convert_fusion.2), kind=kOutput, calls=%fused_computation.35 | convolution fusion | flops 4299160576 | bytes 14684164 | tf_op jit(solution)/shard_map/dot_general | solution.py:24
  76.5 3.2 select_reduce_fusion
  79.7 0.6 subtract_reduce_fusion
  80.3 2.8 divide_convert_fusion
  83.1 0.0 copy-start.2
  83.1 4.7 %convolution_convert_fusion.4 = bf16[1024,1024]{1,0:T(8,128)(2,1)S(1)} fusion(bf16[1024,2048]{1,0:T(8,128)(2,1)S(1)} %divide_convert_fusion, bf16[2048,1024]{1,0:T(8,128)(2,1)S(1)} %convolution_convert_fusion.2), kind=kOutput, calls=%fused_computation.9 | convolution fusion | flops 4296015872 | bytes 10485760 | tf_op jit(solution)/shard_map/dot_general | solution.py:20
  87.9 1.3 copy-done.5
  89.2 0.8 fusion.2
  90.0 5.1 %convolution_convert_fusion.1 = bf16[2048,1024]{1,0:T(8,128)(2,1)S(1)} fusion(bf16[1024,2048]{1,0:T(8,128)(2,1)S(1)} %divide_convert_fusion, bf16[1024,1024]{1,0:T(8,128)(2,1)S(1)} %convolution_convert_fusion.5), kind=kOutput, calls=%fused_computation.6 | convolution fusion | flops 4297064448 | bytes 10485760 | tf_op jit(solution)/shard_map/dot_general | solution.py:28
  95.1 0.0 copy-start.3
  95.1 2.0 copy-done.3
  97.1 0.8 fusion
  97.9 0.9 pad_maximum_fusion.e_ref
  98.9 21.3 %chain.1 = bf16[192,1024]{1,0:T(8,128)(2,1)} custom-call(bf16[192,1024]{1,0:T(8,128)(2,1)} %get-tuple-element.35.h_ref, f32[192,1024]{1,0:T(8,128)} %pad_maximum_fusion.e_ref, bf16[2,1024,4096]{2,1,0:T(8,128)(2,1)} %w1_ref.7, bf16[2,4096,1024]{2,1,0:T(8,128)(2,1)} %w2_ref.7, bf16[2,1024,4096]{2,1,0:T(8,128)(2,1)} %w1_ref.9, bf16[2,4096,1024]{2,1,0:T(8,128)(2,1)} %w2_ref.9), custom_call_target="tpu_custom_call" | custom-call | flops 3221225472 | bytes 37748736 | tf_op jit(solution)/shard_map/chain/pallas_call | solution.py:267
  120.2 0.0 all-gather.9.cloned.1.call-update
  120.2 5.9 %convolution_convert_fusion.3 = bf16[1024,1024]{1,0:T(8,128)(2,1)} fusion(bf16[1024,1024]{1,0:T(8,128)(2,1)} %copy-done.5, bf16[1024,1024]{1,0:T(8,128)(2,1)} %param.14), kind=kOutput, calls=%fused_computation.8 | convolution fusion | flops 2148532224 | bytes 6291456 | tf_op jit(solution)/shard_map/dot_general | solution.py:24
  126.1 25.3 %layer_grads.6 = (f32[2,1024,4096]{2,1,0:T(8,128)}, f32[2,4096,1024]{2,1,0:T(8,128)}, f32[1,1024,2048]{2,1,0:T(8,128)}, f32[1,2048,1024]{2,1,0:T(8,128)}) custom-call(s32[1]{0:T(128)} %bitcast.3.core_ref, bf16[16,192,1024]{2,1,0:T(8,128)(2,1)} %bitcast.36, bf16[16,64,1024]{2,1,0:T(8,128)(2,1)} %bitcast.43, bf16[2,1024,4096]{2,1,0:T(8,128)(2,1)} %w1_ref.9, ...), custom_call_target="tpu_custom_call" | custom-call | flops 17179869184 | bytes 41943040 | tf_op jit(solution)/shard_map/layer_grads/pallas_call | solution.py:353
  151.4 0.3 collective-permute-start
  151.7 0.2 collective-permute-start.1
  151.9 8.7 %convolution_convert_fusion = bf16[2048,1024]{1,0:T(8,128)(2,1)} fusion(bf16[2048,1024]{1,0:T(8,128)(2,1)} %copy-done.3, bf16[1024,1024]{1,0:T(8,128)(2,1)S(1)} %copy-done), kind=kOutput, calls=%fused_computation.5 | convolution fusion | flops 4297064448 | bytes 10485760 | tf_op jit(solution)/shard_map/dot_general | solution.py:24
  160.6 43.8 %layer_grads.5 = (f32[2,1024,4096]{2,1,0:T(8,128)}, f32[2,4096,1024]{2,1,0:T(8,128)}, f32[1,1024,2048]{2,1,0:T(8,128)}, f32[1,2048,1024]{2,1,0:T(8,128)}) custom-call(s32[1]{0:T(128)} %bitcast.3.core_ref, bf16[16,192,1024]{2,1,0:T(8,128)(2,1)} %bitcast.37, bf16[16,128,1024]{2,1,0:T(8,128)(2,1)} %bitcast.42, bf16[2,1024,4096]{2,1,0:T(8,128)(2,1)} %w1_ref.7, ...), custom_call_target="tpu_custom_call" | custom-call | flops 34359738368 | bytes 41943040 | tf_op jit(solution)/shard_map/layer_grads/pallas_call | solution.py:353
  204.4 0.3 collective-permute-start.2
  204.7 0.2 collective-permute-start.3
  204.9 0.0 collective-permute-done.rest_2_
  204.9 0.0 collective-permute-done.1.rest_3_
  204.9 47.6 %layer_grads.7 = (f32[2,1024,4096]{2,1,0:T(8,128)}, f32[2,4096,1024]{2,1,0:T(8,128)}, f32[1,1024,2048]{2,1,0:T(8,128)}, f32[1,2048,1024]{2,1,0:T(8,128)}, f32[2,...) custom-call(s32[1]{0:T(128)} %bitcast.3.core_ref, ...), custom_call_target="tpu_custom_call", output_to_operand_aliasing={{0}: (5, {}), {1}: (6, {}), {4}: (9, {}), {5}: (10, {})} | custom-call | flops 34359738368 | bytes 41943040 | tf_op jit(solution)/shard_map/layer_grads/pallas_call | solution.py:353
  252.5 0.3 collective-permute-start.4
  252.8 0.2 collective-permute-start.5
  253.7 0.0 copy-start.4
  253.7 6.1 %fusion.16 = f32[1024,1024]{1,0:T(8,128)} fusion(bf16[1024,1024]{1,0:T(8,128)(2,1)} %bitcast.41, bf16[1024,1024]{1,0:T(8,128)(2,1)S(1)} %copy-done.6), kind=kOutput, calls=%fused_computation.36 | convolution fusion | flops 2147483648 | bytes 8388608 | tf_op jit(solution)/shard_map/dot_general | solution.py:28
  259.9 6.1 %fusion.17 = f32[1024,1024]{1,0:T(8,128)} fusion(bf16[2048,1024]{1,0:T(8,128)(2,1)S(1)} %bitcast.39, bf16[2048,1024]{1,0:T(8,128)(2,1)S(1)} %copy-done.4), kind=kOutput, calls=%fused_computation.37 | convolution fusion | flops 4294967296 | bytes 12582912 | tf_op jit(solution)/shard_map/dot_general | solution.py:28
  265.9 0.0 collective-permute-done.2.rest_2_
  265.9 0.0 collective-permute-done.3.rest_3_
  265.9 27.6 %layer_grads.8 = (f32[2,1024,4096]{2,1,0:T(8,128)}, f32[2,4096,1024]{2,1,0:T(8,128)}, f32[2,1024,4096]{2,1,0:T(8,128)}, f32[2,4096,1024]{2,1,0:T(8,128)}) custom-call(s32[1]{0:T(128)} %bitcast.3.core_ref, bf16[16,192,1024]{2,1,0:T(8,128)(2,1)} %bitcast.30, ...), custom_call_target="tpu_custom_call", output_to_operand_aliasing={{0}: (5, {}), {1}: (6, {}), {2}: (9, {}), {3}: (10, {})} | custom-call | flops 17179869184 | bytes 41943040 | tf_op jit(solution)/shard_map/layer_grads/pallas_call | solution.py:353
  293.6 0.0 collective-permute-done.4.rest_2_
  293.6 0.0 collective-permute-done.5.rest_3_
  293.6 0.0 copy-start.1
  293.6 27.5 %layer_grads.9 = (f32[2,1024,4096]{2,1,0:T(8,128)}, f32[2,4096,1024]{2,1,0:T(8,128)}, f32[2,1024,4096]{2,1,0:T(8,128)}, f32[2,4096,1024]{2,1,0:T(8,128)}) custom-call(s32[1]{0:T(128)} %bitcast.3.core_ref, bf16[16,192,1024]{2,1,0:T(8,128)(2,1)} %bitcast.31, ...), custom_call_target="tpu_custom_call", output_to_operand_aliasing={{0}: (5, {}), {1}: (6, {}), {2}: (9, {}), {3}: (10, {})} | custom-call | flops 17179869184 | bytes 41943040 | tf_op jit(solution)/shard_map/layer_grads/pallas_call | solution.py:353
  (16 shorter events, 0.0 us)
Async XLA Ops:
  7.2 59.8 %copy-start = (bf16[1024,1024]{1,0:T(8,128)(2,1)S(1)}, bf16[1024,1024]{1,0:T(8,128)(2,1)}, u32[]{:S(2)}) copy-start(bf16[1024,1024]{1,0:T(8,128)(2,1)} %param.17) | copy-start | bytes 6291460
  7.2 118.9 %all-gather.11.cloned.1.call-start = ((), (), s32[]{:S(2)}) async-start(), calls=%async_computation.2 | async-start | bytes 6684672 | tf_op jit(solution)/shard_map/all_gather | solution.py:368
  60.7 144.2 %all-gather.7.cloned.1.call-start = ((), (), s32[]{:S(2)}) async-start(), calls=%async_computation | async-start | bytes 6684672 | tf_op jit(solution)/shard_map/all_gather | solution.py:368
  61.5 143.4 %all-gather.9.cloned.1.call-start = ((), (), s32[]{:S(2)}) async-start(), calls=%async_computation.1 | async-start | bytes 6684672 | tf_op jit(solution)/shard_map/all_gather | solution.py:368
  62.2 4.7 %copy-start.7 = (bf16[16,128,1024]{2,1,0:T(8,128)(2,1)S(1)}, bf16[16,128,1024]{2,1,0:T(8,128)(2,1)}, u32[]{:S(2)}) copy-start(bf16[16,128,1024]{2,1,0:T(8,128)(2,1)} %get-tuple-element.34) | copy-start | bytes 12582916
  83.1 6.1 %copy-start.2 = (bf16[1024,1024]{1,0:T(8,128)(2,1)S(1)}, bf16[1024,1024]{1,0:T(8,128)(2,1)}, u32[]{:S(2)}) copy-start(bf16[1024,1024]{1,0:T(8,128)(2,1)} %param.14) | copy-start | bytes 6291460
  87.9 1.3 copy-start.5
  95.1 2.0 copy-start.3
  151.4 53.5 %collective-permute-start = (f32[1,1024,2048]{2,1,0:T(8,128)}, f32[1,1024,2048]{2,1,0:T(8,128)}, u32[]{:S(2)}, u32[]{:S(2)}) collective-permute-start(f32[1,1024,2048]{2,1,0:T(8,128)} %get-tuple-element.39), channel_id=1, source_target_pairs={{0,1},{1,0},{2,3},{3,2},{4,5},{5,4},{6,7},{7,6},{8,9},{9,8},{10,11... | collective-permute-start | bytes 25165832 | tf_op jit(solution)/shard_map/ppermute | solution.py:408
  151.7 53.2 %collective-permute-start.1 = (f32[1,2048,1024]{2,1,0:T(8,128)}, f32[1,2048,1024]{2,1,0:T(8,128)}, u32[]{:S(2)}, u32[]{:S(2)}) collective-permute-start(f32[1,2048,1024]{2,1,0:T(8,128)} %get-tuple-element.40), channel_id=1, source_target_pairs={{0,1},{1,0},{2,3},{3,2},{4,5},{5,4},{6,7},{7,6},{8,9},{9,8},{10,11... | collective-permute-start | bytes 25165832 | tf_op jit(solution)/shard_map/ppermute | solution.py:408
  204.4 61.5 %collective-permute-start.2 = (f32[1,1024,2048]{2,1,0:T(8,128)}, f32[1,1024,2048]{2,1,0:T(8,128)}, u32[]{:S(2)}, u32[]{:S(2)}) collective-permute-start(f32[1,1024,2048]{2,1,0:T(8,128)} %get-tuple-element.45), channel_id=1, source_target_pairs={{0,1},{1,0},{2,3},{3,2},{4,5},{5,4},{6,7},{7,6},{8,9},{9,8},{10,11... | collective-permute-start | bytes 25165832 | tf_op jit(solution)/shard_map/ppermute | solution.py:408
  204.7 61.3 %collective-permute-start.3 = (f32[1,2048,1024]{2,1,0:T(8,128)}, f32[1,2048,1024]{2,1,0:T(8,128)}, u32[]{:S(2)}, u32[]{:S(2)}) collective-permute-start(f32[1,2048,1024]{2,1,0:T(8,128)} %get-tuple-element.46), channel_id=1, source_target_pairs={{0,1},{1,0},{2,3},{3,2},{4,5},{5,4},{6,7},{7,6},{8,9},{9,8},{10,11... | collective-permute-start | bytes 25165832 | tf_op jit(solution)/shard_map/ppermute | solution.py:408
  204.9 48.8 %copy-start.6 = (bf16[1024,1024]{1,0:T(8,128)(2,1)S(1)}, bf16[1024,1024]{1,0:T(8,128)(2,1)}, u32[]{:S(2)}) copy-start(bf16[1024,1024]{1,0:T(8,128)(2,1)} %copy-done.5) | copy-start | bytes 6291460
  252.5 41.1 %collective-permute-start.4 = (f32[1,1024,2048]{2,1,0:T(8,128)}, f32[1,1024,2048]{2,1,0:T(8,128)}, u32[]{:S(2)}, u32[]{:S(2)}) collective-permute-start(f32[1,1024,2048]{2,1,0:T(8,128)} %get-tuple-element.51), channel_id=1, source_target_pairs={{0,1},{1,0},{2,3},{3,2},{4,5},{5,4},{6,7},{7,6},{8,9},{9,8},{10,11... | collective-permute-start | bytes 25165832 | tf_op jit(solution)/shard_map/ppermute | solution.py:408
  252.8 40.8 %collective-permute-start.5 = (f32[1,2048,1024]{2,1,0:T(8,128)}, f32[1,2048,1024]{2,1,0:T(8,128)}, u32[]{:S(2)}, u32[]{:S(2)}) collective-permute-start(f32[1,2048,1024]{2,1,0:T(8,128)} %get-tuple-element.52), channel_id=1, source_target_pairs={{0,1},{1,0},{2,3},{3,2},{4,5},{5,4},{6,7},{7,6},{8,9},{9,8},{10,11... | collective-permute-start | bytes 25165832 | tf_op jit(solution)/shard_map/ppermute | solution.py:408
  253.7 6.2 %copy-start.4 = (bf16[2048,1024]{1,0:T(8,128)(2,1)S(1)}, bf16[2048,1024]{1,0:T(8,128)(2,1)}, u32[]{:S(2)}) copy-start(bf16[2048,1024]{1,0:T(8,128)(2,1)} %copy-done.3) | copy-start | bytes 12582916
  253.7 6.2 %copy-start.8 = (bf16[16,128,1024]{2,1,0:T(8,128)(2,1)S(1)}, bf16[16,128,1024]{2,1,0:T(8,128)(2,1)}, u32[]{:S(2)}) copy-start(bf16[16,128,1024]{2,1,0:T(8,128)(2,1)} %get-tuple-element.34) | copy-start | bytes 12582916
  293.6 27.6 %copy-start.1 = (bf16[1024,1024]{1,0:T(8,128)(2,1)S(1)}, bf16[1024,1024]{1,0:T(8,128)(2,1)}, u32[]{:S(2)}) copy-start(bf16[1024,1024]{1,0:T(8,128)(2,1)} %param.17) | copy-start | bytes 6291460
Sparse Core Ops, SparseCore 0:
  60.9 41.3 all-gather.10
  104.5 41.7 all-gather.6
  148.5 41.7 all-gather.8

commit v5 on v4

--- a/solution.py
+++ b/solution.py
@@ -41,6 +41,7 @@
 
 
 BLOCK = 1024
+RING = 4
 THIRDS = ((0, 384), (384, 384), (768, 256))
 ORDERS = ((2, 4, 8), (4, 8, 2), (8, 2, 4))
 
@@ -49,10 +50,11 @@
     return device + bit * (1 - 2 * (lax.div(device, bit) % 2))
 
 
-def forward_kernel(x_ref, dw1_ref, dw2_ref, qw1_ref, qw2_ref, h1_ref, d_all, q_all, acc_ref, h_ref, h2_ref,
-                   send_sem, recv_sem, pair_send, pair_recv, own_sem, own_send, own_recv):
+def forward_kernel(xd_ref, xq_ref, dw1_ref, dw2_ref, qw1_ref, qw2_ref, h1_ref, d_all, q_all, acc_ref, h_ref, h2_ref,
+                   w1_buf, w2_buf, w1_sem, w2_sem, send_sem, recv_sem, pair_send, pair_recv, own_sem, own_send, own_recv):
     s = pl.program_id(0)
-    per = pl.num_programs(0) // 4
+    per = dw1_ref.shape[2] // BLOCK
+    slot = s % RING
     me = lax.axis_index('data')
     partner = flip(me, 1)
     d_rows = d_all.shape[1]
@@ -109,17 +111,38 @@
                     hop(t, p, mask, step).start()
                 relay(t, p, mask).start()
 
-    def layers(first, rows, w1_ref, w2_ref):
+    def blocks(step, w1_ref, w2_ref):
+        layer = (step // per) % 2
+        cols = pl.ds((step % per) * BLOCK, BLOCK)
+        at = step % RING
+        return (pltpu.make_async_copy(w1_ref.at[layer, :, cols], w1_buf.at[at], w1_sem.at[at]),
+                pltpu.make_async_copy(w2_ref.at[layer, cols, :], w2_buf.at[at], w2_sem.at[at]))
+
+    def fetch(step):
+        @pl.when(step < 2 * per)
+        def _():
+            for copy in blocks(step, dw1_ref, dw2_ref):
+                copy.start()
+
+        @pl.when((step >= 2 * per) & (step < 4 * per))
+        def _():
+            for copy in blocks(step, qw1_ref, qw2_ref):
+                copy.start()
+
+    def layers(first, rows, x_ref, w1_ref, w2_ref):
+        for copy in blocks(s, w1_ref, w2_ref):
+            copy.wait()
+
         @pl.when(s == first)
         def _():
-            h_ref[rows, :] = x_ref[rows, :]
+            h_ref[rows, :] = x_ref[...]
 
         @pl.when((s - first) % per == 0)
         def _():
             acc_ref[rows, :] = h_ref[rows, :].astype(F32)
 
-        pre = dot(h_ref[rows, :], w1_ref[0])
-        acc_ref[rows, :] += dot((pre * gelu_cdf(pre)[1]).astype(BF16), w2_ref[0])
+        pre = dot(h_ref[rows, :], w1_buf[slot])
+        acc_ref[rows, :] += dot((pre * gelu_cdf(pre)[1]).astype(BF16), w2_buf[slot])
 
         @pl.when(s == first + per - 1)
         def _():
@@ -133,11 +156,16 @@
 
     @pl.when(s == 0)
     def _():
+        for step in range(RING - 1):
+            for copy in blocks(step, dw1_ref, dw2_ref):
+                copy.start()
         barrier = pltpu.get_barrier_semaphore()
         for bit in (1, 2, 4, 8):
             pl.semaphore_signal(barrier, inc=1, device_id=(flip(me, bit),), device_id_type=pl.DeviceIdType.MESH)
         pl.semaphore_wait(barrier, 4)
 
+    fetch(s + RING - 1)
+
     @pl.when(s == 2 * per)
     def _():
         begin(0)
@@ -156,11 +184,11 @@
 
     @pl.when(s < 2 * per)
     def _():
-        layers(0, towers[0][0], dw1_ref, dw2_ref)
+        layers(0, towers[0][0], xd_ref, dw1_ref, dw2_ref)
 
     @pl.when((s >= 2 * per) & (s < 4 * per))
     def _():
-        layers(2 * per, towers[1][0], qw1_ref, qw2_ref)
+        layers(2 * per, towers[1][0], xq_ref, qw1_ref, qw2_ref)
 
     @pl.when(s == 4 * per)
     def _():
@@ -178,106 +206,76 @@
             own_pair(t).wait()
 
 
-def forward(own0, d_w1, d_w2, q_w1, q_w2):
-    rows, width = own0.shape
+def forward(d_own, q_own, d_w1, d_w2, q_w1, q_w2):
+    third, width = q_own.shape
+    rows = 3 * third
     per = d_w1.shape[2] // BLOCK
 
-    def place(s):
-        f = s // (2 * per)
-        return f - f // 2, f // 2, (s // per) % 2, s % per
-
-    def at_d(s):
-        f, _, layer, j = place(s)
-        f = s // (2 * per)
-        f = f - f // 2
-        return layer * (1 - f) + f, j * (1 - f) + (per - 1) * f
-
-    def at_q(s):
-        f, end, layer, j = place(s)
-        live = f - end
-        return layer * live + end, j * live + (per - 1) * end
-
-    def wide(at):
-        return pl.BlockSpec((1, width, BLOCK), lambda s: (at(s)[0], 0, at(s)[1]))
-
-    def tall(at):
-        return pl.BlockSpec((1, BLOCK, width), lambda s: (at(s)[0], at(s)[1], 0))
-
-    third = rows // 3
+    anywhere = pl.BlockSpec(memory_space=pl.ANY)
     sems = pltpu.SemaphoreType.DMA
     return pl.pallas_call(
         forward_kernel,
         grid=(4 * per + 1,),
-        in_specs=[pl.BlockSpec((rows, width), lambda s: (0, 0)), wide(at_d), tall(at_d), wide(at_q), tall(at_q)],
-        out_specs=[pl.BlockSpec((rows, width), lambda s: (0, 0))] + [pl.BlockSpec(memory_space=pl.ANY)] * 2,
+        in_specs=[pl.BlockSpec((2 * third, width), lambda s: (0, 0)), pl.BlockSpec((third, width), lambda s: (0, 0)),
+                  *[anywhere] * 4],
+        out_specs=[pl.BlockSpec((rows, width), lambda s: (0, 0))] + [anywhere] * 2,
         out_shape=[jax.ShapeDtypeStruct((rows, width), BF16), jax.ShapeDtypeStruct((16, 2 * third, width), BF16),
                    jax.ShapeDtypeStruct((16, third, width), BF16)],
         scratch_shapes=[pltpu.VMEM((rows, width), F32), pltpu.VMEM((rows, width), BF16), pltpu.VMEM((rows, width), BF16),
+                        pltpu.VMEM((RING, width, BLOCK), BF16), pltpu.VMEM((RING, BLOCK, width), BF16), sems((RING,)), sems((RING,)),
                         sems((2, 3, 8)), sems((2, 3, 8)), sems((2, 3, 8)), sems((2, 3, 8)), sems((2,)), sems((2,)), sems((2,))],
         compiler_params=pltpu.CompilerParams(collective_id=0, has_side_effects=True, dimension_semantics=('arbitrary',)),
         cost_estimate=pl.CostEstimate(flops=8 * rows * width * d_w1.shape[2], bytes_accessed=72 * MIB, transcendentals=0),
         name='forward',
-    )(own0, d_w1, d_w2, q_w1, q_w2)
-
-
-def chain_kernel(h_ref, e_ref, dw1_ref, dw2_ref, qw1_ref, qw2_ref, out_ref, acc_ref):
+    )(d_own, q_own, d_w1, d_w2, q_w1, q_w2)
+
+
+def chain_kernel(h_ref, de_ref, qe_ref, dw1_ref, dw2_ref, qw1_ref, qw2_ref, out_ref, acc_ref):
     s = pl.program_id(0)
-    per = pl.num_programs(0) // 2
     third = h_ref.shape[0] // 3
-
-    def block(rows, w1_ref, w2_ref):
-        pre = dot(h_ref[rows, :], w1_ref[0])
-        t = dot_nt(e_ref[rows, :].astype(BF16), w2_ref[0])
-        acc_ref[rows, :] += dot_nt(gelu_and_back(pre, t)[1], w1_ref[0])
+    parts = ((pl.ds(0, 2 * third), de_ref, dw1_ref, dw2_ref), (pl.ds(2 * third, third), qe_ref, qw1_ref, qw2_ref))
 
     @pl.when(s == 0)
     def _():
-        acc_ref[...] = e_ref[...]
-
-    @pl.when(s < per)
-    def _():
-        block(pl.ds(0, 2 * third), dw1_ref, dw2_ref)
-
-    @pl.when(s >= per)
-    def _():
-        block(pl.ds(2 * third, third), qw1_ref, qw2_ref)
-
-    @pl.when(s == 2 * per - 1)
+        for rows, e_ref, _, _ in parts:
+            acc_ref[rows, :] = e_ref[...]
+
+    pre = [dot(h_ref[rows, :], w1_ref[0]) for rows, _, w1_ref, _ in parts]
+    t = [dot_nt(e_ref[...].astype(BF16), w2_ref[0]) for _, e_ref, _, w2_ref in parts]
+    delta = [gelu_and_back(*pair)[1] for pair in zip(pre, t)]
+    for (rows, _, w1_ref, _), d in zip(parts, delta):
+        acc_ref[rows, :] += dot_nt(d, w1_ref[0])
+
+    @pl.when(s == pl.num_programs(0) - 1)
     def _():
         out_ref[...] = acc_ref[...].astype(BF16)
 
 
-def chain(h1_own, e1_own, d_w1, d_w2, q_w1, q_w2):
+def chain(h1_own, d_e1, q_e1, d_w1, d_w2, q_w1, q_w2):
     rows, width = h1_own.shape
-    per = d_w1.shape[2] // BLOCK
-
-    def at_d(s):
-        return (s % per) * (1 - s // per) + (per - 1) * (s // per)
-
-    def at_q(s):
-        return (s % per) * (s // per)
-
-    def wide(at):
-        return pl.BlockSpec((1, width, BLOCK), lambda s: (1, 0, at(s)))
-
-    def tall(at):
-        return pl.BlockSpec((1, BLOCK, width), lambda s: (1, at(s), 0))
-
-    whole = pl.BlockSpec((rows, width), lambda s: (0, 0))
+    block = 512
+    wide = pl.BlockSpec((1, width, block), lambda s: (1, 0, s))
+    tall = pl.BlockSpec((1, block, width), lambda s: (1, s, 0))
+
+    def whole(x):
+        return pl.BlockSpec(x.shape, lambda s: (0, 0))
+
     return pl.pallas_call(
         chain_kernel,
-        grid=(2 * per,),
-        in_specs=[whole, whole, wide(at_d), tall(at_d), wide(at_q), tall(at_q)],
-        out_specs=whole,
+        grid=(d_w1.shape[2] // block,),
+        in_specs=[whole(h1_own), whole(d_e1), whole(q_e1), wide, tall, wide, tall],
+        out_specs=whole(h1_own),
         out_shape=jax.ShapeDtypeStruct((rows, width), BF16),
         scratch_shapes=[pltpu.VMEM((rows, width), F32)],
         compiler_params=pltpu.CompilerParams(dimension_semantics=('arbitrary',)),
         cost_estimate=pl.CostEstimate(flops=4 * rows * width * d_w1.shape[2], bytes_accessed=36 * MIB, transcendentals=0),
         name='chain',
-    )(h1_own, e1_own, d_w1, d_w2, q_w1, q_w2)
-
-
-def layer_kernel(row_tile, in_place, incoming, send, core_ref, h_ref, e_ref, w1_ref, w2_ref, *rest):
+    )(h1_own, d_e1, q_e1, d_w1, d_w2, q_w1, q_w2)
+
+
+def layer_kernel(row_tile, in_place, incoming, send, top, core_ref, h_ref, e_ref, w1_ref, w2_ref, *rest):
+    if top:
+        up_ref, (proj_ref, last_ref), e_ref, rest = e_ref, rest[:2], rest[-1], rest[2:-1]
     u_ref, delta_ref = rest[-2:]
     rest = rest[2 if in_place else 0:-2]
     if incoming:
@@ -289,6 +287,16 @@
     n, r, width = h_ref.shape
     h = h_ref.reshape(n * r, width)
     e = e_ref.reshape(n * r, width)
+    if top:
+        up = up_ref.reshape(n * r, width)
+
+        @pl.when(pl.program_id(0) == 0)
+        def _():
+            for i in range(n * r // row_tile):
+                rows = pl.ds(i * row_tile, row_tile)
+                e_ref[rows, :] = dot_nt(up[rows, :], proj_ref[...]).astype(BF16)
+
+        rest[4][...] = dot_tn(last_ref.reshape(n * r, last_ref.shape[2])[...], up[...])
     w1_t = w1_ref[0].T
     for i in range(n * r // row_tile):
         rows = pl.ds(i * row_tile, row_tile)
@@ -306,7 +314,7 @@
             rest[2][0, cols, :] = one
 
 
-def layer_grads(core, layer, first, h_all, h_place, e_all, e_place, rows, w1, w2, grads=None, incoming=None):
+def layer_grads(core, layer, first, h_all, h_place, e_all, e_place, rows, w1, w2, grads=None, incoming=None, top=None):
     _, width, ffn_width = w1.shape
     n = h_all.shape[0]
     block, row_tile, steps = 512, 512, 4
@@ -336,6 +344,12 @@
     out_shape = [jax.ShapeDtypeStruct(w1.shape, F32), jax.ShapeDtypeStruct(w2.shape, F32)]
     aliases = {}
     anywhere = [pl.BlockSpec(memory_space=pl.ANY)] * 2
+    scratch = [pltpu.VMEM((block, total), BF16)] * 2
+    if top is not None:
+        in_specs += [pl.BlockSpec((width, width), lambda j, c: (0, 0), pipeline_mode=resident),
+                     pl.BlockSpec((n, rows, width // steps), lambda j, c: (0, 0, j))]
+        args += list(top)
+        scratch.append(pltpu.VMEM((total, width), BF16))
     if grads is not None:
         aliases.update({len(args): 0, len(args) + 1: 1})
         in_specs += anywhere
@@ -343,6 +357,9 @@
     if send:
         out_specs += [wide(0, lambda j, c: j), tall(0, lambda j, c: j)]
         out_shape += [jax.ShapeDtypeStruct((1, width, ffn_width // 2), F32), jax.ShapeDtypeStruct((1, ffn_width // 2, width), F32)]
+    if top is not None:
+        out_specs.append(pl.BlockSpec((width // steps, width), lambda j, c: (j, 0)))
+        out_shape.append(jax.ShapeDtypeStruct((width, width), F32))
     if incoming is not None:
         at, halves, targets = incoming
         in_specs += [wide(0, lambda j, c: j), tall(0, lambda j, c: j)] + anywhere
@@ -351,10 +368,10 @@
         out_specs += [wide(at, other), tall(at, other)]
         out_shape += [jax.ShapeDtypeStruct(t.shape, F32) for t in targets]
     out = pl.pallas_call(
-        functools.partial(layer_kernel, row_tile, grads is not None, incoming is not None, send),
+        functools.partial(layer_kernel, row_tile, grads is not None, incoming is not None, send, top is not None),
         grid_spec=pltpu.PrefetchScalarGridSpec(
             num_scalar_prefetch=1, grid=(steps,), in_specs=in_specs, out_specs=out_specs,
-            scratch_shapes=[pltpu.VMEM((block, total), BF16)] * 2),
+            scratch_shapes=scratch),
         out_shape=out_shape,
         input_output_aliases=aliases,
         compiler_params=pltpu.CompilerParams(vmem_limit_bytes=58 * MIB, dimension_semantics=('arbitrary',)),
@@ -371,12 +388,13 @@
 def local_step(q_loc, d_loc, temperature, q_w1, q_w2, q_proj, d_w1, d_w2, d_proj):
     rows, width = q_loc.shape
     me = lax.axis_index('data')
-    own0 = jnp.concatenate([d_loc.reshape(2 * rows, width), q_loc], axis=0)
-    h1_own, d_last, q_last = forward(own0, d_w1, d_w2, q_w1, q_w2)
+    d_own = d_loc.reshape(2 * rows, width)
+    h1_own, d_last, q_last = forward(d_own, q_loc, d_w1, d_w2, q_w1, q_w2)
     d_last = d_last.reshape(-1, width)
     q_last = q_last.reshape(-1, width)
     h1_all = gather(h1_own)
-    h0_all = gather(lax.optimization_barrier((own0, h1_own))[0])
+    d_own, q_own, _ = lax.optimization_barrier((d_own, q_loc, h1_own))
+    h0_all = gather(jnp.concatenate([d_own, q_own], axis=0))
     docs = dot(d_last, d_proj).astype(BF16)
     queries = dot(q_last, q_proj).astype(BF16)
     batch = queries.shape[0]
@@ -393,23 +411,19 @@
 
     def start(up, proj):
         own = up.shape[0] // 16
-        e1_own = dot_nt(lax.dynamic_slice_in_dim(up, me * own, own, 0), proj)
-        return dot_nt(up, proj).astype(BF16).reshape(16, own, width), e1_own
-
-    d_e1, d_e1_own = start(d_up, d_proj)
-    q_e1, q_e1_own = start(q_up, q_proj)
-    e1_own = jnp.concatenate([d_e1_own, q_e1_own], axis=0)
-    e0_all = gather(chain(h1_own, e1_own, d_w1, d_w2, q_w1, q_w2))
-    d_p = dot_tn(d_last, d_up)
-    q_p = dot_tn(q_last, q_up)
+        return dot_nt(lax.dynamic_slice_in_dim(up, me * own, own, 0), proj)
+
+    e0_all = gather(chain(h1_own, start(d_up, d_proj), start(q_up, q_proj), d_w1, d_w2, q_w1, q_w2))
+    d_up, d_last = [x.reshape(16, 2 * rows, width) for x in (d_up, d_last)]
+    q_up, q_last = [x.reshape(16, rows, width) for x in (q_up, q_last)]
     core = (me % 2).reshape(1)
 
     def swap(halves):
         return [lax.ppermute(x, 'data', [(i, i ^ 1) for i in range(16)]) for x in halves]
 
-    q_g, q1 = layer_grads(core, 1, None, h1_all, 2, q_e1, 0, rows, q_w1, q_w2)
+    q_g, q1, (q_p,) = layer_grads(core, 1, None, h1_all, 2, q_up, 0, rows, q_w1, q_w2, top=(q_proj, q_last))
     q1 = swap(q1)
-    d_g, d1 = layer_grads(core, 1, None, h1_all, 0, d_e1, 0, 2 * rows, d_w1, d_w2)
+    d_g, d1, (d_p,) = layer_grads(core, 1, None, h1_all, 0, d_up, 0, 2 * rows, d_w1, d_w2, top=(d_proj, d_last))
     d1 = swap(d1)
     d_g, d0, q_g = layer_grads(core, 0, None, h0_all, 0, e0_all, 0, 2 * rows, d_w1, d_w2, d_g, (1, q1, q_g))
     d0 = swap(d0)

time: 333 us -> 312 us (0.937)
  matrix products: 52.5 us -> 26.9 us
  Pallas kernels: 245 us -> 252 us
    pallas_call x5, Pallas kernels: 172 us -> 188 us  [layer_grads(): pl.pallas_call(functools.partial(layer_kernel, row_tile, grads is not Non...]
    dot_general x5 -> x3, matrix products: 20.8 us -> 7.73 us  [dot_nt(): return lax.dot_general(a, b, LAST_CONTRACT, preferred_element_type=F32)]
    dot_general x3 -> x1, matrix products: 17.3 us -> 5.04 us  [dot_tn(): return lax.dot_general(a, b, ROWS_CONTRACT, preferred_element_type=F32)]
    pallas_call x1, Pallas kernels: 51.5 us -> 44.7 us  [forward(): pl.pallas_call(forward_kernel, grid=(4 * per + 1,), in_specs=[pl.BlockSpe...]
  transfers between devices with their start and end apart: 9 -> 9, of which waited for: 0 -> 0; matrix products, arithmetic and copies ran while one was open for 18% -> 11% of each run, Pallas kernels for 50% -> 58%
where the time goes in v5:
time: 312 us; the launch traced here: 308 us
  Pallas kernels  252 us (81%)
  matrix products  26.9 us (9%)
  between operations  16.6 us (5%)
  other arithmetic  7.42 us (2%)
  local copies, waits for them, and re-layouts  3.44 us (1%)
    pallas_call x5, Pallas kernels, layer_grads(): pl.pallas_call(functools.partial(layer_kernel, row_tile, grads is not Non...  188 us
    pallas_call x1, Pallas kernels, forward(): pl.pallas_call(forward_kernel, grid=(4 * per + 1,), in_specs=[pl.BlockSpe...  44.7 us
    pallas_call x1, Pallas kernels, chain(): pl.pallas_call(chain_kernel, grid=(d_w1.shape[2] // block,), in_specs=[wh...  19.6 us
    dot_general x3, matrix products, dot(): return jnp.dot(a, b, preferred_element_type=F32)  14.1 us
    dot_general x3, matrix products, dot_nt(): return lax.dot_general(a, b, LAST_CONTRACT, preferred_element_type=F32)  7.73 us
  transfers between devices with their start and end apart: 9, of which 0 were waited for; matrix products, arithmetic and copies ran while one was open for 11% of the time, Pallas kernels for 58%

profile of v5, /device:TPU:0, one launch (start us, length us, event | category | flops | bytes accessed | tf_op | source)
XLA Modules:
  0.0 308.2 jit_solution(17058237401759341513)
XLA Ops:
  7.2 0.0 all-gather.11.cloned.1.call-start
  7.2 0.0 copy-start.2
  7.2 0.0 copy-start.3
  7.2 0.0 copy-start.1
  7.2 44.7 %forward.1 = (bf16[192,1024]{1,0:T(8,128)(2,1)}, bf16[16,128,1024]{2,1,0:T(8,128)(2,1)}, bf16[16,64,1024]{2,1,0:T(8,128)(2,1)}) custom-call(bf16[128,1024]{1,0:T(8,128)(2,1)} %bitcast.27, bf16[64,1024]{1,0:T(8,128)(2,1)} %xq_ref.1, bf16[2,1024,4096]{2,1,0:T(8,128)(2,1)} %w1_ref.7, bf16[2,4096,1024]{2,1,0:T(8,128)(2,1)} %w2_ref.7, ...), custom_call_target="tpu_custom_call" | custom-call | flops 6442450944 | bytes 75497472 | tf_op jit(solution)/shard_map/forward/pallas_call | solution.py:216
  52.0 0.0 all-gather.11.cloned.1.call-update
  52.0 0.0 all-gather.7.cloned.1.call-start
  52.0 0.0 copy-done.2
  52.0 0.0 copy-done.3
  52.0 0.8 pad_maximum_fusion
  52.9 0.0 all-gather.7.cloned.1.call-update
  52.9 0.0 all-gather.9.cloned.1.call-start
  53.6 0.0 copy-done.1
  53.6 0.0 copy-start
  53.6 4.1 %convolution_convert_fusion.3 = bf16[1024,1024]{1,0:T(8,128)(2,1)S(1)} fusion(bf16[1024,1024]{1,0:T(8,128)(2,1)} %bitcast.34, bf16[1024,1024]{1,0:T(8,128)(2,1)S(1)} %copy-done.1), kind=kOutput, calls=%fused_computation.8 | convolution fusion | flops 2148532224 | bytes 6291456 | tf_op jit(solution)/shard_map/dot_general | solution.py:20
  57.7 5.3 %convolution_convert_fusion.1 = bf16[2048,1024]{1,0:T(8,128)(2,1)S(1)} fusion(bf16[2048,1024]{1,0:T(8,128)(2,1)S(1)} %bitcast.33, bf16[1024,1024]{1,0:T(8,128)(2,1)S(1)} %copy-done), kind=kOutput, calls=%fused_computation.6 | convolution fusion | flops 4297064448 | bytes 10485760 | tf_op jit(solution)/shard_map/dot_general | solution.py:20
  63.0 4.6 %fusion.15 = (f32[1024]{0:T(1024)S(1)}, f32[1024,2048]{1,0:T(8,128)S(1)}) fusion(f32[]{:T(128)S(6)} %copy.40, bf16[1024,1024]{1,0:T(8,128)(2,1)S(1)} %convolution_convert_fusion.3, bf16[2048,1024]{1,0:T(8,128)(2,1)S(1)} %convolution_convert_fusion.1), kind=kOutput, calls=%fused_computation.32 | convolution fusion | flops 4299160576 | bytes 14684164 | tf_op jit(solution)/shard_map/dot_general | solution.py:24
  67.7 3.2 %select_reduce_fusion = (f32[1024]{0:T(1024)S(1)}, f32[1024]{0:T(1024)S(1)}) fusion(f32[1024,2048]{1,0:T(8,128)S(1)} %get-tuple-element.70, s32[1024]{0:T(1024)S(1)} %fusion.11, f32[1024]{0:T(1024)S(1)} %is-finite_select_fusion), kind=kLoop, calls=%fused_computation.1 | loop fusion | flops 10483712 | bytes 8404992 | tf_op jit(solution)/shard_map/reduce_sum | solution.py:405
  70.9 0.6 subtract_reduce_fusion
  71.5 2.8 divide_convert_fusion
  74.3 4.7 %convolution_convert_fusion.2 = bf16[1024,1024]{1,0:T(8,128)(2,1)S(1)} fusion(bf16[1024,2048]{1,0:T(8,128)(2,1)S(1)} %divide_convert_fusion, bf16[2048,1024]{1,0:T(8,128)(2,1)S(1)} %convolution_convert_fusion.1), kind=kOutput, calls=%fused_computation.7 | convolution fusion | flops 4296015872 | bytes 10485760 | tf_op jit(solution)/shard_map/dot_general | solution.py:20
  79.0 0.0 copy-start.5
  79.1 1.3 copy-done.5
  80.4 1.5 fusion.2.qe_ref
  81.8 5.0 %convolution_convert_fusion = bf16[2048,1024]{1,0:T(8,128)(2,1)S(1)} fusion(bf16[1024,2048]{1,0:T(8,128)(2,1)S(1)} %divide_convert_fusion, bf16[1024,1024]{1,0:T(8,128)(2,1)S(1)} %convolution_convert_fusion.3), kind=kOutput, calls=%fused_computation.5 | convolution fusion | flops 4297064448 | bytes 10485760 | tf_op jit(solution)/shard_map/dot_general | solution.py:28
  86.9 0.0 copy-start.4
  86.9 2.1 copy-done.4
  89.0 1.6 fusion.de_ref
  90.6 19.6 %chain.1 = bf16[192,1024]{1,0:T(8,128)(2,1)} custom-call(bf16[192,1024]{1,0:T(8,128)(2,1)} %get-tuple-element.38.h_ref, f32[128,1024]{1,0:T(8,128)} %fusion.de_ref, f32[64,1024]{1,0:T(8,128)} %fusion.2.qe_ref, bf16[2,1024,4096]{2,1,0:T(8,128)(2,1)} %w1_ref.7, bf16[2,4096,1024]{2,1,0:T(8,128)(2,1)} %w2_ref.7, bf16[2,1024,4096]{2,1,0:T(8,128)(2,1)} %w1_ref.9, ...), custom_call_target="tpu_custom_call" | custom-call | flops 3221225472 | bytes 37748736 | tf_op jit(solution)/shard_map/chain/pallas_call | solution.py:263
  110.3 0.0 all-gather.9.cloned.1.call-update
  110.3 0.0 all-gather.11.cloned.1.call-done
  110.3 30.9 %layer_grads.6 = (f32[2,1024,4096]{2,1,0:T(8,128)}, f32[2,4096,1024]{2,1,0:T(8,128)}, f32[1,1024,2048]{2,1,0:T(8,128)}, f32[1,2048,1024]{2,1,0:T(8,128)}, f32[1024,1024]{1,0:T(8,128)}) custom-call(s32[1]{0:T(128)} %bitcast.3.core_ref, bf16[16,192,1024]{2,1,0:T(8,128)(2,1)} %bitcast.31, bf16[16,64,1024]{2,1,0:T(8,128)(2,1)} %bitcast.30, ...), custom_call_target="tpu_custom_call" | custom-call | flops 17179869184 | bytes 41943040 | tf_op jit(solution)/shard_map/layer_grads/pallas_call | solution.py:370
  141.3 0.3 collective-permute-start
  141.6 0.2 collective-permute-start.1
  141.8 54.5 %layer_grads.5 = (f32[2,1024,4096]{2,1,0:T(8,128)}, f32[2,4096,1024]{2,1,0:T(8,128)}, f32[1,1024,2048]{2,1,0:T(8,128)}, f32[1,2048,1024]{2,1,0:T(8,128)}, f32[1024,1024]{1,0:T(8,128)}) custom-call(s32[1]{0:T(128)} %bitcast.3.core_ref, bf16[16,192,1024]{2,1,0:T(8,128)(2,1)} %bitcast.32, bf16[16,128,1024]{2,1,0:T(8,128)(2,1)} %bitcast.29, ...), custom_call_target="tpu_custom_call" | custom-call | flops 34359738368 | bytes 41943040 | tf_op jit(solution)/shard_map/layer_grads/pallas_call | solution.py:370
  196.3 0.3 collective-permute-start.2
  196.6 0.2 collective-permute-start.3
  196.8 0.0 collective-permute-done.rest_2_
  196.8 0.0 collective-permute-done.1.rest_3_
  196.8 47.3 %layer_grads.7 = (f32[2,1024,4096]{2,1,0:T(8,128)}, f32[2,4096,1024]{2,1,0:T(8,128)}, f32[1,1024,2048]{2,1,0:T(8,128)}, f32[1,2048,1024]{2,1,0:T(8,128)}, f32[2,...) custom-call(s32[1]{0:T(128)} %bitcast.3.core_ref, ...), custom_call_target="tpu_custom_call", output_to_operand_aliasing={{0}: (5, {}), {1}: (6, {}), {4}: (9, {}), {5}: (10, {})} | custom-call | flops 34359738368 | bytes 41943040 | tf_op jit(solution)/shard_map/layer_grads/pallas_call | solution.py:370
  244.1 0.3 collective-permute-start.4
  244.5 0.2 collective-permute-start.5
  245.3 0.0 collective-permute-done.2.rest_2_
  245.3 0.0 collective-permute-done.3.rest_3_
  245.4 27.6 %layer_grads.8 = (f32[2,1024,4096]{2,1,0:T(8,128)}, f32[2,4096,1024]{2,1,0:T(8,128)}, f32[2,1024,4096]{2,1,0:T(8,128)}, f32[2,4096,1024]{2,1,0:T(8,128)}) custom-call(s32[1]{0:T(128)} %bitcast.3.core_ref, bf16[16,192,1024]{2,1,0:T(8,128)(2,1)} %bitcast.22, ...), custom_call_target="tpu_custom_call", output_to_operand_aliasing={{0}: (5, {}), {1}: (6, {}), {2}: (9, {}), {3}: (10, {})} | custom-call | flops 17179869184 | bytes 41943040 | tf_op jit(solution)/shard_map/layer_grads/pallas_call | solution.py:370
  272.9 0.0 collective-permute-done.4.rest_2_
  272.9 0.0 collective-permute-done.5.rest_3_
  273.0 27.4 %layer_grads.9 = (f32[2,1024,4096]{2,1,0:T(8,128)}, f32[2,4096,1024]{2,1,0:T(8,128)}, f32[2,1024,4096]{2,1,0:T(8,128)}, f32[2,4096,1024]{2,1,0:T(8,128)}) custom-call(s32[1]{0:T(128)} %bitcast.3.core_ref, bf16[16,192,1024]{2,1,0:T(8,128)(2,1)} %bitcast.23, ...), custom_call_target="tpu_custom_call", output_to_operand_aliasing={{0}: (5, {}), {1}: (6, {}), {2}: (9, {}), {3}: (10, {})} | custom-call | flops 17179869184 | bytes 41943040 | tf_op jit(solution)/shard_map/layer_grads/pallas_call | solution.py:370
  (7 shorter events, 0.0 us)
Async XLA Ops:
  7.2 103.1 %all-gather.11.cloned.1.call-start = ((), (), s32[]{:S(2)}) async-start(), calls=%async_computation.2 | async-start | bytes 6684672 | tf_op jit(solution)/shard_map/all_gather | solution.py:385
  7.2 44.8 %copy-start.2 = (bf16[2,64,1024]{2,1,0:T(8,128)(2,1)S(1)}, bf16[2,64,1024]{2,1,0:T(8,128)(2,1)}, u32[]{:S(2)}) copy-start(bf16[2,64,1024]{2,1,0:T(8,128)(2,1)} %param.10) | copy-start | bytes 786436
  7.2 44.8 %copy-start.3 = (bf16[64,1024]{1,0:T(8,128)(2,1)S(1)}, bf16[64,1024]{1,0:T(8,128)(2,1)}, u32[]{:S(2)}) copy-start(bf16[64,1024]{1,0:T(8,128)(2,1)} %xq_ref.1) | copy-start | bytes 393220
  7.2 46.4 %copy-start.1 = (bf16[1024,1024]{1,0:T(8,128)(2,1)S(1)}, bf16[1024,1024]{1,0:T(8,128)(2,1)}, u32[]{:S(2)}) copy-start(bf16[1024,1024]{1,0:T(8,128)(2,1)} %rest_0_.3) | copy-start | bytes 6291460
  52.0 144.9 %all-gather.7.cloned.1.call-start = ((), (), s32[]{:S(2)}) async-start(), calls=%async_computation | async-start | bytes 6684672 | tf_op jit(solution)/shard_map/all_gather | solution.py:385
  52.9 144.0 %all-gather.9.cloned.1.call-start = ((), (), s32[]{:S(2)}) async-start(), calls=%async_computation.1 | async-start | bytes 6684672 | tf_op jit(solution)/shard_map/all_gather | solution.py:385
  53.6 4.1 %copy-start = (bf16[1024,1024]{1,0:T(8,128)(2,1)S(1)}, bf16[1024,1024]{1,0:T(8,128)(2,1)}, u32[]{:S(2)}) copy-start(bf16[1024,1024]{1,0:T(8,128)(2,1)} %rest_0_.2) | copy-start | bytes 6291460
  53.6 4.1 %copy-start.6 = (bf16[16,128,1024]{2,1,0:T(8,128)(2,1)S(1)}, bf16[16,128,1024]{2,1,0:T(8,128)(2,1)}, u32[]{:S(2)}) copy-start(bf16[16,128,1024]{2,1,0:T(8,128)(2,1)} %get-tuple-element.37.rest_1_) | copy-start | bytes 12582916
  79.0 1.3 copy-start.5
  86.9 2.1 copy-start.4
  141.3 55.6 %collective-permute-start = (f32[1,1024,2048]{2,1,0:T(8,128)}, f32[1,1024,2048]{2,1,0:T(8,128)}, u32[]{:S(2)}, u32[]{:S(2)}) collective-permute-start(f32[1,1024,2048]{2,1,0:T(8,128)} %get-tuple-element.43), channel_id=1, source_target_pairs={{0,1},{1,0},{2,3},{3,2},{4,5},{5,4},{6,7},{7,6},{8,9},{9,8},{10,11... | collective-permute-start | bytes 25165832 | tf_op jit(solution)/shard_map/ppermute | solution.py:422
  141.6 55.3 %collective-permute-start.1 = (f32[1,2048,1024]{2,1,0:T(8,128)}, f32[1,2048,1024]{2,1,0:T(8,128)}, u32[]{:S(2)}, u32[]{:S(2)}) collective-permute-start(f32[1,2048,1024]{2,1,0:T(8,128)} %get-tuple-element.44), channel_id=1, source_target_pairs={{0,1},{1,0},{2,3},{3,2},{4,5},{5,4},{6,7},{7,6},{8,9},{9,8},{10,11... | collective-permute-start | bytes 25165832 | tf_op jit(solution)/shard_map/ppermute | solution.py:422
  196.3 49.1 %collective-permute-start.2 = (f32[1,1024,2048]{2,1,0:T(8,128)}, f32[1,1024,2048]{2,1,0:T(8,128)}, u32[]{:S(2)}, u32[]{:S(2)}) collective-permute-start(f32[1,1024,2048]{2,1,0:T(8,128)} %get-tuple-element.49), channel_id=1, source_target_pairs={{0,1},{1,0},{2,3},{3,2},{4,5},{5,4},{6,7},{7,6},{8,9},{9,8},{10,11... | collective-permute-start | bytes 25165832 | tf_op jit(solution)/shard_map/ppermute | solution.py:422
  196.6 48.7 %collective-permute-start.3 = (f32[1,2048,1024]{2,1,0:T(8,128)}, f32[1,2048,1024]{2,1,0:T(8,128)}, u32[]{:S(2)}, u32[]{:S(2)}) collective-permute-start(f32[1,2048,1024]{2,1,0:T(8,128)} %get-tuple-element.50), channel_id=1, source_target_pairs={{0,1},{1,0},{2,3},{3,2},{4,5},{5,4},{6,7},{7,6},{8,9},{9,8},{10,11... | collective-permute-start | bytes 25165832 | tf_op jit(solution)/shard_map/ppermute | solution.py:422
  244.1 28.8 %collective-permute-start.4 = (f32[1,1024,2048]{2,1,0:T(8,128)}, f32[1,1024,2048]{2,1,0:T(8,128)}, u32[]{:S(2)}, u32[]{:S(2)}) collective-permute-start(f32[1,1024,2048]{2,1,0:T(8,128)} %get-tuple-element.55), channel_id=1, source_target_pairs={{0,1},{1,0},{2,3},{3,2},{4,5},{5,4},{6,7},{7,6},{8,9},{9,8},{10,11... | collective-permute-start | bytes 25165832 | tf_op jit(solution)/shard_map/ppermute | solution.py:422
  244.5 28.5 %collective-permute-start.5 = (f32[1,2048,1024]{2,1,0:T(8,128)}, f32[1,2048,1024]{2,1,0:T(8,128)}, u32[]{:S(2)}, u32[]{:S(2)}) collective-permute-start(f32[1,2048,1024]{2,1,0:T(8,128)} %get-tuple-element.56), channel_id=1, source_target_pairs={{0,1},{1,0},{2,3},{3,2},{4,5},{5,4},{6,7},{7,6},{8,9},{9,8},{10,11... | collective-permute-start | bytes 25165832 | tf_op jit(solution)/shard_map/ppermute | solution.py:422
Sparse Core Ops, SparseCore 0:
  52.1 42.0 all-gather.10
  96.4 41.7 all-gather.6
  140.5 41.7 all-gather.8

commit v6 on v5

--- a/solution.py
+++ b/solution.py
@@ -230,20 +230,22 @@
     )(d_own, q_own, d_w1, d_w2, q_w1, q_w2)
 
 
-def chain_kernel(h_ref, de_ref, qe_ref, dw1_ref, dw2_ref, qw1_ref, qw2_ref, out_ref, acc_ref):
+def chain_kernel(me_ref, h_ref, d_up, q_up, d_proj, q_proj, dw1_ref, dw2_ref, qw1_ref, qw2_ref, out_ref, acc_ref, e_ref):
     s = pl.program_id(0)
     third = h_ref.shape[0] // 3
-    parts = ((pl.ds(0, 2 * third), de_ref, dw1_ref, dw2_ref), (pl.ds(2 * third, third), qe_ref, qw1_ref, qw2_ref))
+    parts = ((pl.ds(0, 2 * third), dw1_ref, dw2_ref), (pl.ds(2 * third, third), qw1_ref, qw2_ref))
 
     @pl.when(s == 0)
     def _():
-        for rows, e_ref, _, _ in parts:
-            acc_ref[rows, :] = e_ref[...]
-
-    pre = [dot(h_ref[rows, :], w1_ref[0]) for rows, _, w1_ref, _ in parts]
-    t = [dot_nt(e_ref[...].astype(BF16), w2_ref[0]) for _, e_ref, _, w2_ref in parts]
+        for (rows, _, _), up_ref, proj_ref in zip(parts, (d_up, q_up), (d_proj, q_proj)):
+            e1 = dot_nt(up_ref[0], proj_ref[...])
+            acc_ref[rows, :] = e1
+            e_ref[rows, :] = e1.astype(BF16)
+
+    pre = [dot(h_ref[rows, :], w1_ref[0]) for rows, w1_ref, _ in parts]
+    t = [dot_nt(e_ref[rows, :], w2_ref[0]) for rows, _, w2_ref in parts]
     delta = [gelu_and_back(*pair)[1] for pair in zip(pre, t)]
-    for (rows, _, w1_ref, _), d in zip(parts, delta):
+    for (rows, w1_ref, _), d in zip(parts, delta):
         acc_ref[rows, :] += dot_nt(d, w1_ref[0])
 
     @pl.when(s == pl.num_programs(0) - 1)
@@ -251,26 +253,30 @@
         out_ref[...] = acc_ref[...].astype(BF16)
 
 
-def chain(h1_own, d_e1, q_e1, d_w1, d_w2, q_w1, q_w2):
+def chain(me, h1_own, d_up, q_up, d_proj, q_proj, d_w1, d_w2, q_w1, q_w2):
     rows, width = h1_own.shape
     block = 512
-    wide = pl.BlockSpec((1, width, block), lambda s: (1, 0, s))
-    tall = pl.BlockSpec((1, block, width), lambda s: (1, s, 0))
+    wide = pl.BlockSpec((1, width, block), lambda s, m: (1, 0, s))
+    tall = pl.BlockSpec((1, block, width), lambda s, m: (1, s, 0))
 
     def whole(x):
-        return pl.BlockSpec(x.shape, lambda s: (0, 0))
+        return pl.BlockSpec(x.shape, lambda s, m: (0, 0))
+
+    def own(x):
+        return pl.BlockSpec((1, *x.shape[1:]), lambda s, m: (m[0], 0, 0))
 
     return pl.pallas_call(
         chain_kernel,
-        grid=(d_w1.shape[2] // block,),
-        in_specs=[whole(h1_own), whole(d_e1), whole(q_e1), wide, tall, wide, tall],
-        out_specs=whole(h1_own),
+        grid_spec=pltpu.PrefetchScalarGridSpec(
+            num_scalar_prefetch=1, grid=(d_w1.shape[2] // block,),
+            in_specs=[whole(h1_own), own(d_up), own(q_up), whole(d_proj), whole(q_proj), wide, tall, wide, tall],
+            out_specs=whole(h1_own),
+            scratch_shapes=[pltpu.VMEM((rows, width), F32), pltpu.VMEM((rows, width), BF16)]),
         out_shape=jax.ShapeDtypeStruct((rows, width), BF16),
-        scratch_shapes=[pltpu.VMEM((rows, width), F32)],
         compiler_params=pltpu.CompilerParams(dimension_semantics=('arbitrary',)),
-        cost_estimate=pl.CostEstimate(flops=4 * rows * width * d_w1.shape[2], bytes_accessed=36 * MIB, transcendentals=0),
+        cost_estimate=pl.CostEstimate(flops=4 * rows * width * d_w1.shape[2], bytes_accessed=40 * MIB, transcendentals=0),
         name='chain',
-    )(h1_own, d_e1, q_e1, d_w1, d_w2, q_w1, q_w2)
+    )(me.reshape(1), h1_own, d_up, q_up, d_proj, q_proj, d_w1, d_w2, q_w1, q_w2)
 
 
 def layer_kernel(row_tile, in_place, incoming, send, top, core_ref, h_ref, e_ref, w1_ref, w2_ref, *rest):
@@ -409,13 +415,9 @@
     q_up = dot(grad, docs).astype(BF16)
     d_up = dot_tn(grad, queries).astype(BF16)
 
-    def start(up, proj):
-        own = up.shape[0] // 16
-        return dot_nt(lax.dynamic_slice_in_dim(up, me * own, own, 0), proj)
-
-    e0_all = gather(chain(h1_own, start(d_up, d_proj), start(q_up, q_proj), d_w1, d_w2, q_w1, q_w2))
     d_up, d_last = [x.reshape(16, 2 * rows, width) for x in (d_up, d_last)]
     q_up, q_last = [x.reshape(16, rows, width) for x in (q_up, q_last)]
+    e0_all = gather(chain(me, h1_own, d_up, q_up, d_proj, q_proj, d_w1, d_w2, q_w1, q_w2))
     core = (me % 2).reshape(1)
 
     def swap(halves):

time: 312 us -> 311 us (level)
  local copies, waits for them, and re-layouts: 3.44 us -> 0.03 us
    unnamed x14 -> x10, local copies, waits for them, and re-layouts: 3.44 us -> 0.03 us
    dot_general x3 -> x1, matrix products: 7.73 us -> 4.64 us  [dot_nt(): return lax.dot_general(a, b, LAST_CONTRACT, preferred_element_type=F32)]
  transfers between devices with their start and end apart: 9 -> 9, of which waited for: 0 -> 0; matrix products, arithmetic and copies ran while one was open for 11% -> 11% of each run, Pallas kernels for 58% -> 60%
where the time goes in v6:
time: 311 us; the launch traced here: 307 us
  Pallas kernels  255 us (82%)
  matrix products  26 us (8%)
  between operations  16.6 us (5%)
  other arithmetic  7.41 us (2%)
    pallas_call x5, Pallas kernels, layer_grads(): pl.pallas_call(functools.partial(layer_kernel, row_tile, grads is not Non...  188 us
    pallas_call x1, Pallas kernels, forward(): pl.pallas_call(forward_kernel, grid=(4 * per + 1,), in_specs=[pl.BlockSpe...  44.7 us
    pallas_call x1, Pallas kernels, chain(): pl.pallas_call(chain_kernel, grid_spec=pltpu.PrefetchScalarGridSpec(num_s...  22.3 us
    dot_general x3, matrix products, dot(): return jnp.dot(a, b, preferred_element_type=F32)  15.1 us
    dot_general x1, matrix products, dot_tn(): return lax.dot_general(a, b, ROWS_CONTRACT, preferred_element_type=F32)  6.25 us
  transfers between devices with their start and end apart: 9, of which 0 were waited for; matrix products, arithmetic and copies ran while one was open for 11% of the time, Pallas kernels for 60%

profile of v6, /device:TPU:0, one launch (start us, length us, event | category | flops | bytes accessed | tf_op | source)
XLA Modules:
  0.0 306.6 jit_solution(2196247553834826259)
XLA Ops:
  7.2 0.0 all-gather.11.cloned.1.call-start
  7.2 0.0 copy-start.2
  7.2 0.0 copy-start.3
  7.2 0.0 copy-start
  7.2 44.7 %forward.1 = (bf16[192,1024]{1,0:T(8,128)(2,1)}, bf16[16,128,1024]{2,1,0:T(8,128)(2,1)}, bf16[16,64,1024]{2,1,0:T(8,128)(2,1)}) custom-call(bf16[128,1024]{1,0:T(8,128)(2,1)} %bitcast.30, bf16[64,1024]{1,0:T(8,128)(2,1)} %xq_ref.1, bf16[2,1024,4096]{2,1,0:T(8,128)(2,1)} %w1_ref.7, bf16[2,4096,1024]{2,1,0:T(8,128)(2,1)} %w2_ref.7, ...), custom_call_target="tpu_custom_call" | custom-call | flops 6442450944 | bytes 75497472 | tf_op jit(solution)/shard_map/forward/pallas_call | solution.py:216
  52.0 0.0 all-gather.11.cloned.1.call-update
  52.0 0.0 all-gather.7.cloned.1.call-start
  52.0 0.0 copy-done.2
  52.0 0.0 copy-done.3
  52.1 0.8 pad_maximum_fusion
  52.9 0.0 all-gather.7.cloned.1.call-update
  52.9 0.0 all-gather.9.cloned.1.call-start
  53.6 0.0 copy-start.1
  53.6 0.0 copy-start.4
  53.6 0.0 copy-done
  53.6 4.1 %convolution_convert_fusion.3 = bf16[1024,1024]{1,0:T(8,128)(2,1)S(1)} fusion(bf16[1024,1024]{1,0:T(8,128)(2,1)} %bitcast.35, bf16[1024,1024]{1,0:T(8,128)(2,1)S(1)} %copy-done), kind=kOutput, calls=%fused_computation.8 | convolution fusion | flops 2148532224 | bytes 6291456 | tf_op jit(solution)/shard_map/dot_general | solution.py:20
  57.7 0.0 copy-done.1
  57.7 0.0 copy-done.4
  57.7 5.2 %convolution_convert_fusion.1 = bf16[2048,1024]{1,0:T(8,128)(2,1)S(1)} fusion(bf16[2048,1024]{1,0:T(8,128)(2,1)S(1)} %bitcast.34, bf16[1024,1024]{1,0:T(8,128)(2,1)S(1)} %copy-done.1), kind=kOutput, calls=%fused_computation.6 | convolution fusion | flops 4297064448 | bytes 10485760 | tf_op jit(solution)/shard_map/dot_general | solution.py:20
  63.0 4.6 %fusion.9 = (f32[1024]{0:T(1024)S(1)}, f32[1024,2048]{1,0:T(8,128)S(1)}) fusion(f32[]{:T(128)S(6)} %copy.40, bf16[1024,1024]{1,0:T(8,128)(2,1)S(1)} %convolution_convert_fusion.3, bf16[2048,1024]{1,0:T(8,128)(2,1)S(1)} %convolution_convert_fusion.1), kind=kOutput, calls=%fused_computation.26 | convolution fusion | flops 4299160576 | bytes 14684164 | tf_op jit(solution)/shard_map/dot_general | solution.py:24
  67.6 3.2 %select_reduce_fusion = (f32[1024]{0:T(1024)S(1)}, f32[1024]{0:T(1024)S(1)}) fusion(f32[1024,2048]{1,0:T(8,128)S(1)} %get-tuple-element.70, s32[1024]{0:T(1024)S(1)} %fusion.7, f32[1024]{0:T(1024)S(1)} %is-finite_select_fusion), kind=kLoop, calls=%fused_computation.1 | loop fusion | flops 10483712 | bytes 8404992 | tf_op jit(solution)/shard_map/reduce_sum | solution.py:411
  70.8 0.6 subtract_reduce_fusion
  71.4 2.8 divide_convert_fusion
  74.2 6.2 %convolution_convert_fusion = bf16[2048,1024]{1,0:T(8,128)(2,1)} fusion(bf16[1024,2048]{1,0:T(8,128)(2,1)S(1)} %divide_convert_fusion, bf16[1024,1024]{1,0:T(8,128)(2,1)S(1)} %convolution_convert_fusion.3), kind=kOutput, calls=%fused_computation.5 | convolution fusion | flops 4297064448 | bytes 10485760 | tf_op jit(solution)/shard_map/dot_general | solution.py:28
  80.5 5.8 %convolution_convert_fusion.2 = bf16[1024,1024]{1,0:T(8,128)(2,1)} fusion(bf16[1024,2048]{1,0:T(8,128)(2,1)S(1)} %divide_convert_fusion, bf16[2048,1024]{1,0:T(8,128)(2,1)S(1)} %convolution_convert_fusion.1), kind=kOutput, calls=%fused_computation.7 | convolution fusion | flops 4296015872 | bytes 10485760 | tf_op jit(solution)/shard_map/dot_general | solution.py:20
  86.3 22.3 %chain.1 = bf16[192,1024]{1,0:T(8,128)(2,1)} custom-call(s32[1]{0:T(128)} %bitcast.5.me_ref, bf16[192,1024]{1,0:T(8,128)(2,1)} %get-tuple-element.38.h_ref, bf16[16,128,1024]{2,1,0:T(8,128)(2,1)} %bitcast.26, bf16[16,64,1024]{2,1,0:T(8,128)(2,1)} %bitcast.28, bf16[1024,1024]{1,0:T(8,128)(2,1)} %rest_0_.2, bf16[1024,1024]{1,0:T(8,128)(2,1)} %rest_0_.3, ...), custom_call_target="tpu_custom_call" | custom-call | flops 3221225472 | bytes 41943040 | tf_op jit(solution)/shard_map/chain/pallas_call | solution.py:268
  108.6 0.0 all-gather.9.cloned.1.call-update
  108.7 0.0 all-gather.11.cloned.1.call-done
  108.7 30.9 %layer_grads.6 = (f32[2,1024,4096]{2,1,0:T(8,128)}, f32[2,4096,1024]{2,1,0:T(8,128)}, f32[1,1024,2048]{2,1,0:T(8,128)}, f32[1,2048,1024]{2,1,0:T(8,128)}, f32[1024,1024]{1,0:T(8,128)}) custom-call(s32[1]{0:T(128)} %bitcast.3.core_ref, bf16[16,192,1024]{2,1,0:T(8,128)(2,1)} %bitcast.32, bf16[16,64,1024]{2,1,0:T(8,128)(2,1)} %bitcast.29, ...), custom_call_target="tpu_custom_call" | custom-call | flops 17179869184 | bytes 41943040 | tf_op jit(solution)/shard_map/layer_grads/pallas_call | solution.py:376
  139.6 0.3 collective-permute-start
  139.9 0.2 collective-permute-start.1
  140.2 54.5 %layer_grads.5 = (f32[2,1024,4096]{2,1,0:T(8,128)}, f32[2,4096,1024]{2,1,0:T(8,128)}, f32[1,1024,2048]{2,1,0:T(8,128)}, f32[1,2048,1024]{2,1,0:T(8,128)}, f32[1024,1024]{1,0:T(8,128)}) custom-call(s32[1]{0:T(128)} %bitcast.3.core_ref, bf16[16,192,1024]{2,1,0:T(8,128)(2,1)} %bitcast.33, bf16[16,128,1024]{2,1,0:T(8,128)(2,1)} %bitcast.27, ...), custom_call_target="tpu_custom_call" | custom-call | flops 34359738368 | bytes 41943040 | tf_op jit(solution)/shard_map/layer_grads/pallas_call | solution.py:376
  194.6 0.3 collective-permute-start.2
  195.0 0.2 collective-permute-start.3
  195.2 0.0 all-gather.7.cloned.1.call-done
  195.2 0.0 all-gather.9.cloned.1.call-done
  195.2 0.0 collective-permute-done.rest_2_
  195.2 0.0 collective-permute-done.1.rest_3_
  195.2 47.3 %layer_grads.7 = (f32[2,1024,4096]{2,1,0:T(8,128)}, f32[2,4096,1024]{2,1,0:T(8,128)}, f32[1,1024,2048]{2,1,0:T(8,128)}, f32[1,2048,1024]{2,1,0:T(8,128)}, f32[2,...) custom-call(s32[1]{0:T(128)} %bitcast.3.core_ref, ...), custom_call_target="tpu_custom_call", output_to_operand_aliasing={{0}: (5, {}), {1}: (6, {}), {4}: (9, {}), {5}: (10, {})} | custom-call | flops 34359738368 | bytes 41943040 | tf_op jit(solution)/shard_map/layer_grads/pallas_call | solution.py:376
  242.5 0.3 collective-permute-start.4
  242.8 0.2 collective-permute-start.5
  243.7 0.0 collective-permute-done.2.rest_2_
  243.7 0.0 collective-permute-done.3.rest_3_
  243.7 27.6 %layer_grads.8 = (f32[2,1024,4096]{2,1,0:T(8,128)}, f32[2,4096,1024]{2,1,0:T(8,128)}, f32[2,1024,4096]{2,1,0:T(8,128)}, f32[2,4096,1024]{2,1,0:T(8,128)}) custom-call(s32[1]{0:T(128)} %bitcast.3.core_ref, bf16[16,192,1024]{2,1,0:T(8,128)(2,1)} %bitcast.21, ...), custom_call_target="tpu_custom_call", output_to_operand_aliasing={{0}: (5, {}), {1}: (6, {}), {2}: (9, {}), {3}: (10, {})} | custom-call | flops 17179869184 | bytes 41943040 | tf_op jit(solution)/shard_map/layer_grads/pallas_call | solution.py:376
  271.3 0.0 collective-permute-done.4.rest_2_
  271.3 0.0 collective-permute-done.5.rest_3_
  271.3 27.4 %layer_grads.9 = (f32[2,1024,4096]{2,1,0:T(8,128)}, f32[2,4096,1024]{2,1,0:T(8,128)}, f32[2,1024,4096]{2,1,0:T(8,128)}, f32[2,4096,1024]{2,1,0:T(8,128)}) custom-call(s32[1]{0:T(128)} %bitcast.3.core_ref, bf16[16,192,1024]{2,1,0:T(8,128)(2,1)} %bitcast.22, ...), custom_call_target="tpu_custom_call", output_to_operand_aliasing={{0}: (5, {}), {1}: (6, {}), {2}: (9, {}), {3}: (10, {})} | custom-call | flops 17179869184 | bytes 41943040 | tf_op jit(solution)/shard_map/layer_grads/pallas_call | solution.py:376
  (2 shorter events, 0.0 us)
Async XLA Ops:
  7.2 101.5 %all-gather.11.cloned.1.call-start = ((), (), s32[]{:S(2)}) async-start(), calls=%async_computation.2 | async-start | bytes 6684672 | tf_op jit(solution)/shard_map/all_gather | solution.py:391
  7.2 44.8 %copy-start.2 = (bf16[2,64,1024]{2,1,0:T(8,128)(2,1)S(1)}, bf16[2,64,1024]{2,1,0:T(8,128)(2,1)}, u32[]{:S(2)}) copy-start(bf16[2,64,1024]{2,1,0:T(8,128)(2,1)} %param.10) | copy-start | bytes 786436
  7.2 44.8 %copy-start.3 = (bf16[64,1024]{1,0:T(8,128)(2,1)S(1)}, bf16[64,1024]{1,0:T(8,128)(2,1)}, u32[]{:S(2)}) copy-start(bf16[64,1024]{1,0:T(8,128)(2,1)} %xq_ref.1) | copy-start | bytes 393220
  7.2 46.4 %copy-start = (bf16[1024,1024]{1,0:T(8,128)(2,1)S(1)}, bf16[1024,1024]{1,0:T(8,128)(2,1)}, u32[]{:S(2)}) copy-start(bf16[1024,1024]{1,0:T(8,128)(2,1)} %rest_0_.3) | copy-start | bytes 6291460
  52.0 143.2 %all-gather.7.cloned.1.call-start = ((), (), s32[]{:S(2)}) async-start(), calls=%async_computation | async-start | bytes 6684672 | tf_op jit(solution)/shard_map/all_gather | solution.py:391
  52.9 142.3 %all-gather.9.cloned.1.call-start = ((), (), s32[]{:S(2)}) async-start(), calls=%async_computation.1 | async-start | bytes 6684672 | tf_op jit(solution)/shard_map/all_gather | solution.py:391
  53.6 4.1 %copy-start.1 = (bf16[1024,1024]{1,0:T(8,128)(2,1)S(1)}, bf16[1024,1024]{1,0:T(8,128)(2,1)}, u32[]{:S(2)}) copy-start(bf16[1024,1024]{1,0:T(8,128)(2,1)} %rest_0_.2) | copy-start | bytes 6291460
  53.6 4.1 %copy-start.4 = (bf16[16,128,1024]{2,1,0:T(8,128)(2,1)S(1)}, bf16[16,128,1024]{2,1,0:T(8,128)(2,1)}, u32[]{:S(2)}) copy-start(bf16[16,128,1024]{2,1,0:T(8,128)(2,1)} %get-tuple-element.37.rest_1_) | copy-start | bytes 12582916
  139.6 55.6 %collective-permute-start = (f32[1,1024,2048]{2,1,0:T(8,128)}, f32[1,1024,2048]{2,1,0:T(8,128)}, u32[]{:S(2)}, u32[]{:S(2)}) collective-permute-start(f32[1,1024,2048]{2,1,0:T(8,128)} %get-tuple-element.43), channel_id=1, source_target_pairs={{0,1},{1,0},{2,3},{3,2},{4,5},{5,4},{6,7},{7,6},{8,9},{9,8},{10,11... | collective-permute-start | bytes 25165832 | tf_op jit(solution)/shard_map/ppermute | solution.py:424
  139.9 55.3 %collective-permute-start.1 = (f32[1,2048,1024]{2,1,0:T(8,128)}, f32[1,2048,1024]{2,1,0:T(8,128)}, u32[]{:S(2)}, u32[]{:S(2)}) collective-permute-start(f32[1,2048,1024]{2,1,0:T(8,128)} %get-tuple-element.44), channel_id=1, source_target_pairs={{0,1},{1,0},{2,3},{3,2},{4,5},{5,4},{6,7},{7,6},{8,9},{9,8},{10,11... | collective-permute-start | bytes 25165832 | tf_op jit(solution)/shard_map/ppermute | solution.py:424
  194.6 49.0 %collective-permute-start.2 = (f32[1,1024,2048]{2,1,0:T(8,128)}, f32[1,1024,2048]{2,1,0:T(8,128)}, u32[]{:S(2)}, u32[]{:S(2)}) collective-permute-start(f32[1,1024,2048]{2,1,0:T(8,128)} %get-tuple-element.49), channel_id=1, source_target_pairs={{0,1},{1,0},{2,3},{3,2},{4,5},{5,4},{6,7},{7,6},{8,9},{9,8},{10,11... | collective-permute-start | bytes 25165832 | tf_op jit(solution)/shard_map/ppermute | solution.py:424
  195.0 48.7 %collective-permute-start.3 = (f32[1,2048,1024]{2,1,0:T(8,128)}, f32[1,2048,1024]{2,1,0:T(8,128)}, u32[]{:S(2)}, u32[]{:S(2)}) collective-permute-start(f32[1,2048,1024]{2,1,0:T(8,128)} %get-tuple-element.50), channel_id=1, source_target_pairs={{0,1},{1,0},{2,3},{3,2},{4,5},{5,4},{6,7},{7,6},{8,9},{9,8},{10,11... | collective-permute-start | bytes 25165832 | tf_op jit(solution)/shard_map/ppermute | solution.py:424
  242.5 28.8 %collective-permute-start.4 = (f32[1,1024,2048]{2,1,0:T(8,128)}, f32[1,1024,2048]{2,1,0:T(8,128)}, u32[]{:S(2)}, u32[]{:S(2)}) collective-permute-start(f32[1,1024,2048]{2,1,0:T(8,128)} %get-tuple-element.55), channel_id=1, source_target_pairs={{0,1},{1,0},{2,3},{3,2},{4,5},{5,4},{6,7},{7,6},{8,9},{9,8},{10,11... | collective-permute-start | bytes 25165832 | tf_op jit(solution)/shard_map/ppermute | solution.py:424
  242.8 28.5 %collective-permute-start.5 = (f32[1,2048,1024]{2,1,0:T(8,128)}, f32[1,2048,1024]{2,1,0:T(8,128)}, u32[]{:S(2)}, u32[]{:S(2)}) collective-permute-start(f32[1,2048,1024]{2,1,0:T(8,128)} %get-tuple-element.56), channel_id=1, source_target_pairs={{0,1},{1,0},{2,3},{3,2},{4,5},{5,4},{6,7},{7,6},{8,9},{9,8},{10,11... | collective-permute-start | bytes 25165832 | tf_op jit(solution)/shard_map/ppermute | solution.py:424
Sparse Core Ops, SparseCore 0:
  52.1 42.0 all-gather.10
  96.4 41.7 all-gather.6
  140.5 41.7 all-gather.8
